TPU v7x, 32 devices: a whole 2x2x4 slice. The times are simulated.
32 devices in a mesh: row: 4 (over y, core), col: 8 (over z, x).
Axes of the slice: x: 2, y: 2, z: 4, core: 2. Of those that a mesh axis runs over, the one named last changes fastest.
Arguments:
- tokens: bfloat16 [256, 2, 4096], P(None, None, 'row'), may hold values from -6 to 6
- task_emb: bfloat16 [512, 1024], replicated, may hold values from -6 to 6
- gen_in: bfloat16 [1024, 512], replicated, may hold values from -0.1875 to 0.1875
- gen_a: bfloat16 [512, 4096, 16], P(None, ('row', 'col')), may hold values from -0.0078125 to 0.0078125
- gen_b: bfloat16 [512, 16, 14336], P(None, 'row', 'col'), may hold values from -0.125 to 0.125
- w_gate: bfloat16 [4096, 14336], P('row', 'col'), may hold values from -0.09375 to 0.09375
- w_up: bfloat16 [4096, 14336], P('row', 'col'), may hold values from -0.09375 to 0.09375
- w_down: bfloat16 [14336, 4096], P('col', 'row'), may hold values from -0.046875 to 0.046875
- group_count: int32 [64], replicated, may hold values from 1 to 16, 256 in all
- group_task: int32 [64], replicated, may hold values from 0 to 511, as said below
Outputs:
- mixed: bfloat16 [256, 2, 4096], P('col', None, 'row')
Inputs may be any that keep to these rules, and one draw needn't show every extreme that they name: `group_count`: requests in each group, in the order of the requests; they sum to 256 and the largest is 16. `group_task`: distinct task ids, one for each group.
All inputs are finite; a program needn't handle non-finite values.
Results may differ from a plain program's by a relative error of at most 0.0078.
Values may be sent and summed in bfloat16 or wider, within the bound.
No kernel may reach another device: no remote copies, remote signals or barrier semaphores. Data moves between devices by JAX's collectives and lax.ppermute only.
A program may use at most 128 MiB of HBM per device.

v0:
```python
import jax
import jax.numpy as jnp
from jax import lax
from jax.sharding import PartitionSpec as P


def shards(tokens, task_emb, gen_in, gen_a, gen_b, w_gate, w_up, w_down, group_count, group_task):
    batch_size, draft_len, width_part = tokens.shape
    row_count = batch_size * draft_len
    flat_tokens = tokens.reshape(row_count, width_part)
    groups = group_count.shape[0]
    group_ends = jnp.cumsum(group_count)
    group_starts = group_ends - group_count
    request_ids = jnp.arange(batch_size, dtype=jnp.int32)
    membership = (request_ids[:, None] >= group_starts[None, :]) & (
        request_ids[:, None] < group_ends[None, :]
    )
    member_rows = jnp.repeat(membership, draft_len, axis=0)
    member_float = member_rows.astype(jnp.float32)
    member_half = member_rows.astype(jnp.bfloat16)
    chosen = jnp.take(task_emb, group_task, axis=0)
    hyper_out = jax.nn.silu(jnp.dot(chosen, gen_in, preferred_element_type=jnp.float32)).astype(
        jnp.bfloat16
    )
    hyper_width, slab_width, rank_dim = gen_a.shape
    a_local = jnp.dot(
        hyper_out,
        gen_a.reshape(hyper_width, slab_width * rank_dim),
        preferred_element_type=jnp.float32,
    )
    a_local = a_local.astype(jnp.bfloat16).reshape(groups, slab_width, rank_dim)
    a_local = a_local.transpose(1, 0, 2).reshape(slab_width, groups * rank_dim)
    wide_low = jnp.dot(
        flat_tokens,
        lax.all_gather(a_local, "col", axis=0, tiled=True),
        preferred_element_type=jnp.float32,
    )
    low_part = jnp.sum(
        wide_low.reshape(row_count, groups, rank_dim) * member_float[:, :, None], axis=1
    )
    gate_part = jnp.dot(flat_tokens, w_gate, preferred_element_type=jnp.float32)
    up_part = jnp.dot(flat_tokens, w_up, preferred_element_type=jnp.float32)
    _, rank_part, ff_part = gen_b.shape
    b_local = jnp.dot(
        hyper_out,
        gen_b.reshape(hyper_width, rank_part * ff_part),
        preferred_element_type=jnp.float32,
    )
    b_local = b_local.astype(jnp.bfloat16).reshape(groups, rank_part, ff_part)
    gate_total, up_total, low_sum = lax.psum((gate_part, up_part, low_part), "row")
    low_half = low_sum.astype(jnp.bfloat16)
    spread = member_half[:, :, None] * low_half[:, None, :]
    share_rows = spread.shape[0]
    block_piece = lax.all_gather(b_local, "row", axis=1, tiled=True)
    ranks_here = block_piece.shape[1]
    picked = spread.reshape(share_rows, groups * ranks_here)
    adapter_update = jnp.dot(
        picked,
        block_piece.reshape(groups * ranks_here, ff_part),
        preferred_element_type=jnp.float32,
    )
    hidden_state = (jax.nn.silu(gate_total) * (up_total + adapter_update)).astype(jnp.bfloat16)
    col_count = lax.axis_size("col")
    picked = hidden_state
    mixed = lax.psum_scatter(
        jnp.dot(picked, w_down, preferred_element_type=jnp.float32),
        "col",
        scatter_dimension=0,
        tiled=True,
    )
    return mixed.astype(jnp.bfloat16).reshape(batch_size // col_count, draft_len, w_down.shape[1])


def solution(mesh):
    in_specs = (
        P(None, None, "row"),
        P(),
        P(),
        P(None, ("row", "col"), None),
        P(None, "row", "col"),
        P("row", "col"),
        P("row", "col"),
        P("col", "row"),
        P(),
        P(),
    )
    out_specs = P("col", None, "row")
    return jax.shard_map(shards, mesh=mesh, in_specs=in_specs, out_specs=out_specs, check_vma=False)
```

profile of v0, /device:TPU:0, one launch (start us, length us, event | category | flops | bytes accessed | tf_op | source)
XLA Modules:
  0.0 278.1 jit_solution(9507470869285489578)
XLA Ops:
  7.4 0.0 copy-start
  7.4 0.0 all-gather.3.cloned.1.call-start
  7.4 0.7 compare_and_fusion
  8.1 0.7 compare_select_fusion
  8.8 3.9 %copy.28 = bf16[512,128,16]{0,2,1:T(8,128)(2,1)S(1)} copy(bf16[512,128,16]{1,2,0:T(8,128)(2,1)} %param.13) | data formatting | bytes 4194304 | tf_op args[3]
  12.7 0.0 copy-done
  12.7 0.7 gather_fusion
  13.4 1.6 multiply_convert_fusion
  15.0 0.7 convolution_convert_fusion.1
  15.8 0.3 copy.29
  16.1 1.3 copy.30
  17.4 0.0 all-gather.3.cloned.1.call-update
  17.4 0.0 all-reduce.3.cloned.1.call-start
  17.5 1.5 reshape.69
  18.9 0.0 copy-start.2
  18.9 6.2 %fusion.28 = f32[512,1792]{1,0:T(8,128)} fusion(bf16[512,1024]{1,0:T(8,128)(2,1)S(1)} %reshape.69, bf16[1024,1792]{1,0:T(8,128)(2,1)} %param.16), kind=kOutput, calls=%fused_computation.30 | convolution fusion | flops 1879048192 | bytes 8388608 | tf_op jit(solution)/shard_map/dot_general | solution.py:42
  25.1 0.0 copy-done.2
  25.1 3.9 %fusion.27 = f32[512,1792]{1,0:T(8,128)} fusion(bf16[512,1024]{1,0:T(8,128)(2,1)S(1)} %reshape.69, bf16[1024,1792]{1,0:T(8,128)(2,1)S(1)} %copy-done.2), kind=kOutput, calls=%fused_computation.29 | convolution fusion | flops 1879048192 | bytes 8388608 | tf_op jit(solution)/shard_map/dot_general | solution.py:41
  29.0 0.0 all-reduce.3.cloned.1.call-update
  29.0 0.0 all-gather.5.cloned.1.call-start
  29.1 4.7 %copy.35 = bf16[64,8,4,1792]{3,1,2,0:T(8,128)(2,1)S(1)} copy(bf16[64,8,4,1792]{3,2,1,0:T(4,128)(2,1)} %bitcast.39) | data formatting | bytes 14680064
  33.8 0.0 copy-start.1
  33.8 1.4 convolution_convert_fusion
  35.2 1.0 copy.43
  36.1 0.0 all-gather.5.cloned.1.call-update
  36.2 0.0 reduce-scatter.2.cloned.1.call-start
  36.2 0.0 copy-done.1
  36.2 0.1 copy.26
  36.3 0.1 reduce-window.8
  36.4 0.1 reduce
  36.6 0.1 broadcast_in_dim.24
  36.7 0.1 copy.27
  36.8 0.1 broadcast_in_dim.28
  36.9 0.1 copy.31
  37.0 33.6 %all-gather.3.cloned.1.call-done = bf16[1024,1024]{0,1:T(8,128)(2,1)} async-done(((bf16[128,1024]{0,1:T(8,128)(2,1)}), bf16[1024,1024]{0,1:T(8,128)(2,1)}) %all-gather.3.cloned.1.call-update) | async-done | bytes 2097168 | tf_op jit(solution)/shard_map/all_gather | solution.py:35
  70.6 2.9 %fusion.29 = f32[1024,512]{1,0:T(8,128)S(1)} fusion(bf16[1024,1024]{0,1:T(8,128)(2,1)} %all-gather.3.cloned.1.call-done, bf16[512,1024]{1,0:T(8,128)(2,1)S(1)} %reshape.69), kind=kOutput, calls=%fused_computation.31 | convolution fusion | flops 1073741824 | bytes 5242880 | tf_op jit(solution)/shard_map/dot_general | solution.py:33
  73.5 0.4 multiply_reduce_fusion
  73.9 12.4 %psum.23 = bf16[512,16]{0,1:T(8,128)(2,1)S(1)} all-reduce(f32[512,16]{0,1:T(8,128)S(1)} %multiply_reduce_fusion), channel_id=1, replica_groups=mesh['row'=4,'col'=8] {'row'}, use_global_device_ids=true, to_apply=%region_4.5 | all-reduce | flops 8192 | bytes 49152 | tf_op jit(solution)/shard_map/psum | solution.py:50
  86.3 102.3 %all-reduce.3.cloned.1.call-done = (f32[512,1792]{1,0:T(8,128)}, f32[512,1792]{1,0:T(8,128)}) async-done(((f32[512,1792]{1,0:T(8,128)}, f32[512,1792]{1,0:T(8,128)}), (f32[512,1792]{1,0:T(8,128)}, f32[512,1792]{1,0:T(8,128)})) %all-reduce.3.cloned.1.call-update) | async-done | bytes 7340048 | tf_op jit(solution)/shard_map/psum | solution.py:50
  188.6 0.0 all-gather.5.cloned.1.call-done
  188.6 12.0 %fusion.9 = f32[512,1024]{1,0:T(8,128)} fusion(bf16[1792,1024]{1,0:T(8,128)(2,1)} %param.17, f32[512,1792]{1,0:T(8,128)} %get-tuple-element.5, f32[512,1792]{1,0:T(8,128)} %get-tuple-element.6, bf16[64,16,1792]{2,0,1:T(8,128)(2,1)} %all-gather.5.cloned.1.call-done, bf16[512,16]{0,1:T(8,128)(2,1)S(1)} %psum.23, bf16[512,64]{0,1:T(8,128)(2,1)S(1)} %copy.27), kind=kOutput, calls=%fused_computation.11 | convolution fusion | flops 3765043200 | bytes 16859136 | tf_op jit(solution)/shard_map/dot_general | solution.py:66
  200.6 0.0 reduce-scatter.2.cloned.1.call-update
  200.6 68.8 %reduce-scatter.2.cloned.1.call-done = f32[64,1024]{1,0:T(8,128)} async-done(((f32[512,1024]{1,0:T(8,128)}), f32[64,1024]{1,0:T(8,128)}) %reduce-scatter.2.cloned.1.call-update) | async-done | bytes 262160 | tf_op jit(solution)/shard_map/reduce_scatter | solution.py:65
  269.3 1.0 convert_element_type.49
  270.3 0.7 reshape.78
  (3 shorter events, 0.0 us)
Async XLA Ops:
  7.4 5.3 %copy-start = (bf16[512,1024]{1,0:T(8,128)(2,1)S(1)}, bf16[512,1024]{1,0:T(8,128)(2,1)}, u32[]{:S(2)}) copy-start(bf16[512,1024]{1,0:T(8,128)(2,1)} %param.11) | copy-start | bytes 3145732
  7.4 63.3 %all-gather.3.cloned.1.call-start = ((), (), s32[]{:S(2)}) async-start(), calls=%async_computation.1 | async-start | bytes 2359296 | tf_op jit(solution)/shard_map/all_gather | solution.py:35
  17.4 171.2 %all-reduce.3.cloned.1.call-start = ((), (), s32[]{:S(2)}) async-start(), calls=%async_computation.4 | async-start | bytes 14680064 | tf_op jit(solution)/shard_map/psum | solution.py:50
  18.9 6.2 %copy-start.2 = (bf16[1024,1792]{1,0:T(8,128)(2,1)S(1)}, bf16[1024,1792]{1,0:T(8,128)(2,1)}, u32[]{:S(2)}) copy-start(bf16[1024,1792]{1,0:T(8,128)(2,1)} %param.15) | copy-start | bytes 11010052
  29.0 159.6 %all-gather.5.cloned.1.call-start = ((), (), s32[]{:S(2)}) async-start(), calls=%async_computation.2 | async-start | bytes 4587520 | tf_op jit(solution)/shard_map/all_gather | solution.py:54
  33.8 2.5 copy-start.1
  36.2 233.2 %reduce-scatter.2.cloned.1.call-start = ((), (), s32[]{:S(2)}) async-start(), calls=%async_computation.3 | async-start | bytes 2359296 | tf_op jit(solution)/shard_map/reduce_scatter | solution.py:65
Sparse Core Ops, SparseCore 0:
  17.5 53.0 all-gather.2
  72.2 47.7 all-gather.4
  200.7 68.5 reduce-scatter.1
Sparse Core Ops, SparseCore 1:
  29.1 159.4 all-reduce.2
where the time goes:
time: 279 us; the launch traced here: 278 us
  waiting for transfers between devices  205 us (73%)
  matrix products  28.6 us (10%)
  between operations  14.7 us (5%)
  local copies, waits for them, and re-layouts  14.5 us (5%)
  blocking collectives  12.4 us (4%)
  other arithmetic  3.03 us (1%)
    psum x1, waiting for transfers between devices, shards(): lax.psum((gate_part, up_part, low_part), 'row')  102 us
    reduce_scatter x1, waiting for transfers between devices, shards(): lax.psum_scatter(jnp.dot(picked, w_down, preferred_element_type=jnp.float...  68.8 us
    all_gather x1, waiting for transfers between devices, shards(): lax.all_gather(a_local, 'col', axis=0, tiled=True)  33.6 us
    psum x1, blocking collectives, shards(): lax.psum((gate_part, up_part, low_part), 'row')  12.4 us
    dot_general x1, matrix products, shards(): jnp.dot(picked, w_down, preferred_element_type=jnp.float32)  12 us
    unnamed x8, local copies, waits for them, and re-layouts  8.6 us
    dot_general x1, matrix products, shards(): up_part = jnp.dot(flat_tokens, w_up, preferred_element_type=jnp.float32)  6.17 us
  transfers between devices with their start and end apart: 4, of which 3 were waited for; matrix products, arithmetic and copies ran while one was open for 8% of the time, Pallas kernels for 0%

commit v1 on v0

v1 whole, which is shorter than its diff:
```python
import jax
import jax.numpy as jnp
from jax import lax
from jax.sharding import PartitionSpec as P

F32 = jnp.float32
BF16 = jnp.bfloat16


def swap(x, axis, mask):
    n = lax.axis_size(axis)
    return lax.ppermute(x, axis, [(i, i ^ mask) for i in range(n)])


def masks_of(n):
    return [1 << b for b in range(n.bit_length() - 1)]


def col_masks(n):
    out, seen = [], 0
    for b in range(n.bit_length() - 1):
        if b == 0:
            out.append(1)
        else:
            seen |= 1 << b
            out.append(seen if b <= 2 else 1 << b)
    return out


def dest_order(n, masks):
    order = []
    for p in range(n):
        d = 0
        for s, m in enumerate(masks):
            if (p >> s) & 1:
                d ^= m
        order.append(d)
    return order


def pick(x, i, axis=0):
    return lax.dynamic_index_in_dim(x, i, axis, keepdims=False)


CHUNKS = 2


def shards(tokens, task_emb, gen_in, gen_a, gen_b, w_gate, w_up, w_down, group_count, group_task):
    batch, draft, width = tokens.shape
    rows = batch * draft
    rn, cn = lax.axis_size("row"), lax.axis_size("col")
    ri, ci = lax.axis_index("row"), lax.axis_index("col")
    core = ri & 1
    rmasks, cmasks = masks_of(rn), col_masks(cn)
    order = dest_order(cn, cmasks)
    place = jnp.array([order.index(d) for d in range(cn)], jnp.int32)[ci]
    groups = group_count.shape[0]
    hyper_width, slab, rank = gen_a.shape
    _, rank_part, ff = gen_b.shape

    per_dest = rows // cn
    step = per_dest // CHUNKS
    half = step // 2

    def arrange(x):
        x = x.reshape((cn, CHUNKS, 2, half) + x.shape[1:])
        x = jnp.concatenate([x[d : d + 1] for d in order])
        return x.transpose((1, 2, 0, 3) + tuple(range(4, x.ndim)))

    toks = arrange(tokens.reshape(rows, width)).reshape(CHUNKS, 2, cn * half, width)

    ends = jnp.cumsum(group_count)
    request = arrange(jnp.arange(rows, dtype=jnp.int32) // draft).reshape(CHUNKS, 2, cn * half)
    member = (request[..., None] >= (ends - group_count)) & (request[..., None] < ends)

    hyper = jax.nn.silu(
        jnp.dot(jnp.take(task_emb, group_task, axis=0), gen_in, preferred_element_type=F32)
    ).astype(BF16)

    a_local = jnp.dot(hyper, gen_a.reshape(hyper_width, slab * rank), preferred_element_type=F32)
    a_local = a_local.astype(BF16).reshape(groups, slab, rank).transpose(1, 0, 2)
    mine = lax.dynamic_slice_in_dim(toks, ci * slab, slab, 3).reshape(rows, slab)
    wide = jnp.dot(mine, a_local.reshape(slab, groups * rank), preferred_element_type=F32)
    low = jnp.sum(
        wide.reshape(rows, groups, rank) * member.reshape(rows, groups, 1).astype(F32), axis=1
    ).reshape(CHUNKS, 2, cn * half, rank)
    low = pick(low, core, 1) + swap(pick(low, 1 - core, 1), "row", 1)
    for m in rmasks[1:]:
        low = low + swap(low, "row", m)
    for m in cmasks:
        low = low + swap(low, "col", m)
    low = low.astype(BF16)
    low_mine = lax.dynamic_slice_in_dim(low, ri * rank_part, rank_part, 2)
    low_peer = lax.dynamic_slice_in_dim(low, (ri ^ 1) * rank_part, rank_part, 2)

    b_mine = jnp.dot(hyper, gen_b.reshape(hyper_width, rank_part * ff), preferred_element_type=F32)
    b_mine = b_mine.astype(BF16).reshape(groups * rank_part, ff)
    b_peer = swap(b_mine, "row", 1)

    own_member = pick(member, core, 1).astype(BF16)

    def spread(lowk, k):
        return (own_member[k][:, :, None] * lowk[k][:, None, :]).reshape(
            cn * half, groups * rank_part
        )

    keep, give = pick(toks, core, 1), pick(toks, 1 - core, 1)

    def partial(w, k):
        sent = jnp.dot(give[k], w, preferred_element_type=F32).astype(BF16)
        return jnp.dot(keep[k], w, preferred_element_type=F32) + swap(sent, "row", 1).astype(F32)

    def across(x):
        for m in rmasks[1:]:
            x = x + swap(x.astype(BF16), "row", m).astype(F32)
        return x

    gates = [across(partial(w_gate, k)) for k in range(CHUNKS)]
    ups = [partial(w_up, k) for k in range(CHUNKS)]
    outs = []
    for k in range(CHUNKS):
        up = (
            ups[k]
            + jnp.dot(spread(low_mine, k), b_mine, preferred_element_type=F32)
            + jnp.dot(spread(low_peer, k), b_peer, preferred_element_type=F32)
        )
        hid = (jax.nn.silu(gates[k]) * across(up)).astype(BF16)
        other = swap(hid, "row", 1)
        acc = jnp.stack(
            [
                jnp.dot(hid, w_down, preferred_element_type=F32),
                jnp.dot(other, w_down, preferred_element_type=F32),
            ]
        )
        out_width = acc.shape[-1]
        acc = acc.reshape((2,) + (2,) * len(cmasks) + (half, out_width))
        for s, m in enumerate(cmasks):
            dim = acc.ndim - 3
            bit = (place >> s) & 1
            sent = pick(acc, 1 - bit, dim).astype(BF16)
            acc = pick(acc, bit, dim) + swap(sent, "col", m).astype(F32)
        acc = acc.astype(BF16)
        outs.append(jnp.stack([pick(acc, core), pick(acc, 1 - core)]))
    out = jnp.stack(outs)
    return out.reshape(batch // cn, draft, out.shape[-1])


def solution(mesh):
    in_specs = (
        P(None, None, "row"),
        P(),
        P(),
        P(None, ("row", "col"), None),
        P(None, "row", "col"),
        P("row", "col"),
        P("row", "col"),
        P("col", "row"),
        P(),
        P(),
    )
    out_specs = P("col", None, "row")
    return jax.shard_map(shards, mesh=mesh, in_specs=in_specs, out_specs=out_specs, check_vma=False)
```

time: 279 us -> 133 us (0.48)
  waiting for transfers between devices: 205 us -> 52.9 us
  starting transfers between devices: 0.13 us -> 24.6 us
  blocking collectives: 12.4 us -> 0 us
  between operations: 14.7 us -> 2.63 us
  local copies, waits for them, and re-layouts: 14.5 us -> 18.7 us
    psum x1 -> x0, waiting for transfers between devices: 102 us -> none  [shards(): lax.psum((gate_part, up_part, low_part), 'row')]
    reduce_scatter x1 -> x0, waiting for transfers between devices: 68.8 us -> none  [shards(): lax.psum_scatter(jnp.dot(picked, w_down, preferred_element_type=jnp.float...]
    ppermute x0 -> x22, waiting for transfers between devices: none -> 52.9 us  [swap(): return lax.ppermute(x, axis, [(i, i ^ mask) for i in range(n)])]
    all_gather x2 -> x0, waiting for transfers between devices: 33.6 us -> none  [the longest x1 33.6 us: shards(): lax.all_gather(a_local, 'col', axis=0, tiled=True)]
    ppermute x0 -> x22, starting transfers between devices: none -> 24.6 us  [swap(): return lax.ppermute(x, axis, [(i, i ^ mask) for i in range(n)])]
    psum x1 -> x0, blocking collectives: 12.4 us -> none  [shards(): lax.psum((gate_part, up_part, low_part), 'row')]
    unnamed x8 -> x29, local copies, waits for them, and re-layouts: 8.6 us -> 10.8 us
    dot_general x7 -> x20, matrix products: 28.6 us -> 29.7 us  [the longest x4 12 us: partial(): sent = jnp.dot(give[k], w, preferred_element_type=F32).astype(BF16)]
  transfers between devices with their start and end apart: 4 -> 22, of which waited for: 3 -> 11; matrix products, arithmetic and copies ran while one was open for 8% -> 27% of each run, Pallas kernels for 0% -> 0%
where the time goes in v1:
time: 133 us; the launch traced here: 132 us
  waiting for transfers between devices  52.9 us (40%)
  matrix products  29.7 us (22%)
  starting transfers between devices  24.6 us (18%)
  local copies, waits for them, and re-layouts  18.7 us (14%)
  other arithmetic  3.72 us (3%)
  between operations  2.63 us (2%)
    ppermute x22, waiting for transfers between devices, swap(): return lax.ppermute(x, axis, [(i, i ^ mask) for i in range(n)])  52.9 us
    ppermute x22, starting transfers between devices, swap(): return lax.ppermute(x, axis, [(i, i ^ mask) for i in range(n)])  24.6 us
    dot_general x4, matrix products, partial(): sent = jnp.dot(give[k], w, preferred_element_type=F32).astype(BF16)  12 us
    unnamed x29, local copies, waits for them, and re-layouts  10.8 us
    dot_general x4, matrix products, partial(): jnp.dot(keep[k], w, preferred_element_type=F32)  4.5 us
    dot_general x2, matrix products, shards(): jnp.dot(spread(low_peer, k), b_peer, preferred_element_type=F32)  3.28 us
  transfers between devices with their start and end apart: 22, of which 11 were waited for; matrix products, arithmetic and copies ran while one was open for 27% of the time, Pallas kernels for 0%

profile of v1, /device:TPU:0, one launch (start us, length us, event | category | flops | bytes accessed | tf_op | source)
XLA Modules:
  0.0 132.3 jit_solution(3796124032285284972)
XLA Ops:
  0.0 0.7 compare_select_fusion
  0.8 0.7 compare_and_fusion
  1.5 2.0 %fusion.47 = (bf16[32,2,1024]{2,1,0:T(2,128)(2,1)S(1)}, bf16[32,2,1024]{2,1,0:T(2,128)(2,1)S(1)}, bf16[32,2,1024]{2,1,0:T(2,128)(2,1)S(1)}, bf16[32,2,1024]{2,1,...) fusion(bf16[256,2,1024]{2,1,0:T(2,128)(2,1)} %param.11), kind=kLoop, calls=%fused_computation.126 | loop fusion | bytes 2097152 | tf_op jit(solution)/shard_map/slice | solution.py:67
  4.6 4.9 %copy.34 = bf16[512,128,16]{0,2,1:T(8,128)(2,1)} copy(bf16[512,128,16]{1,2,0:T(8,128)(2,1)} %param.14) | data formatting | bytes 4194304 | tf_op args[3]
  9.6 0.7 gather_fusion
  10.3 1.6 %multiply_convert_fusion.2 = bf16[64,512]{1,0:T(8,128)(2,1)S(1)} fusion(bf16[1024,512]{1,0:T(8,128)(2,1)} %param.13, bf16[64,1024]{1,0:T(8,128)(2,1)S(1)} %gather_fusion, pred[64]{0:T(512)(128)(4,1)S(1)} %compare_and_fusion), kind=kOutput, calls=%fused_computation.58 | convolution fusion | flops 67338240 | bytes 1245248 | tf_op jit(solution)/shard_map/dot_general | solution.py:77
  11.9 2.3 %convolution_convert_fusion.5 = bf16[64,2048]{1,0:T(8,128)(2,1)S(1)} fusion(bf16[64,512]{1,0:T(8,128)(2,1)S(1)} %multiply_convert_fusion.2, bf16[512,2048]{0,1:T(8,128)(2,1)} %bitcast.151), kind=kOutput, calls=%fused_computation.6 | convolution fusion | flops 134348800 | bytes 2424832 | tf_op jit(solution)/shard_map/dot_general | solution.py:80
  15.8 3.5 %convolution_convert_fusion.3 = bf16[128,1792]{1,0:T(8,128)(2,1)} fusion(bf16[1024,1792]{1,0:T(8,128)(2,1)} %param.17, bf16[2,2,128,1024]{3,2,1,0:T(8,128)(2,1)S(1)} %bitcast.143, s32[]{:T(128)S(6)} %select_n.83), kind=kOutput, calls=%fused_computation.4 | convolution fusion | flops 469991424 | bytes 4390916 | tf_op jit(solution)/shard_map/dot_general | solution.py:110
  19.3 4.7 %copy.46 = bf16[64,8,4,1792]{3,1,2,0:T(8,128)(2,1)S(1)} copy(bf16[64,8,4,1792]{3,2,1,0:T(4,128)(2,1)} %bitcast.152) | data formatting | bytes 14680064
  24.0 2.3 %convolution_convert_fusion = bf16[64,7168]{1,0:T(8,128)(2,1)} fusion(bf16[64,512]{1,0:T(8,128)(2,1)S(1)} %multiply_convert_fusion.2, bf16[512,7168]{1,0:T(8,128)(2,1)S(1)} %bitcast.141), kind=kOutput, calls=%fused_computation.1 | convolution fusion | flops 470220800 | bytes 8323072 | tf_op jit(solution)/shard_map/dot_general | solution.py:96
  26.3 1.9 %reshape.296 = bf16[256,1792]{1,0:T(8,128)(2,1)S(1)} reshape(bf16[64,7168]{1,0:T(8,128)(2,1)} %convolution_convert_fusion) | data formatting | bytes 1835008 | tf_op jit(solution)/shard_map/reshape | solution.py:97
  28.8 3.5 %convolution_convert_fusion.4 = bf16[128,1792]{1,0:T(8,128)(2,1)} fusion(bf16[1024,1792]{1,0:T(8,128)(2,1)} %param.16, bf16[2,2,128,1024]{3,2,1,0:T(8,128)(2,1)S(1)} %bitcast.144, s32[]{:T(128)S(6)} %select_n.83), kind=kOutput, calls=%fused_computation.5 | convolution fusion | flops 469991424 | bytes 4390916 | tf_op jit(solution)/shard_map/dot_general | solution.py:110
  32.3 3.6 %convolution_convert_fusion.1 = bf16[128,1792]{1,0:T(8,128)(2,1)} fusion(bf16[1024,1792]{1,0:T(8,128)(2,1)} %param.17, bf16[2,2,128,1024]{3,2,1,0:T(8,128)(2,1)S(1)} %bitcast.145, s32[]{:T(128)S(6)} %add.368, s32[]{:T(128)S(6)} %select_n.83), kind=kOutput, calls=%fused_computation.2 | convolution fusion | flops 469991424 | bytes 4390920 | tf_op jit(solution)/shard_map/dot_general | solution.py:110
  36.4 1.6 %fusion.13 = f32[128,1792]{1,0:T(8,128)} fusion(bf16[1024,1792]{1,0:T(8,128)(2,1)S(1)} %copy-done.1, bf16[2,2,128,1024]{3,2,1,0:T(8,128)(2,1)S(1)} %bitcast.146, s32[]{:T(128)S(6)} %select_n.82), kind=kOutput, calls=%fused_computation.45 | convolution fusion | flops 469762048 | bytes 4849668 | tf_op jit(solution)/shard_map/dot_general | solution.py:111
  38.0 1.6 %fusion.15 = f32[128,1792]{1,0:T(8,128)} fusion(bf16[1024,1792]{1,0:T(8,128)(2,1)S(1)} %copy-done.1, bf16[2,2,128,1024]{3,2,1,0:T(8,128)(2,1)S(1)} %bitcast.147, s32[]{:T(128)S(6)} %add.368, s32[]{:T(128)S(6)} %select_n.82), kind=kOutput, calls=%fused_computation.47 | convolution fusion | flops 469762048 | bytes 4849672 | tf_op jit(solution)/shard_map/dot_general | solution.py:111
  39.6 2.5 %collective-permute-start.4 = (f32[2,128,16]{1,2,0:T(8,128)S(1)}, f32[2,128,16]{1,2,0:T(8,128)S(1)}, u32[]{:S(2)}, u32[]{:S(2)}) collective-permute-start(f32[2,128,16]{1,2,0:T(8,128)S(1)} %bitcast_add_fusion.4), channel_id=1, source_target_pairs={{0,16},{8,24},{16,0},{24,8},{1,17},{9,25},{17,1},{25,9},{2,18},{10... | collective-permute-start | bytes 49160 | tf_op jit(solution)/shard_map/ppermute | solution.py:12
  42.1 1.5 %convolution_convert_fusion.2 = bf16[128,1792]{1,0:T(8,128)(2,1)} fusion(bf16[1024,1792]{1,0:T(8,128)(2,1)S(1)} %copy-done.2, bf16[2,2,128,1024]{3,2,1,0:T(8,128)(2,1)S(1)} %bitcast.148, s32[]{:T(128)S(6)} %add.368, s32[]{:T(128)S(6)} %select_n.83), kind=kOutput, calls=%fused_computation.3 | convolution fusion | flops 469991424 | bytes 4390920 | tf_op jit(solution)/shard_map/dot_general | solution.py:110
  43.8 2.0 %collective-permute-start.5 = (f32[2,128,16]{1,2,0:T(8,128)S(1)}, f32[2,128,16]{1,2,0:T(8,128)S(1)}, u32[]{:S(2)}, u32[]{:S(2)}) collective-permute-start(f32[2,128,16]{1,2,0:T(8,128)S(1)} %add.336), channel_id=1, source_target_pairs={{0,1},{1,0},{2,3},{3,2},{4,5},{5,4},{6,7},{7,6},{8,9},{9,8},{10,11... | collective-permute-start | bytes 49160 | tf_op jit(solution)/shard_map/ppermute | solution.py:12
  45.8 1.7 %collective-permute-done.5 = f32[2,128,16]{1,2,0:T(8,128)S(1)} collective-permute-done((f32[2,128,16]{1,2,0:T(8,128)S(1)}, f32[2,128,16]{1,2,0:T(8,128)S(1)}, u32[]{:S(2)}, u32[]{:S(2)}) %collective-permute-start.5) | collective-permute-done | bytes 16416 | tf_op jit(solution)/shard_map/ppermute | solution.py:12
  47.6 2.1 %collective-permute-start.6 = (f32[2,128,16]{1,2,0:T(8,128)S(1)}, f32[2,128,16]{1,2,0:T(8,128)S(1)}, u32[]{:S(2)}, u32[]{:S(2)}) collective-permute-start(f32[2,128,16]{1,2,0:T(8,128)S(1)} %add.337), channel_id=1, source_target_pairs={{0,2},{1,3},{2,0},{3,1},{4,6},{5,7},{6,4},{7,5},{8,10},{9,11},{10,... | collective-permute-start | bytes 49160 | tf_op jit(solution)/shard_map/ppermute | solution.py:12
  49.7 0.7 and_convert_fusion.1
  50.4 1.0 collective-permute-done.6
  51.4 4.0 %collective-permute-start.7 = (f32[2,128,16]{1,2,0:T(8,128)S(1)}, f32[2,128,16]{1,2,0:T(8,128)S(1)}, u32[]{:S(2)}, u32[]{:S(2)}) collective-permute-start(f32[2,128,16]{1,2,0:T(8,128)S(1)} %add.338), channel_id=1, source_target_pairs={{0,6},{1,7},{2,4},{3,5},{4,2},{5,3},{6,0},{7,1},{8,14},{9,15},{10,... | collective-permute-start | bytes 49160 | tf_op jit(solution)/shard_map/ppermute | solution.py:12
  55.4 1.2 dynamic_slice.90
  59.5 1.1 copy-done.3
  60.7 0.7 fusion
  61.3 1.6 %collective-permute-start.1 = (bf16[128,1792]{1,0:T(8,128)(2,1)S(1)}, bf16[128,1792]{1,0:T(8,128)(2,1)S(1)}, u32[]{:S(2)}, u32[]{:S(2)}) collective-permute-start(bf16[128,1792]{1,0:T(8,128)(2,1)S(1)} %get-tuple-element.37), channel_id=1, source_target_pairs={{0,16},{8,24},{16,0},{24,8},{1,17},{9,25},{17,1},{25,9},{2,18},{10... | collective-permute-start | bytes 1376264 | tf_op jit(solution)/shard_map/ppermute | solution.py:12
  62.9 1.6 %fusion.45 = (bf16[128,1792]{1,0:T(8,128)(2,1)S(1)}, f32[128,1792]{1,0:T(8,128)S(1)}) fusion(f32[128,1792]{1,0:T(8,128)S(1)} %fusion.49, f32[128,1792]{1,0:T(8,128)S(1)} %copy-done.5, bf16[128,1792]{1,0:T(8,128)(2,1)} %collective-permute-done.2, bf16[128,256]{0,1:T(8,128)(2,1)S(1)} %bitcast.164, bf16[256,1792]{1,0:T(8,128)(2,1)} %collective-permute-done.8), kind=kOutput, calls=%fused_computation.124 | convolution fusion | flops 118587392 | bytes 4653056 | tf_op jit(solution)/shard_map/dot_general | solution.py:125
  65.2 0.7 fusion.1
  65.8 1.6 %collective-permute-start.15 = (bf16[128,1792]{1,0:T(8,128)(2,1)S(1)}, bf16[128,1792]{1,0:T(8,128)(2,1)S(1)}, u32[]{:S(2)}, u32[]{:S(2)}) collective-permute-start(bf16[128,1792]{1,0:T(8,128)(2,1)S(1)} %get-tuple-element.35), channel_id=1, source_target_pairs={{0,16},{8,24},{16,0},{24,8},{1,17},{9,25},{17,1},{25,9},{2,18},{10... | collective-permute-start | bytes 1376264 | tf_op jit(solution)/shard_map/ppermute | solution.py:12
  67.4 1.6 %fusion.46 = (bf16[128,1792]{1,0:T(8,128)(2,1)S(1)}, f32[128,1792]{1,0:T(8,128)S(1)}) fusion(f32[128,1792]{1,0:T(8,128)S(1)} %fusion.52, f32[128,1792]{1,0:T(8,128)S(1)} %copy-done.6, bf16[128,1792]{1,0:T(8,128)(2,1)} %collective-permute-done.16, bf16[128,256]{0,1:T(8,128)(2,1)S(1)} %bitcast.163, bf16[256,1792]{1,0:T(8,128)(2,1)} %collective-permute-done.8), kind=kOutput, calls=%fused_computation.125 | convolution fusion | flops 118587392 | bytes 4653056 | tf_op jit(solution)/shard_map/dot_general | solution.py:125
  69.6 5.1 %collective-permute-done.1 = bf16[128,1792]{1,0:T(8,128)(2,1)S(1)} collective-permute-done((bf16[128,1792]{1,0:T(8,128)(2,1)S(1)}, bf16[128,1792]{1,0:T(8,128)(2,1)S(1)}, u32[]{:S(2)}, u32[]{:S(2)}) %collective-permute-start.1) | collective-permute-done | bytes 458784 | tf_op jit(solution)/shard_map/ppermute | solution.py:12
  74.8 9.8 %collective-permute-done.9 = bf16[128,1792]{1,0:T(8,128)(2,1)S(1)} collective-permute-done((bf16[128,1792]{1,0:T(8,128)(2,1)S(1)}, bf16[128,1792]{1,0:T(8,128)(2,1)S(1)}, u32[]{:S(2)}, u32[]{:S(2)}) %collective-permute-start.9) | collective-permute-done | bytes 458784 | tf_op jit(solution)/shard_map/ppermute | solution.py:12
  85.1 9.4 %collective-permute-done.15 = bf16[128,1792]{1,0:T(8,128)(2,1)S(1)} collective-permute-done((bf16[128,1792]{1,0:T(8,128)(2,1)S(1)}, bf16[128,1792]{1,0:T(8,128)(2,1)S(1)}, u32[]{:S(2)}, u32[]{:S(2)}) %collective-permute-start.15) | collective-permute-done | bytes 458784 | tf_op jit(solution)/shard_map/ppermute | solution.py:12
  94.5 8.2 %collective-permute-done.17 = bf16[128,1792]{1,0:T(8,128)(2,1)S(1)} collective-permute-done((bf16[128,1792]{1,0:T(8,128)(2,1)S(1)}, bf16[128,1792]{1,0:T(8,128)(2,1)S(1)}, u32[]{:S(2)}, u32[]{:S(2)}) %collective-permute-start.17) | collective-permute-done | bytes 458784 | tf_op jit(solution)/shard_map/ppermute | solution.py:12
  103.1 0.6 fusion.50
  103.8 0.6 fusion.53
  104.5 0.6 fusion.51
  105.2 1.6 %collective-permute-start.11 = (bf16[2,2,2,16,1024]{4,3,2,1,0:T(8,128)(2,1)S(1)}, bf16[2,2,2,16,1024]{4,3,2,1,0:T(8,128)(2,1)S(1)}, u32[]{:S(2)}, u32[]{:S(2)}) collective-permute-start(bf16[2,2,2,16,1024]{4,3,2,1,0:T(8,128)(2,1)S(1)} %fusion.12), channel_id=1, source_target_pairs={{0,1},{1,0},{2,3},{3,2},{4,5},{5,4},{6,7},{7,6},{8,9},{9,8},{10,11... | collective-permute-start | bytes 786440 | tf_op jit(solution)/shard_map/ppermute | solution.py:12
  106.7 0.6 fusion.54
  107.4 0.6 collective-permute-start.19
  108.0 6.4 %collective-permute-done.11 = bf16[2,2,2,16,1024]{4,3,2,1,0:T(8,128)(2,1)S(1)} collective-permute-done((bf16[2,2,2,16,1024]{4,3,2,1,0:T(8,128)(2,1)S(1)}, bf16[2,2,2,16,1024]{4,3,2,1,0:T(8,128)(2,1)S(1)}, u32[]{:S(2)}, u32[]{:S(2)}) %collective-permute-start.11) | collective-permute-done | bytes 262176 | tf_op jit(solution)/shard_map/ppermute | solution.py:12
  114.6 5.0 %collective-permute-done.19 = bf16[2,2,2,16,1024]{4,3,0,1,2:T(8,128)(2,1)S(1)} collective-permute-done((bf16[2,2,2,16,1024]{4,3,0,1,2:T(8,128)(2,1)S(1)}, bf16[2,2,2,16,1024]{4,3,0,1,2:T(8,128)(2,1)S(1)}, u32[]{:S(2)}, u32[]{:S(2)}) %collective-permute-start.19) | collective-permute-done | bytes 262176 | tf_op jit(solution)/shard_map/ppermute | solution.py:12
  119.8 2.3 %collective-permute-start.13 = (bf16[2,16,1024]{2,1,0:T(8,128)(2,1)S(1)}, bf16[2,16,1024]{2,1,0:T(8,128)(2,1)S(1)}, u32[]{:S(2)}, u32[]{:S(2)}) collective-permute-start(bf16[2,16,1024]{2,1,0:T(8,128)(2,1)S(1)} %fusion.26), channel_id=1, source_target_pairs={{0,6},{1,7},{2,4},{3,5},{4,2},{5,3},{6,0},{7,1},{8,14},{9,15},{10,... | collective-permute-start | bytes 196616 | tf_op jit(solution)/shard_map/ppermute | solution.py:12
  122.1 3.2 %collective-permute-done.20 = bf16[2,2,16,1024]{3,2,0,1:T(8,128)(2,1)S(1)} collective-permute-done((bf16[2,2,16,1024]{3,2,0,1:T(8,128)(2,1)S(1)}, bf16[2,2,16,1024]{3,2,0,1:T(8,128)(2,1)S(1)}, u32[]{:S(2)}, u32[]{:S(2)}) %collective-permute-start.20) | collective-permute-done | bytes 131104 | tf_op jit(solution)/shard_map/ppermute | solution.py:12
  125.4 3.2 %collective-permute-start.21 = (bf16[2,16,1024]{2,1,0:T(8,128)(2,1)S(1)}, bf16[2,16,1024]{2,1,0:T(8,128)(2,1)S(1)}, u32[]{:S(2)}, u32[]{:S(2)}) collective-permute-start(bf16[2,16,1024]{2,1,0:T(8,128)(2,1)S(1)} %fusion.27), channel_id=1, source_target_pairs={{0,6},{1,7},{2,4},{3,5},{4,2},{5,3},{6,0},{7,1},{8,14},{9,15},{10,... | collective-permute-start | bytes 196616 | tf_op jit(solution)/shard_map/ppermute | solution.py:12
  128.6 2.9 %collective-permute-done.21 = bf16[2,16,1024]{2,1,0:T(8,128)(2,1)S(1)} collective-permute-done((bf16[2,16,1024]{2,1,0:T(8,128)(2,1)S(1)}, bf16[2,16,1024]{2,1,0:T(8,128)(2,1)S(1)}, u32[]{:S(2)}, u32[]{:S(2)}) %collective-permute-start.21) | collective-permute-done | bytes 65568 | tf_op jit(solution)/shard_map/ppermute | solution.py:12
  131.6 0.7 reshape.297
  (108 shorter events, 7.5 us)
Async XLA Ops:
  0.0 9.6 %copy-start = (bf16[512,1024]{1,0:T(8,128)(2,1)S(1)}, bf16[512,1024]{1,0:T(8,128)(2,1)}, u32[]{:S(2)}) copy-start(bf16[512,1024]{1,0:T(8,128)(2,1)} %param.12) | copy-start | bytes 3145732
  3.5 0.8 copy-start.9
  4.6 10.0 %copy-start.7 = (s32[64]{0:T(128)}, s32[64]{0:T(128)S(1)}, u32[]{:S(2)}) copy-start(s32[64]{0:T(128)S(1)} %reduce) | copy-start | bytes 772
  4.6 10.0 %copy-start.8 = (s32[64]{0:T(128)}, s32[64]{0:T(128)S(1)}, u32[]{:S(2)}) copy-start(s32[64]{0:T(128)S(1)} %sub.33) | copy-start | bytes 772
  15.3 24.3 %collective-permute-start.3 = (f32[2,128,16]{1,2,0:T(8,128)S(1)}, f32[2,128,16]{1,2,0:T(8,128)S(1)}, u32[]{:S(2)}, u32[]{:S(2)}) collective-permute-start(f32[2,128,16]{1,2,0:T(8,128)S(1)} %bitcast.168), channel_id=1, source_target_pairs={{0,8},{8,0},{16,24},{24,16},{1,9},{9,1},{17,25},{25,17},{2,10},{10... | collective-permute-start | bytes 49160 | tf_op jit(solution)/shard_map/ppermute | solution.py:12
  19.3 43.6 %collective-permute-start.2 = (bf16[128,1792]{1,0:T(8,128)(2,1)}, bf16[128,1792]{1,0:T(8,128)(2,1)}, u32[]{:S(2)}, u32[]{:S(2)}) collective-permute-start(bf16[128,1792]{1,0:T(8,128)(2,1)} %convolution_convert_fusion.3), channel_id=1, source_target_pairs={{0,8},{8,0},{16,24},{24,16},{1,9},{9,1},{17,25},{25,17},{2,10},{10... | collective-permute-start | bytes 1376264 | tf_op jit(solution)/shard_map/ppermute | solution.py:12
  28.2 34.7 %collective-permute-start.8 = (bf16[256,1792]{1,0:T(8,128)(2,1)S(1)}, bf16[256,1792]{1,0:T(8,128)(2,1)}, u32[]{:S(2)}, u32[]{:S(2)}) collective-permute-start(bf16[256,1792]{1,0:T(8,128)(2,1)S(1)} %reshape.296), channel_id=1, source_target_pairs={{0,8},{8,0},{16,24},{24,16},{1,9},{9,1},{17,25},{25,17},{2,10},{10... | collective-permute-start | bytes 2752520 | tf_op jit(solution)/shard_map/ppermute | solution.py:12
  32.3 27.3 %collective-permute-start = (bf16[128,1792]{1,0:T(8,128)(2,1)}, bf16[128,1792]{1,0:T(8,128)(2,1)S(1)}, u32[]{:S(2)}, u32[]{:S(2)}) collective-permute-start(bf16[128,1792]{1,0:T(8,128)(2,1)} %convolution_convert_fusion.4), channel_id=1, source_target_pairs={{0,8},{8,0},{16,24},{24,16},{1,9},{9,1},{17,25},{25,17},{2,10},{10... | collective-permute-start | bytes 1376264 | tf_op jit(solution)/shard_map/ppermute | solution.py:12
  32.3 4.1 %copy-start.1 = (bf16[1024,1792]{1,0:T(8,128)(2,1)S(1)}, bf16[1024,1792]{1,0:T(8,128)(2,1)}, u32[]{:S(2)}) copy-start(bf16[1024,1792]{1,0:T(8,128)(2,1)} %param.17) | copy-start | bytes 11010052
  35.9 6.2 %copy-start.2 = (bf16[1024,1792]{1,0:T(8,128)(2,1)S(1)}, bf16[1024,1792]{1,0:T(8,128)(2,1)}, u32[]{:S(2)}) copy-start(bf16[1024,1792]{1,0:T(8,128)(2,1)} %param.16) | copy-start | bytes 11010052
  35.9 31.5 %collective-permute-start.16 = (bf16[128,1792]{1,0:T(8,128)(2,1)}, bf16[128,1792]{1,0:T(8,128)(2,1)}, u32[]{:S(2)}, u32[]{:S(2)}) collective-permute-start(bf16[128,1792]{1,0:T(8,128)(2,1)} %convolution_convert_fusion.1), channel_id=1, source_target_pairs={{0,8},{8,0},{16,24},{24,16},{1,9},{9,1},{17,25},{25,17},{2,10},{10... | collective-permute-start | bytes 1376264 | tf_op jit(solution)/shard_map/ppermute | solution.py:12
  39.6 4.2 %collective-permute-start.4 = (f32[2,128,16]{1,2,0:T(8,128)S(1)}, f32[2,128,16]{1,2,0:T(8,128)S(1)}, u32[]{:S(2)}, u32[]{:S(2)}) collective-permute-start(f32[2,128,16]{1,2,0:T(8,128)S(1)} %bitcast_add_fusion.4), channel_id=1, source_target_pairs={{0,16},{8,24},{16,0},{24,8},{1,17},{9,25},{17,1},{25,9},{2,18},{10... | collective-permute-start | bytes 49160 | tf_op jit(solution)/shard_map/ppermute | solution.py:12
  43.8 3.7 %collective-permute-start.5 = (f32[2,128,16]{1,2,0:T(8,128)S(1)}, f32[2,128,16]{1,2,0:T(8,128)S(1)}, u32[]{:S(2)}, u32[]{:S(2)}) collective-permute-start(f32[2,128,16]{1,2,0:T(8,128)S(1)} %add.336), channel_id=1, source_target_pairs={{0,1},{1,0},{2,3},{3,2},{4,5},{5,4},{6,7},{7,6},{8,9},{9,8},{10,11... | collective-permute-start | bytes 49160 | tf_op jit(solution)/shard_map/ppermute | solution.py:12
  47.6 3.8 %collective-permute-start.6 = (f32[2,128,16]{1,2,0:T(8,128)S(1)}, f32[2,128,16]{1,2,0:T(8,128)S(1)}, u32[]{:S(2)}, u32[]{:S(2)}) collective-permute-start(f32[2,128,16]{1,2,0:T(8,128)S(1)} %add.337), channel_id=1, source_target_pairs={{0,2},{1,3},{2,0},{3,1},{4,6},{5,7},{6,4},{7,5},{8,10},{9,11},{10,... | collective-permute-start | bytes 49160 | tf_op jit(solution)/shard_map/ppermute | solution.py:12
  51.4 7.3 %collective-permute-start.7 = (f32[2,128,16]{1,2,0:T(8,128)S(1)}, f32[2,128,16]{1,2,0:T(8,128)S(1)}, u32[]{:S(2)}, u32[]{:S(2)}) collective-permute-start(f32[2,128,16]{1,2,0:T(8,128)S(1)} %add.338), channel_id=1, source_target_pairs={{0,6},{1,7},{2,4},{3,5},{4,2},{5,3},{6,0},{7,1},{8,14},{9,15},{10,... | collective-permute-start | bytes 49160 | tf_op jit(solution)/shard_map/ppermute | solution.py:12
  58.6 2.0 %copy-start.3 = (bf16[1024,1792]{1,0:T(8,128)(2,1)S(1)}, bf16[1024,1792]{1,0:T(8,128)(2,1)}, u32[]{:S(2)}) copy-start(bf16[1024,1792]{1,0:T(8,128)(2,1)} %param.16) | copy-start | bytes 11010052
  58.6 6.5 %collective-permute-start.14 = (bf16[128,1792]{1,0:T(8,128)(2,1)}, bf16[128,1792]{1,0:T(8,128)(2,1)S(1)}, u32[]{:S(2)}, u32[]{:S(2)}) collective-permute-start(bf16[128,1792]{1,0:T(8,128)(2,1)} %convolution_convert_fusion.2), channel_id=1, source_target_pairs={{0,8},{8,0},{16,24},{24,16},{1,9},{9,1},{17,25},{25,17},{2,10},{10... | collective-permute-start | bytes 1376264 | tf_op jit(solution)/shard_map/ppermute | solution.py:12
  59.2 3.7 %copy-start.5 = (f32[128,1792]{1,0:T(8,128)S(1)}, f32[128,1792]{1,0:T(8,128)}, u32[]{:S(2)}) copy-start(f32[128,1792]{1,0:T(8,128)} %fusion.13) | copy-start | bytes 2752516
  61.3 13.5 %collective-permute-start.1 = (bf16[128,1792]{1,0:T(8,128)(2,1)S(1)}, bf16[128,1792]{1,0:T(8,128)(2,1)S(1)}, u32[]{:S(2)}, u32[]{:S(2)}) collective-permute-start(bf16[128,1792]{1,0:T(8,128)(2,1)S(1)} %get-tuple-element.37), channel_id=1, source_target_pairs={{0,16},{8,24},{16,0},{24,8},{1,17},{9,25},{17,1},{25,9},{2,18},{10... | collective-permute-start | bytes 1376264 | tf_op jit(solution)/shard_map/ppermute | solution.py:12
  64.6 2.8 %copy-start.6 = (f32[128,1792]{1,0:T(8,128)S(1)}, f32[128,1792]{1,0:T(8,128)}, u32[]{:S(2)}) copy-start(f32[128,1792]{1,0:T(8,128)} %fusion.15) | copy-start | bytes 2752516
  64.6 20.0 %collective-permute-start.9 = (bf16[128,1792]{1,0:T(8,128)(2,1)S(1)}, bf16[128,1792]{1,0:T(8,128)(2,1)S(1)}, u32[]{:S(2)}, u32[]{:S(2)}) collective-permute-start(bf16[128,1792]{1,0:T(8,128)(2,1)S(1)} %get-tuple-element.5), channel_id=1, source_target_pairs={{0,16},{8,24},{16,0},{24,8},{1,17},{9,25},{17,1},{25,9},{2,18},{10... | collective-permute-start | bytes 1376264 | tf_op jit(solution)/shard_map/ppermute | solution.py:12
  65.8 28.6 %collective-permute-start.15 = (bf16[128,1792]{1,0:T(8,128)(2,1)S(1)}, bf16[128,1792]{1,0:T(8,128)(2,1)S(1)}, u32[]{:S(2)}, u32[]{:S(2)}) collective-permute-start(bf16[128,1792]{1,0:T(8,128)(2,1)S(1)} %get-tuple-element.35), channel_id=1, source_target_pairs={{0,16},{8,24},{16,0},{24,8},{1,17},{9,25},{17,1},{25,9},{2,18},{10... | collective-permute-start | bytes 1376264 | tf_op jit(solution)/shard_map/ppermute | solution.py:12
  69.1 33.6 %collective-permute-start.17 = (bf16[128,1792]{1,0:T(8,128)(2,1)S(1)}, bf16[128,1792]{1,0:T(8,128)(2,1)S(1)}, u32[]{:S(2)}, u32[]{:S(2)}) collective-permute-start(bf16[128,1792]{1,0:T(8,128)(2,1)S(1)} %get-tuple-element.7), channel_id=1, source_target_pairs={{0,16},{8,24},{16,0},{24,8},{1,17},{9,25},{17,1},{25,9},{2,18},{10... | collective-permute-start | bytes 1376264 | tf_op jit(solution)/shard_map/ppermute | solution.py:12
  84.6 18.5 %copy-start.4 = (bf16[1792,1024]{1,0:T(8,128)(2,1)S(1)}, bf16[1792,1024]{1,0:T(8,128)(2,1)}, u32[]{:S(2)}) copy-start(bf16[1792,1024]{1,0:T(8,128)(2,1)} %param.18) | copy-start | bytes 11010052
  85.0 19.5 %collective-permute-start.10 = (bf16[128,1792]{1,0:T(8,128)(2,1)S(1)}, bf16[128,1792]{1,0:T(8,128)(2,1)S(1)}, u32[]{:S(2)}, u32[]{:S(2)}) collective-permute-start(bf16[128,1792]{1,0:T(8,128)(2,1)S(1)} %multiply_convert_fusion.1), channel_id=1, source_target_pairs={{0,8},{8,0},{16,24},{24,16},{1,9},{9,1},{17,25},{25,17},{2,10},{10... | collective-permute-start | bytes 1376264 | tf_op jit(solution)/shard_map/ppermute | solution.py:12
  103.7 3.0 %collective-permute-start.18 = (bf16[128,1792]{1,0:T(8,128)(2,1)S(1)}, bf16[128,1792]{1,0:T(8,128)(2,1)S(1)}, u32[]{:S(2)}, u32[]{:S(2)}) collective-permute-start(bf16[128,1792]{1,0:T(8,128)(2,1)S(1)} %multiply_convert_fusion), channel_id=1, source_target_pairs={{0,8},{8,0},{16,24},{24,16},{1,9},{9,1},{17,25},{25,17},{2,10},{10... | collective-permute-start | bytes 1376264 | tf_op jit(solution)/shard_map/ppermute | solution.py:12
  105.2 9.2 %collective-permute-start.11 = (bf16[2,2,2,16,1024]{4,3,2,1,0:T(8,128)(2,1)S(1)}, bf16[2,2,2,16,1024]{4,3,2,1,0:T(8,128)(2,1)S(1)}, u32[]{:S(2)}, u32[]{:S(2)}) collective-permute-start(bf16[2,2,2,16,1024]{4,3,2,1,0:T(8,128)(2,1)S(1)} %fusion.12), channel_id=1, source_target_pairs={{0,1},{1,0},{2,3},{3,2},{4,5},{5,4},{6,7},{7,6},{8,9},{9,8},{10,11... | collective-permute-start | bytes 786440 | tf_op jit(solution)/shard_map/ppermute | solution.py:12
  107.4 12.1 %collective-permute-start.19 = (bf16[2,2,2,16,1024]{4,3,0,1,2:T(8,128)(2,1)S(1)}, bf16[2,2,2,16,1024]{4,3,0,1,2:T(8,128)(2,1)S(1)}, u32[]{:S(2)}, u32[]{:S(2)}) collective-permute-start(bf16[2,2,2,16,1024]{4,3,0,1,2:T(8,128)(2,1)S(1)} %fusion.11), channel_id=1, source_target_pairs={{0,1},{1,0},{2,3},{3,2},{4,5},{5,4},{6,7},{7,6},{8,9},{9,8},{10,11... | collective-permute-start | bytes 786440 | tf_op jit(solution)/shard_map/ppermute | solution.py:12
  114.5 5.2 %collective-permute-start.12 = (bf16[2,2,16,1024]{3,2,1,0:T(8,128)(2,1)S(1)}, bf16[2,2,16,1024]{3,2,1,0:T(8,128)(2,1)S(1)}, u32[]{:S(2)}, u32[]{:S(2)}) collective-permute-start(bf16[2,2,16,1024]{3,2,1,0:T(8,128)(2,1)S(1)} %fusion.17), channel_id=1, source_target_pairs={{0,2},{1,3},{2,0},{3,1},{4,6},{5,7},{6,4},{7,5},{8,10},{9,11},{10,... | collective-permute-start | bytes 393224 | tf_op jit(solution)/shard_map/ppermute | solution.py:12
  119.7 5.6 %collective-permute-start.20 = (bf16[2,2,16,1024]{3,2,0,1:T(8,128)(2,1)S(1)}, bf16[2,2,16,1024]{3,2,0,1:T(8,128)(2,1)S(1)}, u32[]{:S(2)}, u32[]{:S(2)}) collective-permute-start(bf16[2,2,16,1024]{3,2,0,1:T(8,128)(2,1)S(1)} %fusion.18), channel_id=1, source_target_pairs={{0,2},{1,3},{2,0},{3,1},{4,6},{5,7},{6,4},{7,5},{8,10},{9,11},{10,... | collective-permute-start | bytes 393224 | tf_op jit(solution)/shard_map/ppermute | solution.py:12
  119.8 8.7 %collective-permute-start.13 = (bf16[2,16,1024]{2,1,0:T(8,128)(2,1)S(1)}, bf16[2,16,1024]{2,1,0:T(8,128)(2,1)S(1)}, u32[]{:S(2)}, u32[]{:S(2)}) collective-permute-start(bf16[2,16,1024]{2,1,0:T(8,128)(2,1)S(1)} %fusion.26), channel_id=1, source_target_pairs={{0,6},{1,7},{2,4},{3,5},{4,2},{5,3},{6,0},{7,1},{8,14},{9,15},{10,... | collective-permute-start | bytes 196616 | tf_op jit(solution)/shard_map/ppermute | solution.py:12
  125.4 6.1 %collective-permute-start.21 = (bf16[2,16,1024]{2,1,0:T(8,128)(2,1)S(1)}, bf16[2,16,1024]{2,1,0:T(8,128)(2,1)S(1)}, u32[]{:S(2)}, u32[]{:S(2)}) collective-permute-start(bf16[2,16,1024]{2,1,0:T(8,128)(2,1)S(1)} %fusion.27), channel_id=1, source_target_pairs={{0,6},{1,7},{2,4},{3,5},{4,2},{5,3},{6,0},{7,1},{8,14},{9,15},{10,... | collective-permute-start | bytes 196616 | tf_op jit(solution)/shard_map/ppermute | solution.py:12

commit v2 on v1

v2 whole, which is shorter than its diff:
```python
import functools

import jax
import jax.numpy as jnp
import numpy as np
from jax import lax
from jax.experimental import pallas as pl
from jax.experimental.pallas import tpu as pltpu
from jax.sharding import PartitionSpec as P


F32 = jnp.float32
BF16 = jnp.bfloat16
CHUNKS = (1, 1)


def swap(x, axis, mask):
    n = lax.axis_size(axis)
    return lax.ppermute(x, axis, [(i, i ^ mask) for i in range(n)])


def masks_of(n):
    return [1 << b for b in range(n.bit_length() - 1)]


def pick(x, i, axis=0):
    return lax.dynamic_index_in_dim(x, i, axis, keepdims=False)


def stay(x):
    return pltpu.with_memory_space_constraint(x, pltpu.HBM)


def halves_of(n):
    return n // 2 if (n // 2) % 128 == 0 else n


def rows_of(tok_ref, request, size):
    draft, width = tok_ref.shape[1:]
    return tok_ref[pl.ds(request, size // draft)].reshape(size, width)


def split_store(x, w_ref, kept_ref, sent_ref, columns):
    half = x.shape[0] // 2
    both = jnp.dot(x, w_ref[:, columns], preferred_element_type=F32)
    kept_ref[:, columns] = both[:half]
    sent_ref[:, columns] = both[half:].astype(BF16)


def low_kernel(
    blocks, slab, shift, lead_ref, count_hbm, task_hbm, request_hbm, tok_hbm, emb_hbm, gen_in_hbm, a_hbm,
    w_hbm, *rest
):
    x_in, rest = (None, rest) if slab % 128 == 0 else (rest[0], rest[1:])
    low_ref, peer_ref, hyper_ref, member_ref, toks_ref, kept_ref, sent_ref = rest[:7]
    count_ref, task_ref, request_ref, tok_ref, emb_ref, gen_in_ref, a_ref, w_ref, ht_ref, sems = rest[7:]
    copies = [
        pltpu.make_async_copy(src, dst, sems.at[i])
        for i, (src, dst) in enumerate(
            (
                (task_hbm, task_ref),
                (count_hbm, count_ref),
                (request_hbm, request_ref),
                (emb_hbm, emb_ref),
                (gen_in_hbm, gen_in_ref),
                (tok_hbm, tok_ref),
                (a_hbm, a_ref),
                (w_hbm, w_ref),
            )
        )
    ]
    for copy in copies:
        copy.start()
    groups = count_ref.shape[1]
    tasks = emb_ref.shape[0]
    hidden = gen_in_ref.shape[1]
    rank, half = low_ref.shape
    rows = 2 * half
    core = lead_ref[1]
    across_rows = (((0,), (0,)), ((), ()))
    for copy in copies[:3]:
        copy.wait()
    chosen = lax.broadcasted_iota(jnp.int32, (tasks, groups), 0) == task_ref[...]
    chosen = chosen.astype(F32).astype(BF16)
    at = lax.broadcasted_iota(jnp.int32, (groups, groups), 0)
    of = lax.broadcasted_iota(jnp.int32, (groups, groups), 1)
    ends = jnp.sum(jnp.where(of <= at, count_ref[...], 0), axis=1, keepdims=True)
    starts = jnp.sum(jnp.where(of < at, count_ref[...], 0), axis=1, keepdims=True)
    first = lax.broadcasted_iota(jnp.int32, (1, rows), 1) < half
    request = request_ref[...] + shift * jnp.where(first, core, 1 - core)
    member = ((request >= starts) & (request < ends)).astype(F32).astype(BF16)
    member_ref[...] = member[:, :half]
    copies[3].wait()
    chosen = lax.dot_general(chosen, emb_ref[...], across_rows, preferred_element_type=F32)
    copies[4].wait()
    hyper = jnp.dot(chosen.astype(BF16), gen_in_ref[...], preferred_element_type=F32)
    hyper = (hyper * (1.0 / (1.0 + jnp.exp(-hyper)))).astype(BF16)
    hyper_ref[...] = hyper
    ht_ref[...] = lax.dot_general(hyper, member, across_rows, preferred_element_type=F32)
    copies[5].wait()
    for side in range(2):
        for source, target, size in blocks:
            begin = source + shift * (core if side == 0 else 1 - core)
            toks_ref[side * half + target : side * half + target + size, :] = rows_of(
                tok_ref, begin, size
            )
    x = toks_ref[:, pl.ds(pl.multiple_of(lead_ref[0], 128), slab)] if x_in is None else x_in[...]
    xt = x.T
    copies[6].wait()
    part = hidden // 4

    def body(i, acc):
        h = pl.multiple_of(i * part, part)
        t = jnp.dot(
            a_ref[pl.ds(pl.multiple_of(h * rank, part * rank), part * rank), :],
            xt,
            preferred_element_type=F32,
        ).reshape(part, rank, rows)
        return acc + jnp.sum(t * ht_ref[pl.ds(h, part), :][:, None, :], axis=0)

    low = lax.fori_loop(0, hidden // part, body, jnp.zeros((rank, rows), F32))
    low_ref[...] = low[:, :half]
    peer_ref[...] = low[:, half:]
    copies[7].wait()
    ff = w_ref.shape[1]
    tile = halves_of(ff)
    for j in range(0, ff, tile):
        split_store(toks_ref[...], w_ref, kept_ref, sent_ref, slice(j, j + tile))


def low_part(blocks, shift, lead, count, task, request, tokens, emb, gen_in, a, w, x):
    hidden, slab, rank = a.shape
    groups, rows = count.shape[1], request.shape[1]
    width, ff = w.shape
    a = a.transpose(0, 2, 1).reshape(hidden * rank, slab)
    vmem = pl.BlockSpec(memory_space=pltpu.VMEM)
    hbm = pl.BlockSpec(memory_space=pltpu.HBM)
    moved = (count, task, request, tokens, emb, gen_in, a, w)
    extra = () if x is None else (x,)
    return pl.pallas_call(
        functools.partial(low_kernel, blocks, slab, shift),
        in_specs=[pl.BlockSpec(memory_space=pltpu.SMEM)] + [hbm] * len(moved) + [vmem] * len(extra),
        out_specs=[vmem] * 7,
        out_shape=(
            jax.ShapeDtypeStruct((rank, rows // 2), F32),
            jax.ShapeDtypeStruct((rank, rows // 2), F32),
            jax.ShapeDtypeStruct((groups, hidden), BF16),
            jax.ShapeDtypeStruct((groups, rows // 2), BF16),
            jax.ShapeDtypeStruct((rows, width), BF16),
            jax.ShapeDtypeStruct((rows // 2, ff), F32),
            jax.ShapeDtypeStruct((rows // 2, ff), BF16),
        ),
        scratch_shapes=[pltpu.VMEM(m.shape, m.dtype) for m in moved]
        + [pltpu.VMEM((hidden, rows), F32), pltpu.SemaphoreType.DMA((len(moved),))],
        compiler_params=pltpu.CompilerParams(vmem_limit_bytes=36 << 20),
        name="low_part",
    )(lead, *[stay(m) for m in moved], *extra)


def split_kernel(x_ref, w_ref, kept_ref, sent_ref):
    split_store(x_ref[...], w_ref, kept_ref, sent_ref, slice(None))


def split_matmul(x, w):
    rows, width = x.shape
    ff = w.shape[1]
    tile = halves_of(ff)
    return pl.pallas_call(
        split_kernel,
        grid=(ff // tile,),
        in_specs=[
            pl.BlockSpec((rows, width), lambda i: (0, 0)),
            pl.BlockSpec((width, tile), lambda i: (0, i)),
        ],
        out_specs=[
            pl.BlockSpec((rows // 2, tile), lambda i: (0, i)),
            pl.BlockSpec((rows // 2, tile), lambda i: (0, i)),
        ],
        out_shape=(
            pltpu.HBM((rows // 2, ff), F32),
            jax.ShapeDtypeStruct((rows // 2, ff), BF16),
        ),
        compiler_params=pltpu.CompilerParams(vmem_limit_bytes=16 << 20),
    )(x, w)


def factor_kernel(hyper_ref, gen_ref, out_ref, wide_ref):
    hidden, ranks, tile = gen_ref.shape
    groups = hyper_ref.shape[0]

    @pl.when(pl.program_id(0) == 0)
    def _():
        part = 128
        spread = part * ranks
        lane = lax.broadcasted_iota(jnp.int32, (part, spread), 1)
        first = lax.broadcasted_iota(jnp.int32, (part, spread), 0) * ranks
        repeat = ((lane >= first) & (lane < first + ranks)).astype(F32).astype(BF16)
        which = lax.rem(lax.broadcasted_iota(jnp.int32, (groups, spread), 1), ranks)
        for k in range(hidden // part):
            wide = jnp.dot(
                hyper_ref[:, k * part : (k + 1) * part], repeat, preferred_element_type=F32
            )
            for r in range(ranks):
                wide_ref[r * groups : (r + 1) * groups, k * spread : (k + 1) * spread] = jnp.where(
                    which == r, wide, 0.0
                ).astype(BF16)

    out_ref[...] = jnp.dot(
        wide_ref[...], gen_ref[...].reshape(hidden * ranks, tile), preferred_element_type=F32
    ).astype(BF16)


def factors(hyper, gen_b):
    hidden, ranks, ff = gen_b.shape
    groups = hyper.shape[0]
    tile = halves_of(ff)
    return pl.pallas_call(
        factor_kernel,
        grid=(ff // tile,),
        in_specs=[
            pl.BlockSpec((groups, hidden), lambda i: (0, 0)),
            pl.BlockSpec((hidden, ranks, tile), lambda i: (0, 0, i)),
        ],
        out_specs=pl.BlockSpec((ranks * groups, tile), lambda i: (0, i)),
        out_shape=jax.ShapeDtypeStruct((ranks * groups, ff), BF16),
        scratch_shapes=[pltpu.VMEM((ranks * groups, hidden * ranks), BF16)],
        compiler_params=pltpu.CompilerParams(vmem_limit_bytes=24 << 20),
        name="factors",
    )(hyper, gen_b)


def delta_kernel(pieces, rank_ref, low_ref, member_ref, mine_ref, peer_ref, kept_ref, got_ref, sum_ref, *sent):
    groups = member_ref.shape[0]
    ranks = mine_ref.shape[0] // groups
    member = member_ref[...].astype(F32)
    total = kept_ref[...] + got_ref[...].astype(F32)
    for which, factor in ((0, mine_ref), (1, peer_ref)):
        first = rank_ref[which]
        spread = jnp.concatenate(
            [
                (member * low_ref[pl.ds(first + r, 1), :].astype(BF16).astype(F32)).astype(BF16)
                for r in range(ranks)
            ],
            axis=0,
        )
        total += lax.dot_general(
            spread, factor[...], (((0,), (0,)), ((), ())), preferred_element_type=F32
        )
    sum_ref[...] = total
    total = total.astype(BF16)
    for (start, size), ref in zip(pieces, sent):
        ref[...] = total[start : start + size]


def add_adapter(pieces, first_ranks, low, member, mine, peer, kept, got):
    rows, ff = kept.shape
    tile = halves_of(ff)
    whole = lambda x: pl.BlockSpec(x.shape, lambda i, c: (0, 0))
    cut = lambda n: pl.BlockSpec((n, tile), lambda i, c: (0, i))
    return pl.pallas_call(
        functools.partial(delta_kernel, pieces),
        grid_spec=pltpu.PrefetchScalarGridSpec(
            num_scalar_prefetch=1,
            grid=(ff // tile,),
            in_specs=[whole(low), whole(member)] + [cut(x.shape[0]) for x in (mine, peer, kept, got)],
            out_specs=[cut(rows)] + [cut(size) for _, size in pieces],
        ),
        out_shape=[pltpu.VMEM((rows, ff), F32)]
        + [jax.ShapeDtypeStruct((size, ff), BF16) for _, size in pieces],
        compiler_params=pltpu.CompilerParams(vmem_limit_bytes=16 << 20),
        name="adapter",
    )(first_ranks, low, member, mine, peer, stay(kept), got)


def gate_kernel(kept_ref, core_ref, rest_ref, later_ref, out_ref):
    gate = kept_ref[...] + core_ref[...].astype(F32) + rest_ref[...].astype(F32)
    out_ref[...] = gate * (1.0 / (1.0 + jnp.exp(-gate)))


def activate(kept, core_got, rest, later):
    return in_vmem(gate_kernel, pltpu.VMEM(kept.shape, F32), kept, core_got, rest, later)


def in_vmem(kernel, out, *args):
    vmem = pl.BlockSpec(memory_space=pltpu.VMEM)
    return pl.pallas_call(
        kernel,
        in_specs=[vmem] * len(args),
        out_specs=vmem,
        out_shape=out,
        compiler_params=pltpu.CompilerParams(vmem_limit_bytes=8 << 20),
    )(*args)


def hidden_kernel(start, act_ref, half_ref, up_ref, out_ref):
    at = slice(start, start + out_ref.shape[0])
    out_ref[...] = (act_ref[at] * (half_ref[at] + up_ref[...].astype(F32))).astype(BF16)


def hidden_units(piece, act, half, up_got):
    start, size = piece
    out = jax.ShapeDtypeStruct((size, act.shape[1]), BF16)
    return in_vmem(functools.partial(hidden_kernel, start), out, act, half, up_got)


def shards(tokens, task_emb, gen_in, gen_a, gen_b, w_gate, w_up, w_down, group_count, group_task):
    batch, draft, _ = tokens.shape
    rows = batch * draft
    rn, cn = lax.axis_size("row"), lax.axis_size("col")
    ri, ci = lax.axis_index("row"), lax.axis_index("col")
    core = ri & 1
    rmasks, cmasks = masks_of(rn), masks_of(cn)
    slab = gen_a.shape[1]
    rank_part, _ = gen_b.shape[1:]

    per_dest = rows // cn
    sizes = [per_dest * part // sum(CHUNKS) for part in CHUNKS]
    blocks, pieces, target, source = [], [], 0, 0
    for size in sizes:
        pieces.append((target, cn * size // 2))
        for d in range(cn):
            blocks.append(((d * per_dest + source) // draft, target, size // 2))
            target += size // 2
        source += size // 2
    shift = per_dest // 2 // draft

    request = np.concatenate([begin + np.arange(size) // draft for begin, _, size in blocks])
    request = np.concatenate([request, request])[None, :].astype(np.int32)
    x = None
    if slab % 128:
        x = lax.dynamic_slice_in_dim(tokens, ci * slab, slab, 2)
        x = jnp.concatenate(
            [
                lax.dynamic_slice_in_dim(x, begin + shift * side, size // draft).reshape(size, slab)
                for side in (core, 1 - core)
                for begin, _, size in blocks
            ]
        )
    low, low_sent, hyper, own_member, toks, gate_kept, gate_sent = low_part(
        tuple(blocks),
        shift,
        jnp.stack([ci * slab, core]),
        group_count[None, :],
        group_task[None, :],
        jnp.asarray(request),
        tokens,
        task_emb,
        gen_in,
        gen_a,
        w_gate,
        x,
    )
    low = low + swap(low_sent, "row", 1)
    gate_got = swap(gate_sent, "row", 1)
    for m in rmasks[1:]:
        low = low + swap(low, "row", m)
    gate_sum = (gate_kept + gate_got.astype(F32)).astype(BF16)

    def others(sent):
        total = None
        for s, m in enumerate(rmasks[1:]):
            got = swap(sent, "row", m)
            if s + 2 == len(rmasks) and total is None:
                return got
            total = got.astype(F32) if total is None else total + got.astype(F32)
            sent = (sent.astype(F32) + got.astype(F32)).astype(BF16)
        return total

    gate_rest = others(gate_sum)

    up_kept, up_sent = split_matmul(toks, w_up)
    up_got = swap(up_sent, "row", 1)
    b_mine = factors(hyper, gen_b)
    b_peer = swap(b_mine, "row", 1)
    for m in cmasks:
        low = low + swap(low, "col", m)

    first_ranks = jnp.stack([ri * rank_part, (ri ^ 1) * rank_part])
    up_half, *up_sums = add_adapter(
        tuple(pieces), first_ranks, low, own_member, b_mine, b_peer, up_kept, up_got
    )

    act = activate(gate_kept, gate_got, gate_rest, w_down)
    outs = []
    for k, piece in enumerate(pieces):
        up_rest = others(up_sums[k])
        hid = hidden_units(piece, act, up_half, up_rest)
        other = swap(hid, "row", 1)
        acc = jnp.dot(hid, w_down, preferred_element_type=F32)
        acc = jnp.stack([acc, jnp.dot(other, w_down, preferred_element_type=F32)])
        out_width = acc.shape[-1]
        acc = acc.reshape((2,) + (2,) * len(cmasks) + (sizes[k] // 2, out_width))
        for s, m in enumerate(cmasks):
            dim = acc.ndim - 3
            bit = (ci >> s) & 1
            sent = pick(acc, 1 - bit, dim).astype(BF16)
            acc = pick(acc, bit, dim) + swap(sent, "col", m).astype(F32)
        acc = acc.astype(BF16)
        outs.append(jnp.stack([pick(acc, core), pick(acc, 1 - core)]))
    out = jnp.concatenate(outs, axis=1)
    return out.reshape(batch // cn, draft, out.shape[-1])


def solution(mesh):
    in_specs = (
        P(None, None, "row"),
        P(),
        P(),
        P(None, ("row", "col"), None),
        P(None, "row", "col"),
        P("row", "col"),
        P("row", "col"),
        P("col", "row"),
        P(),
        P(),
    )
    out_specs = P("col", None, "row")

    return jax.shard_map(shards, mesh=mesh, in_specs=in_specs, out_specs=out_specs, check_vma=False)
```

time: 133 us -> 109 us (0.82)
  matrix products: 29.7 us -> 2.58 us
  Pallas kernels: 0 us -> 22.9 us
  local copies, waits for them, and re-layouts: 18.7 us -> 7.74 us
  waiting for transfers between devices: 52.9 us -> 50 us
  between operations: 2.63 us -> 0.26 us
  other arithmetic: 3.72 us -> 1.64 us
    dot_general x20 -> x4, matrix products: 29.7 us -> 2.58 us  [the longest x2 1.29 us: shards(): acc = jnp.dot(hid, w_down, preferred_element_type=F32)]
    pallas_call x0 -> x7, Pallas kernels: none -> 22.9 us  [the longest x1 8.64 us: low_part(): pl.pallas_call(functools.partial(low_kernel, blocks, slab, shift), in_spe...]
    unnamed x29 -> x20, local copies, waits for them, and re-layouts: 10.8 us -> 6.92 us
    ppermute x22 -> x19, waiting for transfers between devices: 52.9 us -> 50 us  [swap(): return lax.ppermute(x, axis, [(i, i ^ mask) for i in range(n)])]
    slice x11 -> x0, local copies, waits for them, and re-layouts: 2.43 us -> none  [arrange(): x = jnp.concatenate([x[d:d + 1] for d in order])]
    reshape x2 -> x0, local copies, waits for them, and re-layouts: 1.94 us -> none  [the longest x1 1.92 us: shards(): b_mine = b_mine.astype(BF16).reshape(groups * rank_part, ff)]
    ppermute x22 -> x19, starting transfers between devices: 24.6 us -> 23.7 us  [swap(): return lax.ppermute(x, axis, [(i, i ^ mask) for i in range(n)])]
  transfers between devices with their start and end apart: 22 -> 19, of which waited for: 11 -> 11; matrix products, arithmetic and copies ran while one was open for 27% -> 4% of each run, Pallas kernels for 0% -> 13%
where the time goes in v2:
time: 109 us
  waiting for transfers between devices  50 us (46%)
  starting transfers between devices  23.7 us (22%)
  Pallas kernels  22.9 us (21%)
  local copies, waits for them, and re-layouts  7.74 us (7%)
  matrix products  2.58 us (2%)
  other arithmetic  1.64 us (2%)
    ppermute x19, waiting for transfers between devices, swap(): return lax.ppermute(x, axis, [(i, i ^ mask) for i in range(n)])  50 us
    ppermute x19, starting transfers between devices, swap(): return lax.ppermute(x, axis, [(i, i ^ mask) for i in range(n)])  23.7 us
    pallas_call x1, Pallas kernels, low_part(): pl.pallas_call(functools.partial(low_kernel, blocks, slab, shift), in_spe...  8.64 us
    unnamed x20, local copies, waits for them, and re-layouts  6.92 us
    pallas_call x1, Pallas kernels, split_matmul(): pl.pallas_call(split_kernel, grid=(ff // tile,), in_specs=[pl.BlockSpec((...  3.9 us
    pallas_call x1, Pallas kernels, add_adapter(): pl.pallas_call(functools.partial(delta_kernel, pieces), grid_spec=pltpu.P...  3.81 us
    pallas_call x1, Pallas kernels, factors(): pl.pallas_call(factor_kernel, grid=(ff // tile,), in_specs=[pl.BlockSpec(...  3.55 us
    pallas_call x3, Pallas kernels, in_vmem(): pl.pallas_call(kernel, in_specs=[vmem] * len(args), out_specs=vmem, out_s...  3.02 us
  transfers between devices with their start and end apart: 19, of which 11 were waited for; matrix products, arithmetic and copies ran while one was open for 4% of the time, Pallas kernels for 13%

profile of v2, /device:TPU:0, one launch (start us, length us, event | category | flops | bytes accessed | tf_op | source)
XLA Modules:
  0.0 108.8 jit_solution(7196218424539251831)
XLA Ops:
  0.0 0.1 pad_add_fusion.lead_ref
  0.1 8.6 %low_part.1 = (f32[16,256]{1,0:T(8,128)S(1)}, f32[16,256]{1,0:T(8,128)S(1)}, bf16[64,512]{1,0:T(8,128)(2,1)S(1)}, bf16[64,256]{1,0:T(8,128)(2,1)S(1)}, bf16[512,...) custom-call(s32[2]{0:T(128)S(1)} %pad_add_fusion.lead_ref, s32[1,64]{1,0:T(1,128)} %bitcast.62, ...), custom_call_target="tpu_custom_call" | custom-call | tf_op jit(solution)/shard_map/low_part/pallas_call | solution.py:140
  8.7 0.6 collective-permute-start
  9.3 3.5 %factors.1.mine_ref = bf16[256,1792]{1,0:T(8,128)(2,1)S(1)} custom-call(bf16[64,512]{1,0:T(8,128)(2,1)S(1)} %get-tuple-element.22.hyper_ref, bf16[512,4,1792]{2,1,0:T(4,128)(2,1)S(1)} %copy-done.2), custom_call_target="tpu_custom_call" | custom-call | tf_op jit(solution)/shard_map/factors/pallas_call | solution.py:217
  12.9 0.1 collective-permute-start.7
  13.0 3.9 %shard_map.110 = (f32[256,1792]{1,0:T(8,128)}, bf16[256,1792]{1,0:T(8,128)(2,1)}) custom-call(bf16[512,1024]{1,0:T(8,128)(2,1)S(1)} %get-tuple-element.23.x_ref, bf16[1024,1792]{1,0:T(8,128)(2,1)S(1)} %copy-done.5), custom_call_target="tpu_custom_call" | custom-call | tf_op jit(solution)/shard_map/pallas_call | solution.py:168
  16.9 0.5 collective-permute-start.8
  17.3 1.2 %add_convert_fusion = bf16[256,1792]{1,0:T(8,128)(2,1)} fusion(f32[256,1792]{1,0:T(8,128)S(1)} %get-tuple-element.17.kept_ref, bf16[256,1792]{1,0:T(8,128)(2,1)S(1)} %collective-permute-done.core_ref), kind=kLoop, calls=%fused_computation | loop fusion | flops 1376256 | bytes 3670016 | tf_op jit(solution)/shard_map/convert_element_type | solution.py:357
  18.5 2.5 %collective-permute-start.1 = (bf16[256,1792]{1,0:T(8,128)(2,1)}, bf16[256,1792]{1,0:T(8,128)(2,1)}, u32[]{:S(2)}, u32[]{:S(2)}) collective-permute-start(bf16[256,1792]{1,0:T(8,128)(2,1)} %add_convert_fusion), channel_id=1, source_target_pairs={{0,16},{8,24},{16,0},{24,8},{1,17},{9,25},{17,1},{25,9},{2,18},{10... | collective-permute-start | bytes 2752520 | tf_op jit(solution)/shard_map/ppermute | solution.py:19
  21.0 0.2 collective-permute-start.2
  21.2 1.0 collective-permute-done.2
  22.2 0.4 collective-permute-start.3
  22.6 19.9 %collective-permute-done.3 = f32[16,256]{1,0:T(8,128)S(1)} collective-permute-done((f32[16,256]{1,0:T(8,128)S(1)}, f32[16,256]{1,0:T(8,128)S(1)}, u32[]{:S(2)}, u32[]{:S(2)}) %collective-permute-start.3) | collective-permute-done | bytes 16416 | tf_op jit(solution)/shard_map/ppermute | solution.py:19
  42.6 1.7 %collective-permute-start.4 = (f32[16,256]{1,0:T(8,128)S(1)}, f32[16,256]{1,0:T(8,128)S(1)}, u32[]{:S(2)}, u32[]{:S(2)}) collective-permute-start(f32[16,256]{1,0:T(8,128)S(1)} %add.78), channel_id=1, source_target_pairs={{0,1},{1,0},{2,3},{3,2},{4,5},{5,4},{6,7},{7,6},{8,9},{9,8},{10,11... | collective-permute-start | bytes 49160 | tf_op jit(solution)/shard_map/ppermute | solution.py:19
  44.3 2.0 %collective-permute-done.4 = f32[16,256]{1,0:T(8,128)S(1)} collective-permute-done((f32[16,256]{1,0:T(8,128)S(1)}, f32[16,256]{1,0:T(8,128)S(1)}, u32[]{:S(2)}, u32[]{:S(2)}) %collective-permute-start.4) | collective-permute-done | bytes 16416 | tf_op jit(solution)/shard_map/ppermute | solution.py:19
  46.3 1.8 %collective-permute-start.5 = (f32[16,256]{1,0:T(8,128)S(1)}, f32[16,256]{1,0:T(8,128)S(1)}, u32[]{:S(2)}, u32[]{:S(2)}) collective-permute-start(f32[16,256]{1,0:T(8,128)S(1)} %add.79), channel_id=1, source_target_pairs={{0,2},{1,3},{2,0},{3,1},{4,6},{5,7},{6,4},{7,5},{8,10},{9,11},{10,... | collective-permute-start | bytes 49160 | tf_op jit(solution)/shard_map/ppermute | solution.py:19
  48.1 1.9 %collective-permute-done.5 = f32[16,256]{1,0:T(8,128)S(1)} collective-permute-done((f32[16,256]{1,0:T(8,128)S(1)}, f32[16,256]{1,0:T(8,128)S(1)}, u32[]{:S(2)}, u32[]{:S(2)}) %collective-permute-start.5) | collective-permute-done | bytes 16416 | tf_op jit(solution)/shard_map/ppermute | solution.py:19
  50.1 2.9 %collective-permute-start.6 = (f32[16,256]{1,0:T(8,128)S(1)}, f32[16,256]{1,0:T(8,128)S(1)}, u32[]{:S(2)}, u32[]{:S(2)}) collective-permute-start(f32[16,256]{1,0:T(8,128)S(1)} %add.80), channel_id=1, source_target_pairs={{0,4},{1,5},{2,6},{3,7},{4,0},{5,1},{6,2},{7,3},{8,12},{9,13},{10,... | collective-permute-start | bytes 49160 | tf_op jit(solution)/shard_map/ppermute | solution.py:19
  53.0 0.1 pad_add_fusion.1.rank_ref
  53.1 1.6 %collective-permute-done.6 = f32[16,256]{1,0:T(8,128)S(1)} collective-permute-done((f32[16,256]{1,0:T(8,128)S(1)}, f32[16,256]{1,0:T(8,128)S(1)}, u32[]{:S(2)}, u32[]{:S(2)}) %collective-permute-start.6) | collective-permute-done | bytes 16416 | tf_op jit(solution)/shard_map/ppermute | solution.py:19
  54.8 1.0 copy-done.8
  55.8 1.2 %copy-done.7 = bf16[256,1792]{1,0:T(8,128)(2,1)S(1)} copy-done((bf16[256,1792]{1,0:T(8,128)(2,1)S(1)}, bf16[256,1792]{1,0:T(8,128)(2,1)}, u32[]{:S(2)}) %copy-start.7) | copy-done | bytes 917528
  56.9 1.2 %copy-done.9 = bf16[256,1792]{1,0:T(8,128)(2,1)S(1)} copy-done((bf16[256,1792]{1,0:T(8,128)(2,1)S(1)}, bf16[256,1792]{1,0:T(8,128)(2,1)}, u32[]{:S(2)}) %copy-start.9) | copy-done | bytes 917528
  58.1 3.8 %adapter.1 = (f32[256,1792]{1,0:T(8,128)S(1)}, bf16[128,1792]{1,0:T(8,128)(2,1)}, bf16[128,1792]{1,0:T(8,128)(2,1)}) custom-call(s32[2]{0:T(128)S(1)} %pad_add_fusion.1.rank_ref, f32[16,256]{1,0:T(8,128)S(1)} %add.81.low_ref, bf16[64,256]{1,0:T(8,128)(2,1)S(1)} %get-tuple-element.21.member_ref, bf16[256,1792]{1,0:T(8,128)(2,1)S(1)} %copy-done.7, ...), custom_call_target="tpu_custom_call" | custom-call | tf_op jit(solution)/shard_map/adapter/pallas_call | solution.py:260
  61.9 1.7 %collective-permute-start.14 = (bf16[128,1792]{1,0:T(8,128)(2,1)}, bf16[128,1792]{1,0:T(8,128)(2,1)}, u32[]{:S(2)}, u32[]{:S(2)}) collective-permute-start(bf16[128,1792]{1,0:T(8,128)(2,1)} %get-tuple-element.28), channel_id=1, source_target_pairs={{0,16},{8,24},{16,0},{24,8},{1,17},{9,25},{17,1},{25,9},{2,18},{10... | collective-permute-start | bytes 1376264 | tf_op jit(solution)/shard_map/ppermute | solution.py:19
  63.7 0.3 collective-permute-start.9
  64.0 2.0 %copy-done = bf16[1792,1024]{1,0:T(8,128)(2,1)S(1)} copy-done((bf16[1792,1024]{1,0:T(8,128)(2,1)S(1)}, bf16[1792,1024]{1,0:T(8,128)(2,1)}, u32[]{:S(2)}) %copy-start) | copy-done | bytes 3670040
  66.0 1.5 %copy-done.4 = f32[256,1792]{1,0:T(8,128)S(1)} copy-done((f32[256,1792]{1,0:T(8,128)S(1)}, f32[256,1792]{1,0:T(8,128)}, u32[]{:S(2)}) %copy-start.4) | copy-done | bytes 1835032
  67.5 1.8 %shard_map.109.act_ref = f32[256,1792]{1,0:T(8,128)S(1)} custom-call(f32[256,1792]{1,0:T(8,128)S(1)} %copy-done.4, bf16[256,1792]{1,0:T(8,128)(2,1)S(1)} %collective-permute-done.core_ref, bf16[256,1792]{1,0:T(8,128)(2,1)} %collective-permute-done.1.rest_ref, bf16[1792,1024]{1,0:T(8,128)(2,1)S(1)} %copy-done), custom_call_target="tpu_custom_call" | custom-call | tf_op jit(solution)/shard_map/pallas_call | solution.py:286
  69.3 6.3 %collective-permute-done.14.up_ref = bf16[128,1792]{1,0:T(8,128)(2,1)} collective-permute-done((bf16[128,1792]{1,0:T(8,128)(2,1)}, bf16[128,1792]{1,0:T(8,128)(2,1)}, u32[]{:S(2)}, u32[]{:S(2)}) %collective-permute-start.14) | collective-permute-done | bytes 458784 | tf_op jit(solution)/shard_map/ppermute | solution.py:19
  75.6 1.1 %shard_map.112 = bf16[128,1792]{1,0:T(8,128)(2,1)S(1)} custom-call(f32[256,1792]{1,0:T(8,128)S(1)} %shard_map.109.act_ref, f32[256,1792]{1,0:T(8,128)S(1)} %get-tuple-element.26.half_ref, bf16[128,1792]{1,0:T(8,128)(2,1)} %collective-permute-done.14.up_ref), custom_call_target="tpu_custom_call" | custom-call | tf_op jit(solution)/shard_map/pallas_call | solution.py:286
  76.9 0.6 fusion.18
  77.5 3.4 %collective-permute-done.9.up_ref = bf16[128,1792]{1,0:T(8,128)(2,1)S(1)} collective-permute-done((bf16[128,1792]{1,0:T(8,128)(2,1)}, bf16[128,1792]{1,0:T(8,128)(2,1)S(1)}, u32[]{:S(2)}, u32[]{:S(2)}) %collective-permute-start.9) | collective-permute-done | bytes 458784 | tf_op jit(solution)/shard_map/ppermute | solution.py:19
  80.9 0.1 shard_map.111
  81.1 0.6 fusion.16
  81.8 0.6 fusion.19
  82.5 1.5 %collective-permute-start.16 = (bf16[2,2,2,16,1024]{4,3,0,1,2:T(8,128)(2,1)S(1)}, bf16[2,2,2,16,1024]{4,3,0,1,2:T(8,128)(2,1)S(1)}, u32[]{:S(2)}, u32[]{:S(2)}) collective-permute-start(bf16[2,2,2,16,1024]{4,3,0,1,2:T(8,128)(2,1)S(1)} %fusion.8), channel_id=1, source_target_pairs={{0,1},{1,0},{2,3},{3,2},{4,5},{5,4},{6,7},{7,6},{8,9},{9,8},{10,11... | collective-permute-start | bytes 786440 | tf_op jit(solution)/shard_map/ppermute | solution.py:19
  84.0 0.6 fusion.17
  84.7 0.7 collective-permute-start.11
  85.3 6.4 %collective-permute-done.16 = bf16[2,2,2,16,1024]{4,3,0,1,2:T(8,128)(2,1)S(1)} collective-permute-done((bf16[2,2,2,16,1024]{4,3,0,1,2:T(8,128)(2,1)S(1)}, bf16[2,2,2,16,1024]{4,3,0,1,2:T(8,128)(2,1)S(1)}, u32[]{:S(2)}, u32[]{:S(2)}) %collective-permute-start.16) | collective-permute-done | bytes 262176 | tf_op jit(solution)/shard_map/ppermute | solution.py:19
  91.8 1.7 %collective-permute-start.17 = (bf16[2,2,16,1024]{3,2,0,1:T(8,128)(2,1)S(1)}, bf16[2,2,16,1024]{3,2,0,1:T(8,128)(2,1)S(1)}, u32[]{:S(2)}, u32[]{:S(2)}) collective-permute-start(bf16[2,2,16,1024]{3,2,0,1:T(8,128)(2,1)S(1)} %fusion.11), channel_id=1, source_target_pairs={{0,2},{1,3},{2,0},{3,1},{4,6},{5,7},{6,4},{7,5},{8,10},{9,11},{10,... | collective-permute-start | bytes 393224 | tf_op jit(solution)/shard_map/ppermute | solution.py:19
  93.5 3.3 %collective-permute-done.11 = bf16[2,2,2,16,1024]{4,3,2,1,0:T(8,128)(2,1)S(1)} collective-permute-done((bf16[2,2,2,16,1024]{4,3,2,1,0:T(8,128)(2,1)S(1)}, bf16[2,2,2,16,1024]{4,3,2,1,0:T(8,128)(2,1)S(1)}, u32[]{:S(2)}, u32[]{:S(2)}) %collective-permute-start.11) | collective-permute-done | bytes 262176 | tf_op jit(solution)/shard_map/ppermute | solution.py:19
  97.0 1.7 %collective-permute-start.12 = (bf16[2,2,16,1024]{3,2,1,0:T(8,128)(2,1)S(1)}, bf16[2,2,16,1024]{3,2,1,0:T(8,128)(2,1)S(1)}, u32[]{:S(2)}, u32[]{:S(2)}) collective-permute-start(bf16[2,2,16,1024]{3,2,1,0:T(8,128)(2,1)S(1)} %fusion.10), channel_id=1, source_target_pairs={{0,2},{1,3},{2,0},{3,1},{4,6},{5,7},{6,4},{7,5},{8,10},{9,11},{10,... | collective-permute-start | bytes 393224 | tf_op jit(solution)/shard_map/ppermute | solution.py:19
  98.7 2.6 %collective-permute-start.18 = (bf16[2,16,1024]{2,1,0:T(8,128)(2,1)S(1)}, bf16[2,16,1024]{2,1,0:T(8,128)(2,1)S(1)}, u32[]{:S(2)}, u32[]{:S(2)}) collective-permute-start(bf16[2,16,1024]{2,1,0:T(8,128)(2,1)S(1)} %fusion.15), channel_id=1, source_target_pairs={{0,4},{1,5},{2,6},{3,7},{4,0},{5,1},{6,2},{7,3},{8,12},{9,13},{10,... | collective-permute-start | bytes 196616 | tf_op jit(solution)/shard_map/ppermute | solution.py:19
  101.3 1.4 %collective-permute-done.12 = bf16[2,2,16,1024]{3,2,1,0:T(8,128)(2,1)S(1)} collective-permute-done((bf16[2,2,16,1024]{3,2,1,0:T(8,128)(2,1)S(1)}, bf16[2,2,16,1024]{3,2,1,0:T(8,128)(2,1)S(1)}, u32[]{:S(2)}, u32[]{:S(2)}) %collective-permute-start.12) | collective-permute-done | bytes 131104 | tf_op jit(solution)/shard_map/ppermute | solution.py:19
  102.8 2.6 %collective-permute-start.13 = (bf16[2,16,1024]{2,1,0:T(8,128)(2,1)S(1)}, bf16[2,16,1024]{2,1,0:T(8,128)(2,1)S(1)}, u32[]{:S(2)}, u32[]{:S(2)}) collective-permute-start(bf16[2,16,1024]{2,1,0:T(8,128)(2,1)S(1)} %fusion.14), channel_id=1, source_target_pairs={{0,4},{1,5},{2,6},{3,7},{4,0},{5,1},{6,2},{7,3},{8,12},{9,13},{10,... | collective-permute-start | bytes 196616 | tf_op jit(solution)/shard_map/ppermute | solution.py:19
  105.5 2.6 %collective-permute-done.13 = bf16[2,16,1024]{2,1,0:T(8,128)(2,1)S(1)} collective-permute-done((bf16[2,16,1024]{2,1,0:T(8,128)(2,1)S(1)}, bf16[2,16,1024]{2,1,0:T(8,128)(2,1)S(1)}, u32[]{:S(2)}, u32[]{:S(2)}) %collective-permute-start.13) | collective-permute-done | bytes 65568 | tf_op jit(solution)/shard_map/ppermute | solution.py:19
  108.1 0.7 reshape.23
  (45 shorter events, 0.6 us)
Async XLA Ops:
  0.1 9.2 %copy-start.2 = (bf16[512,4,1792]{2,1,0:T(4,128)(2,1)S(1)}, bf16[512,4,1792]{2,1,0:T(4,128)(2,1)}, u32[]{:S(2)}) copy-start(bf16[512,4,1792]{2,1,0:T(4,128)(2,1)} %gen_ref.1) | copy-start | bytes 22020100
  8.7 8.6 %copy-start.3 = (f32[256,1792]{1,0:T(8,128)}, f32[256,1792]{1,0:T(8,128)S(1)}, u32[]{:S(2)}) copy-start(f32[256,1792]{1,0:T(8,128)S(1)} %get-tuple-element.17.kept_ref) | copy-start | bytes 5505028
  8.7 8.6 %collective-permute-start = (bf16[256,1792]{1,0:T(8,128)(2,1)S(1)}, bf16[256,1792]{1,0:T(8,128)(2,1)S(1)}, u32[]{:S(2)}, u32[]{:S(2)}) collective-permute-start(bf16[256,1792]{1,0:T(8,128)(2,1)S(1)} %get-tuple-element.18), channel_id=1, source_target_pairs={{0,8},{8,0},{16,24},{24,16},{1,9},{9,1},{17,25},{25,17},{2,10},{10... | collective-permute-start | bytes 2752520 | tf_op jit(solution)/shard_map/ppermute | solution.py:19
  9.3 3.7 %copy-start.5 = (bf16[1024,1792]{1,0:T(8,128)(2,1)S(1)}, bf16[1024,1792]{1,0:T(8,128)(2,1)}, u32[]{:S(2)}) copy-start(bf16[1024,1792]{1,0:T(8,128)(2,1)} %w_ref.1) | copy-start | bytes 11010052
  12.9 5.7 %copy-start.6 = (bf16[256,1792]{1,0:T(8,128)(2,1)}, bf16[256,1792]{1,0:T(8,128)(2,1)S(1)}, u32[]{:S(2)}) copy-start(bf16[256,1792]{1,0:T(8,128)(2,1)S(1)} %factors.1.mine_ref) | copy-start | bytes 2752516
  12.9 41.9 %collective-permute-start.7 = (bf16[256,1792]{1,0:T(8,128)(2,1)S(1)}, bf16[256,1792]{1,0:T(8,128)(2,1)S(1)}, u32[]{:S(2)}, u32[]{:S(2)}) collective-permute-start(bf16[256,1792]{1,0:T(8,128)(2,1)S(1)} %factors.1.mine_ref), channel_id=1, source_target_pairs={{0,8},{8,0},{16,24},{24,16},{1,9},{9,1},{17,25},{25,17},{2,10},{10... | collective-permute-start | bytes 2752520 | tf_op jit(solution)/shard_map/ppermute | solution.py:19
  16.9 38.9 %collective-permute-start.8 = (bf16[256,1792]{1,0:T(8,128)(2,1)}, bf16[256,1792]{1,0:T(8,128)(2,1)}, u32[]{:S(2)}, u32[]{:S(2)}) collective-permute-start(bf16[256,1792]{1,0:T(8,128)(2,1)} %get-tuple-element.25), channel_id=1, source_target_pairs={{0,8},{8,0},{16,24},{24,16},{1,9},{9,1},{17,25},{25,17},{2,10},{10... | collective-permute-start | bytes 2752520 | tf_op jit(solution)/shard_map/ppermute | solution.py:19
  18.5 45.4 %collective-permute-start.1 = (bf16[256,1792]{1,0:T(8,128)(2,1)}, bf16[256,1792]{1,0:T(8,128)(2,1)}, u32[]{:S(2)}, u32[]{:S(2)}) collective-permute-start(bf16[256,1792]{1,0:T(8,128)(2,1)} %add_convert_fusion), channel_id=1, source_target_pairs={{0,16},{8,24},{16,0},{24,8},{1,17},{9,25},{17,1},{25,9},{2,18},{10... | collective-permute-start | bytes 2752520 | tf_op jit(solution)/shard_map/ppermute | solution.py:19
  21.0 1.2 %collective-permute-start.2 = (f32[16,256]{1,0:T(8,128)S(1)}, f32[16,256]{1,0:T(8,128)S(1)}, u32[]{:S(2)}, u32[]{:S(2)}) collective-permute-start(f32[16,256]{1,0:T(8,128)S(1)} %get-tuple-element.20), channel_id=1, source_target_pairs={{0,8},{8,0},{16,24},{24,16},{1,9},{9,1},{17,25},{25,17},{2,10},{10... | collective-permute-start | bytes 49160 | tf_op jit(solution)/shard_map/ppermute | solution.py:19
  22.2 20.4 %collective-permute-start.3 = (f32[16,256]{1,0:T(8,128)S(1)}, f32[16,256]{1,0:T(8,128)S(1)}, u32[]{:S(2)}, u32[]{:S(2)}) collective-permute-start(f32[16,256]{1,0:T(8,128)S(1)} %add.77), channel_id=1, source_target_pairs={{0,16},{8,24},{16,0},{24,8},{1,17},{9,25},{17,1},{25,9},{2,18},{10... | collective-permute-start | bytes 49160 | tf_op jit(solution)/shard_map/ppermute | solution.py:19
  42.6 3.7 %collective-permute-start.4 = (f32[16,256]{1,0:T(8,128)S(1)}, f32[16,256]{1,0:T(8,128)S(1)}, u32[]{:S(2)}, u32[]{:S(2)}) collective-permute-start(f32[16,256]{1,0:T(8,128)S(1)} %add.78), channel_id=1, source_target_pairs={{0,1},{1,0},{2,3},{3,2},{4,5},{5,4},{6,7},{7,6},{8,9},{9,8},{10,11... | collective-permute-start | bytes 49160 | tf_op jit(solution)/shard_map/ppermute | solution.py:19
  46.3 3.7 %collective-permute-start.5 = (f32[16,256]{1,0:T(8,128)S(1)}, f32[16,256]{1,0:T(8,128)S(1)}, u32[]{:S(2)}, u32[]{:S(2)}) collective-permute-start(f32[16,256]{1,0:T(8,128)S(1)} %add.79), channel_id=1, source_target_pairs={{0,2},{1,3},{2,0},{3,1},{4,6},{5,7},{6,4},{7,5},{8,10},{9,11},{10,... | collective-permute-start | bytes 49160 | tf_op jit(solution)/shard_map/ppermute | solution.py:19
  50.1 4.7 %collective-permute-start.6 = (f32[16,256]{1,0:T(8,128)S(1)}, f32[16,256]{1,0:T(8,128)S(1)}, u32[]{:S(2)}, u32[]{:S(2)}) collective-permute-start(f32[16,256]{1,0:T(8,128)S(1)} %add.80), channel_id=1, source_target_pairs={{0,4},{1,5},{2,6},{3,7},{4,0},{5,1},{6,2},{7,3},{8,12},{9,13},{10,... | collective-permute-start | bytes 49160 | tf_op jit(solution)/shard_map/ppermute | solution.py:19
  54.7 1.0 copy-start.8
  55.8 1.2 %copy-start.7 = (bf16[256,1792]{1,0:T(8,128)(2,1)S(1)}, bf16[256,1792]{1,0:T(8,128)(2,1)}, u32[]{:S(2)}) copy-start(bf16[256,1792]{1,0:T(8,128)(2,1)} %copy-done.6) | copy-start | bytes 2752516
  56.9 1.2 %copy-start.9 = (bf16[256,1792]{1,0:T(8,128)(2,1)S(1)}, bf16[256,1792]{1,0:T(8,128)(2,1)}, u32[]{:S(2)}) copy-start(bf16[256,1792]{1,0:T(8,128)(2,1)} %copy-done.8) | copy-start | bytes 2752516
  61.9 13.7 %collective-permute-start.14 = (bf16[128,1792]{1,0:T(8,128)(2,1)}, bf16[128,1792]{1,0:T(8,128)(2,1)}, u32[]{:S(2)}, u32[]{:S(2)}) collective-permute-start(bf16[128,1792]{1,0:T(8,128)(2,1)} %get-tuple-element.28), channel_id=1, source_target_pairs={{0,16},{8,24},{16,0},{24,8},{1,17},{9,25},{17,1},{25,9},{2,18},{10... | collective-permute-start | bytes 1376264 | tf_op jit(solution)/shard_map/ppermute | solution.py:19
  63.7 17.3 %collective-permute-start.9 = (bf16[128,1792]{1,0:T(8,128)(2,1)}, bf16[128,1792]{1,0:T(8,128)(2,1)S(1)}, u32[]{:S(2)}, u32[]{:S(2)}) collective-permute-start(bf16[128,1792]{1,0:T(8,128)(2,1)} %get-tuple-element.27), channel_id=1, source_target_pairs={{0,16},{8,24},{16,0},{24,8},{1,17},{9,25},{17,1},{25,9},{2,18},{10... | collective-permute-start | bytes 1376264 | tf_op jit(solution)/shard_map/ppermute | solution.py:19
  64.0 2.0 %copy-start = (bf16[1792,1024]{1,0:T(8,128)(2,1)S(1)}, bf16[1792,1024]{1,0:T(8,128)(2,1)}, u32[]{:S(2)}) copy-start(bf16[1792,1024]{1,0:T(8,128)(2,1)} %later_ref.1) | copy-start | bytes 11010052
  66.0 1.5 %copy-start.4 = (f32[256,1792]{1,0:T(8,128)S(1)}, f32[256,1792]{1,0:T(8,128)}, u32[]{:S(2)}) copy-start(f32[256,1792]{1,0:T(8,128)} %copy-done.3) | copy-start | bytes 5505028
  69.3 7.6 %copy-start.1 = (bf16[1792,1024]{1,0:T(8,128)(2,1)S(1)}, bf16[1792,1024]{1,0:T(8,128)(2,1)}, u32[]{:S(2)}) copy-start(bf16[1792,1024]{1,0:T(8,128)(2,1)} %later_ref.1) | copy-start | bytes 11010052
  76.8 5.0 %collective-permute-start.15 = (bf16[128,1792]{1,0:T(8,128)(2,1)S(1)}, bf16[128,1792]{1,0:T(8,128)(2,1)S(1)}, u32[]{:S(2)}, u32[]{:S(2)}) collective-permute-start(bf16[128,1792]{1,0:T(8,128)(2,1)S(1)} %shard_map.112), channel_id=1, source_target_pairs={{0,8},{8,0},{16,24},{24,16},{1,9},{9,1},{17,25},{25,17},{2,10},{10... | collective-permute-start | bytes 1376264 | tf_op jit(solution)/shard_map/ppermute | solution.py:19
  81.0 2.9 %collective-permute-start.10 = (bf16[128,1792]{1,0:T(8,128)(2,1)S(1)}, bf16[128,1792]{1,0:T(8,128)(2,1)S(1)}, u32[]{:S(2)}, u32[]{:S(2)}) collective-permute-start(bf16[128,1792]{1,0:T(8,128)(2,1)S(1)} %shard_map.111), channel_id=1, source_target_pairs={{0,8},{8,0},{16,24},{24,16},{1,9},{9,1},{17,25},{25,17},{2,10},{10... | collective-permute-start | bytes 1376264 | tf_op jit(solution)/shard_map/ppermute | solution.py:19
  82.5 9.2 %collective-permute-start.16 = (bf16[2,2,2,16,1024]{4,3,0,1,2:T(8,128)(2,1)S(1)}, bf16[2,2,2,16,1024]{4,3,0,1,2:T(8,128)(2,1)S(1)}, u32[]{:S(2)}, u32[]{:S(2)}) collective-permute-start(bf16[2,2,2,16,1024]{4,3,0,1,2:T(8,128)(2,1)S(1)} %fusion.8), channel_id=1, source_target_pairs={{0,1},{1,0},{2,3},{3,2},{4,5},{5,4},{6,7},{7,6},{8,9},{9,8},{10,11... | collective-permute-start | bytes 786440 | tf_op jit(solution)/shard_map/ppermute | solution.py:19
  84.7 12.2 %collective-permute-start.11 = (bf16[2,2,2,16,1024]{4,3,2,1,0:T(8,128)(2,1)S(1)}, bf16[2,2,2,16,1024]{4,3,2,1,0:T(8,128)(2,1)S(1)}, u32[]{:S(2)}, u32[]{:S(2)}) collective-permute-start(bf16[2,2,2,16,1024]{4,3,2,1,0:T(8,128)(2,1)S(1)} %fusion.9), channel_id=1, source_target_pairs={{0,1},{1,0},{2,3},{3,2},{4,5},{5,4},{6,7},{7,6},{8,9},{9,8},{10,11... | collective-permute-start | bytes 786440 | tf_op jit(solution)/shard_map/ppermute | solution.py:19
  91.8 6.8 %collective-permute-start.17 = (bf16[2,2,16,1024]{3,2,0,1:T(8,128)(2,1)S(1)}, bf16[2,2,16,1024]{3,2,0,1:T(8,128)(2,1)S(1)}, u32[]{:S(2)}, u32[]{:S(2)}) collective-permute-start(bf16[2,2,16,1024]{3,2,0,1:T(8,128)(2,1)S(1)} %fusion.11), channel_id=1, source_target_pairs={{0,2},{1,3},{2,0},{3,1},{4,6},{5,7},{6,4},{7,5},{8,10},{9,11},{10,... | collective-permute-start | bytes 393224 | tf_op jit(solution)/shard_map/ppermute | solution.py:19
  97.0 5.8 %collective-permute-start.12 = (bf16[2,2,16,1024]{3,2,1,0:T(8,128)(2,1)S(1)}, bf16[2,2,16,1024]{3,2,1,0:T(8,128)(2,1)S(1)}, u32[]{:S(2)}, u32[]{:S(2)}) collective-permute-start(bf16[2,2,16,1024]{3,2,1,0:T(8,128)(2,1)S(1)} %fusion.10), channel_id=1, source_target_pairs={{0,2},{1,3},{2,0},{3,1},{4,6},{5,7},{6,4},{7,5},{8,10},{9,11},{10,... | collective-permute-start | bytes 393224 | tf_op jit(solution)/shard_map/ppermute | solution.py:19
  98.7 6.7 %collective-permute-start.18 = (bf16[2,16,1024]{2,1,0:T(8,128)(2,1)S(1)}, bf16[2,16,1024]{2,1,0:T(8,128)(2,1)S(1)}, u32[]{:S(2)}, u32[]{:S(2)}) collective-permute-start(bf16[2,16,1024]{2,1,0:T(8,128)(2,1)S(1)} %fusion.15), channel_id=1, source_target_pairs={{0,4},{1,5},{2,6},{3,7},{4,0},{5,1},{6,2},{7,3},{8,12},{9,13},{10,... | collective-permute-start | bytes 196616 | tf_op jit(solution)/shard_map/ppermute | solution.py:19
  102.8 5.2 %collective-permute-start.13 = (bf16[2,16,1024]{2,1,0:T(8,128)(2,1)S(1)}, bf16[2,16,1024]{2,1,0:T(8,128)(2,1)S(1)}, u32[]{:S(2)}, u32[]{:S(2)}) collective-permute-start(bf16[2,16,1024]{2,1,0:T(8,128)(2,1)S(1)} %fusion.14), channel_id=1, source_target_pairs={{0,4},{1,5},{2,6},{3,7},{4,0},{5,1},{6,2},{7,3},{8,12},{9,13},{10,... | collective-permute-start | bytes 196616 | tf_op jit(solution)/shard_map/ppermute | solution.py:19

commit v3 on v2

--- a/solution.py
+++ b/solution.py
@@ -11,7 +11,12 @@
 
 F32 = jnp.float32
 BF16 = jnp.bfloat16
-CHUNKS = (1, 1)
+
+
+def plan(per_dest):
+    if per_dest % 64 == 0:
+        return (2, 1, 1), ((0, 1), (2,))
+    return (1, 1), ((0,), (1,))
 
 
 def swap(x, axis, mask):
@@ -21,10 +26,6 @@
 
 def masks_of(n):
     return [1 << b for b in range(n.bit_length() - 1)]
-
-
-def pick(x, i, axis=0):
-    return lax.dynamic_index_in_dim(x, i, axis, keepdims=False)
 
 
 def stay(x):
@@ -48,7 +49,7 @@
 
 
 def low_kernel(
-    blocks, slab, shift, lead_ref, count_hbm, task_hbm, request_hbm, tok_hbm, emb_hbm, gen_in_hbm, a_hbm,
+    blocks, slab, shift, count_hbm, task_hbm, request_hbm, tok_hbm, emb_hbm, gen_in_hbm, a_hbm,
     w_hbm, *rest
 ):
     x_in, rest = (None, rest) if slab % 128 == 0 else (rest[0], rest[1:])
@@ -76,7 +77,7 @@
     hidden = gen_in_ref.shape[1]
     rank, half = low_ref.shape
     rows = 2 * half
-    core = lead_ref[1]
+    core = lax.axis_index("row") & 1
     across_rows = (((0,), (0,)), ((), ()))
     for copy in copies[:3]:
         copy.wait()
@@ -104,7 +105,7 @@
             toks_ref[side * half + target : side * half + target + size, :] = rows_of(
                 tok_ref, begin, size
             )
-    x = toks_ref[:, pl.ds(pl.multiple_of(lead_ref[0], 128), slab)] if x_in is None else x_in[...]
+    x = toks_ref[:, pl.ds(pl.multiple_of(lax.axis_index("col") * slab, 128), slab)] if x_in is None else x_in[...]
     xt = x.T
     copies[6].wait()
     part = hidden // 4
@@ -128,7 +129,7 @@
         split_store(toks_ref[...], w_ref, kept_ref, sent_ref, slice(j, j + tile))
 
 
-def low_part(blocks, shift, lead, count, task, request, tokens, emb, gen_in, a, w, x):
+def low_part(blocks, shift, count, task, request, tokens, emb, gen_in, a, w, x):
     hidden, slab, rank = a.shape
     groups, rows = count.shape[1], request.shape[1]
     width, ff = w.shape
@@ -139,7 +140,7 @@
     extra = () if x is None else (x,)
     return pl.pallas_call(
         functools.partial(low_kernel, blocks, slab, shift),
-        in_specs=[pl.BlockSpec(memory_space=pltpu.SMEM)] + [hbm] * len(moved) + [vmem] * len(extra),
+        in_specs=[hbm] * len(moved) + [vmem] * len(extra),
         out_specs=[vmem] * 7,
         out_shape=(
             jax.ShapeDtypeStruct((rank, rows // 2), F32),
@@ -154,7 +155,7 @@
         + [pltpu.VMEM((hidden, rows), F32), pltpu.SemaphoreType.DMA((len(moved),))],
         compiler_params=pltpu.CompilerParams(vmem_limit_bytes=36 << 20),
         name="low_part",
-    )(lead, *[stay(m) for m in moved], *extra)
+    )(*[stay(m) for m in moved], *extra)
 
 
 def split_kernel(x_ref, w_ref, kept_ref, sent_ref):
@@ -177,7 +178,7 @@
             pl.BlockSpec((rows // 2, tile), lambda i: (0, i)),
         ],
         out_shape=(
-            pltpu.HBM((rows // 2, ff), F32),
+            pltpu.VMEM((rows // 2, ff), F32),
             jax.ShapeDtypeStruct((rows // 2, ff), BF16),
         ),
         compiler_params=pltpu.CompilerParams(vmem_limit_bytes=16 << 20),
@@ -229,13 +230,13 @@
     )(hyper, gen_b)
 
 
-def delta_kernel(pieces, rank_ref, low_ref, member_ref, mine_ref, peer_ref, kept_ref, got_ref, sum_ref, *sent):
+def delta_kernel(pieces, low_ref, member_ref, mine_ref, peer_ref, kept_ref, got_ref, sum_ref, *sent):
     groups = member_ref.shape[0]
     ranks = mine_ref.shape[0] // groups
     member = member_ref[...].astype(F32)
     total = kept_ref[...] + got_ref[...].astype(F32)
     for which, factor in ((0, mine_ref), (1, peer_ref)):
-        first = rank_ref[which]
+        first = (lax.axis_index("row") ^ which) * ranks
         spread = jnp.concatenate(
             [
                 (member * low_ref[pl.ds(first + r, 1), :].astype(BF16).astype(F32)).astype(BF16)
@@ -252,24 +253,21 @@
         ref[...] = total[start : start + size]
 
 
-def add_adapter(pieces, first_ranks, low, member, mine, peer, kept, got):
+def add_adapter(pieces, low, member, mine, peer, kept, got):
     rows, ff = kept.shape
     tile = halves_of(ff)
-    whole = lambda x: pl.BlockSpec(x.shape, lambda i, c: (0, 0))
-    cut = lambda n: pl.BlockSpec((n, tile), lambda i, c: (0, i))
+    whole = lambda x: pl.BlockSpec(x.shape, lambda i: (0, 0))
+    cut = lambda n: pl.BlockSpec((n, tile), lambda i: (0, i))
     return pl.pallas_call(
         functools.partial(delta_kernel, pieces),
-        grid_spec=pltpu.PrefetchScalarGridSpec(
-            num_scalar_prefetch=1,
-            grid=(ff // tile,),
-            in_specs=[whole(low), whole(member)] + [cut(x.shape[0]) for x in (mine, peer, kept, got)],
-            out_specs=[cut(rows)] + [cut(size) for _, size in pieces],
-        ),
+        grid=(ff // tile,),
+        in_specs=[whole(low), whole(member)] + [cut(x.shape[0]) for x in (mine, peer, kept, got)],
+        out_specs=[cut(rows)] + [cut(size) for _, size in pieces],
         out_shape=[pltpu.VMEM((rows, ff), F32)]
         + [jax.ShapeDtypeStruct((size, ff), BF16) for _, size in pieces],
         compiler_params=pltpu.CompilerParams(vmem_limit_bytes=16 << 20),
         name="adapter",
-    )(first_ranks, low, member, mine, peer, stay(kept), got)
+    )(low, member, mine, peer, kept, got)
 
 
 def gate_kernel(kept_ref, core_ref, rest_ref, later_ref, out_ref):
@@ -286,10 +284,97 @@
     return pl.pallas_call(
         kernel,
         in_specs=[vmem] * len(args),
-        out_specs=vmem,
+        out_specs=jax.tree.map(lambda _: vmem, out),
         out_shape=out,
         compiler_params=pltpu.CompilerParams(vmem_limit_bytes=8 << 20),
     )(*args)
+
+
+def split_rows(hid_ref, w_ref):
+    acc = jnp.dot(hid_ref[...], w_ref[...], preferred_element_type=F32)
+    col = lax.axis_size("col")
+    acc = acc.reshape(col // 2, 2, acc.shape[0] // col, acc.shape[1])
+    low_bit = (lax.axis_index("col") & 1) == 0
+    keep = jnp.where(low_bit, acc[:, 0], acc[:, 1])
+    give = jnp.where(low_bit, acc[:, 1], acc[:, 0])
+    return keep, give.astype(BF16)
+
+
+def down_kernel(hid_ref, w_ref, keep_ref, give_ref):
+    keep_ref[...], give_ref[...] = split_rows(hid_ref, w_ref)
+
+
+def cross_kernel(hid_ref, w_ref, own_keep_ref, own_give_ref, keep_ref, give_ref):
+    keep_ref[0], give_ref[0] = own_keep_ref[...], own_give_ref[...]
+    keep_ref[1], give_ref[1] = split_rows(hid_ref, w_ref)
+
+
+def down(hid, w):
+    col = lax.axis_size("col")
+    shape = (col // 2, hid.shape[0] // col, w.shape[1])
+    out = (jax.ShapeDtypeStruct(shape, F32), jax.ShapeDtypeStruct(shape, BF16))
+    return in_vmem(down_kernel, out, hid, w)
+
+
+def cross(other, w, own):
+    out = tuple(jax.ShapeDtypeStruct((2,) + x.shape, x.dtype) for x in own)
+    return in_vmem(cross_kernel, out, other, w, *own)
+
+
+def fold_kernel(bit, keep_ref, got_ref, new_ref, give_ref):
+    parts = keep_ref.shape[1]
+    side = (lax.axis_index("col") >> bit) & 1
+    for j in range(parts // 2):
+        for ref, which in ((new_ref, side), (give_ref, 1 - side)):
+            at = pl.ds(2 * j + which, 1)
+            ref[:, j : j + 1] = (keep_ref[:, at] + got_ref[:, at].astype(F32)).astype(ref.dtype)
+
+
+def fold(bit, keep, got):
+    shape = keep.shape[:1] + (keep.shape[1] // 2,) + keep.shape[2:]
+    out = (jax.ShapeDtypeStruct(shape, F32), jax.ShapeDtypeStruct(shape, BF16))
+    return in_vmem(functools.partial(fold_kernel, bit), out, keep, got)
+
+
+def last_kernel(bit, count, *refs):
+    here = lax.axis_index("col") >> bit
+    start = 0
+    for k in range(count):
+        keep_ref, got_ref = refs[2 * k : 2 * k + 2]
+        rows = slice(start, start + keep_ref.shape[2])
+        for q, ref in enumerate(refs[2 * count :]):
+            at = pl.ds(here ^ q, 1)
+            ref[:, :, rows] = (keep_ref[:, at] + got_ref[:, at].astype(F32)).astype(ref.dtype)
+        start = rows.stop
+
+
+def last_split(bit, parts):
+    keep = parts[0][0]
+    shape = keep.shape[:1] + (1, sum(k.shape[2] for k, _ in parts)) + keep.shape[3:]
+    out = [jax.ShapeDtypeStruct(shape, F32)] + [jax.ShapeDtypeStruct(shape, BF16)] * 3
+    kernel = functools.partial(last_kernel, bit, len(parts))
+    return in_vmem(kernel, out, *[x for part in parts for x in part])
+
+
+def join_kernel(count, *refs):
+    out_ref = refs[-1]
+    requests, draft, width = out_ref.shape
+    core = lax.axis_index("row") & 1
+    start = 0
+    for k in range(count):
+        total, *got = refs[4 * k : 4 * k + 4]
+        for side in range(2):
+            value = total[side, 0]
+            for g in got:
+                value += g[side, 0].astype(F32)
+            size = value.shape[0] // draft
+            at = start + (requests // 2) * (core if side == 0 else 1 - core)
+            out_ref[pl.ds(at, size)] = value.astype(BF16).reshape(size, draft, width)
+        start += size
+
+
+def join(parts, out):
+    return in_vmem(functools.partial(join_kernel, len(parts)), out, *[x for p in parts for x in p])
 
 
 def hidden_kernel(start, act_ref, half_ref, up_ref, out_ref):
@@ -311,10 +396,10 @@
     core = ri & 1
     rmasks, cmasks = masks_of(rn), masks_of(cn)
     slab = gen_a.shape[1]
-    rank_part, _ = gen_b.shape[1:]
 
     per_dest = rows // cn
-    sizes = [per_dest * part // sum(CHUNKS) for part in CHUNKS]
+    chunks, joint = plan(per_dest)
+    sizes = [per_dest * part // sum(chunks) for part in chunks]
     blocks, pieces, target, source = [], [], 0, 0
     for size in sizes:
         pieces.append((target, cn * size // 2))
@@ -339,7 +424,6 @@
     low, low_sent, hyper, own_member, toks, gate_kept, gate_sent = low_part(
         tuple(blocks),
         shift,
-        jnp.stack([ci * slab, core]),
         group_count[None, :],
         group_task[None, :],
         jnp.asarray(request),
@@ -375,9 +459,8 @@
     for m in cmasks:
         low = low + swap(low, "col", m)
 
-    first_ranks = jnp.stack([ri * rank_part, (ri ^ 1) * rank_part])
     up_half, *up_sums = add_adapter(
-        tuple(pieces), first_ranks, low, own_member, b_mine, b_peer, up_kept, up_got
+        tuple(pieces), low, own_member, b_mine, b_peer, up_kept, up_got
     )
 
     act = activate(gate_kept, gate_got, gate_rest, w_down)
@@ -386,19 +469,19 @@
         up_rest = others(up_sums[k])
         hid = hidden_units(piece, act, up_half, up_rest)
         other = swap(hid, "row", 1)
-        acc = jnp.dot(hid, w_down, preferred_element_type=F32)
-        acc = jnp.stack([acc, jnp.dot(other, w_down, preferred_element_type=F32)])
-        out_width = acc.shape[-1]
-        acc = acc.reshape((2,) + (2,) * len(cmasks) + (sizes[k] // 2, out_width))
-        for s, m in enumerate(cmasks):
-            dim = acc.ndim - 3
-            bit = (ci >> s) & 1
-            sent = pick(acc, 1 - bit, dim).astype(BF16)
-            acc = pick(acc, bit, dim) + swap(sent, "col", m).astype(F32)
-        acc = acc.astype(BF16)
-        outs.append(jnp.stack([pick(acc, core), pick(acc, 1 - core)]))
-    out = jnp.concatenate(outs, axis=1)
-    return out.reshape(batch // cn, draft, out.shape[-1])
+        keep, give = cross(other, w_down, down(hid, w_down))
+        for s, m in enumerate(cmasks[:-2]):
+            got = swap(give, "col", m)
+            if s + 3 < len(cmasks):
+                keep, give = fold(s + 1, keep, got)
+        outs.append((keep, got))
+    low_bit = len(cmasks) - 2
+    parts = []
+    for members in joint:
+        total, *gives = last_split(low_bit, [outs[k] for k in members])
+        gots = [swap(give, "col", (q + 1) << low_bit) for q, give in enumerate(gives)]
+        parts.append([total] + gots)
+    return join(parts, jax.ShapeDtypeStruct((batch // cn, draft, w_down.shape[1]), BF16))
 
 
 def solution(mesh):

time: 109 us -> 105 us (0.963)
  starting transfers between devices: 23.7 us -> 31.9 us
  local copies, waits for them, and re-layouts: 7.74 us -> 0.01 us
  matrix products: 2.58 us -> 0 us
  other arithmetic: 1.64 us -> 0.18 us
    ppermute x19 -> x24, starting transfers between devices: 23.7 us -> 31.9 us  [swap(): return lax.ppermute(x, axis, [(i, i ^ mask) for i in range(n)])]
    unnamed x20 -> x6, local copies, waits for them, and re-layouts: 6.92 us -> 0.01 us
    dot_general x4 -> x0, matrix products: 2.58 us -> none  [the longest x2 1.29 us: shards(): acc = jnp.dot(hid, w_down, preferred_element_type=F32)]
    ppermute x19 -> x24, waiting for transfers between devices: 50 us -> 50.8 us  [swap(): return lax.ppermute(x, axis, [(i, i ^ mask) for i in range(n)])]
    pallas_call x4 -> x14, Pallas kernels: 6.83 us -> 7.59 us  [the longest x13 6.01 us: in_vmem(): pl.pallas_call(kernel, in_specs=[vmem] * len(args), out_specs=jax.tree.ma...]
  transfers between devices with their start and end apart: 19 -> 24, of which waited for: 11 -> 12; matrix products, arithmetic and copies ran while one was open for 4% -> 0% of each run, Pallas kernels for 13% -> 13%
where the time goes in v3:
time: 105 us
  waiting for transfers between devices  50.8 us (48%)
  starting transfers between devices  31.9 us (30%)
  Pallas kernels  22.1 us (21%)
    ppermute x24, waiting for transfers between devices, swap(): return lax.ppermute(x, axis, [(i, i ^ mask) for i in range(n)])  50.8 us
    ppermute x24, starting transfers between devices, swap(): return lax.ppermute(x, axis, [(i, i ^ mask) for i in range(n)])  31.9 us
    pallas_call x1, Pallas kernels, low_part(): pl.pallas_call(functools.partial(low_kernel, blocks, slab, shift), in_spe...  8 us
    pallas_call x13, Pallas kernels, in_vmem(): pl.pallas_call(kernel, in_specs=[vmem] * len(args), out_specs=jax.tree.ma...  6.01 us
    pallas_call x1, Pallas kernels, factors(): pl.pallas_call(factor_kernel, grid=(ff // tile,), in_specs=[pl.BlockSpec(...  3.54 us
    pallas_call x1, Pallas kernels, split_matmul(): pl.pallas_call(split_kernel, grid=(ff // tile,), in_specs=[pl.BlockSpec((...  3 us
  transfers between devices with their start and end apart: 24, of which 12 were waited for; matrix products, arithmetic and copies ran while one was open for 0% of the time, Pallas kernels for 13%

profile of v3, /device:TPU:0, one launch (start us, length us, event | category | flops | bytes accessed | tf_op | source)
XLA Modules:
  0.0 105.2 jit_solution(2654788834022192646)
XLA Ops:
  0.0 8.0 %low_part.1 = (f32[16,256]{1,0:T(8,128)S(1)}, f32[16,256]{1,0:T(8,128)S(1)}, bf16[64,512]{1,0:T(8,128)(2,1)S(1)}, bf16[64,256]{1,0:T(8,128)(2,1)S(1)}, bf16[512,...) custom-call(s32[1,64]{1,0:T(1,128)} %bitcast.6, s32[1,64]{1,0:T(1,128)} %bitcast.7, ...), custom_call_target="tpu_custom_call" | custom-call | tf_op jit(solution)/shard_map/low_part/pallas_call | solution.py:141
  8.0 0.6 collective-permute-start
  8.6 3.5 %factors.1.mine_ref = bf16[256,1792]{1,0:T(8,128)(2,1)S(1)} custom-call(bf16[64,512]{1,0:T(8,128)(2,1)S(1)} %get-tuple-element.43.hyper_ref, bf16[512,4,1792]{2,1,0:T(4,128)(2,1)S(1)} %copy-done.1), custom_call_target="tpu_custom_call" | custom-call | tf_op jit(solution)/shard_map/factors/pallas_call | solution.py:218
  12.1 0.1 collective-permute-start.7
  12.2 3.0 %shard_map.110 = (f32[256,1792]{1,0:T(8,128)S(1)}, bf16[256,1792]{1,0:T(8,128)(2,1)S(1)}) custom-call(bf16[512,1024]{1,0:T(8,128)(2,1)S(1)} %get-tuple-element.44.x_ref, bf16[1024,1792]{1,0:T(8,128)(2,1)S(1)} %copy-done.2), custom_call_target="tpu_custom_call" | custom-call | tf_op jit(solution)/shard_map/pallas_call | solution.py:169
  15.3 0.5 collective-permute-start.8
  15.8 0.2 add_convert_fusion
  16.0 2.6 %collective-permute-start.1 = (bf16[256,1792]{1,0:T(8,128)(2,1)S(1)}, bf16[256,1792]{1,0:T(8,128)(2,1)S(1)}, u32[]{:S(2)}, u32[]{:S(2)}) collective-permute-start(bf16[256,1792]{1,0:T(8,128)(2,1)S(1)} %add_convert_fusion), channel_id=1, source_target_pairs={{0,16},{8,24},{16,0},{24,8},{1,17},{9,25},{17,1},{25,9},{2,18},{10... | collective-permute-start | bytes 2752520 | tf_op jit(solution)/shard_map/ppermute | solution.py:24
  18.6 0.2 collective-permute-start.2
  18.7 1.0 collective-permute-done.2
  19.7 1.0 collective-permute-start.3
  20.8 19.1 %collective-permute-done.3 = f32[16,256]{1,0:T(8,128)S(1)} collective-permute-done((f32[16,256]{1,0:T(8,128)S(1)}, f32[16,256]{1,0:T(8,128)S(1)}, u32[]{:S(2)}, u32[]{:S(2)}) %collective-permute-start.3) | collective-permute-done | bytes 16416 | tf_op jit(solution)/shard_map/ppermute | solution.py:24
  39.9 1.7 %collective-permute-start.4 = (f32[16,256]{1,0:T(8,128)S(1)}, f32[16,256]{1,0:T(8,128)S(1)}, u32[]{:S(2)}, u32[]{:S(2)}) collective-permute-start(f32[16,256]{1,0:T(8,128)S(1)} %add.20), channel_id=1, source_target_pairs={{0,1},{1,0},{2,3},{3,2},{4,5},{5,4},{6,7},{7,6},{8,9},{9,8},{10,11... | collective-permute-start | bytes 49160 | tf_op jit(solution)/shard_map/ppermute | solution.py:24
  41.6 2.0 %collective-permute-done.4 = f32[16,256]{1,0:T(8,128)S(1)} collective-permute-done((f32[16,256]{1,0:T(8,128)S(1)}, f32[16,256]{1,0:T(8,128)S(1)}, u32[]{:S(2)}, u32[]{:S(2)}) %collective-permute-start.4) | collective-permute-done | bytes 16416 | tf_op jit(solution)/shard_map/ppermute | solution.py:24
  43.6 1.8 %collective-permute-start.5 = (f32[16,256]{1,0:T(8,128)S(1)}, f32[16,256]{1,0:T(8,128)S(1)}, u32[]{:S(2)}, u32[]{:S(2)}) collective-permute-start(f32[16,256]{1,0:T(8,128)S(1)} %add.21), channel_id=1, source_target_pairs={{0,2},{1,3},{2,0},{3,1},{4,6},{5,7},{6,4},{7,5},{8,10},{9,11},{10,... | collective-permute-start | bytes 49160 | tf_op jit(solution)/shard_map/ppermute | solution.py:24
  45.4 1.9 %collective-permute-done.5 = f32[16,256]{1,0:T(8,128)S(1)} collective-permute-done((f32[16,256]{1,0:T(8,128)S(1)}, f32[16,256]{1,0:T(8,128)S(1)}, u32[]{:S(2)}, u32[]{:S(2)}) %collective-permute-start.5) | collective-permute-done | bytes 16416 | tf_op jit(solution)/shard_map/ppermute | solution.py:24
  47.4 3.0 %collective-permute-start.6 = (f32[16,256]{1,0:T(8,128)S(1)}, f32[16,256]{1,0:T(8,128)S(1)}, u32[]{:S(2)}, u32[]{:S(2)}) collective-permute-start(f32[16,256]{1,0:T(8,128)S(1)} %add.22), channel_id=1, source_target_pairs={{0,4},{1,5},{2,6},{3,7},{4,0},{5,1},{6,2},{7,3},{8,12},{9,13},{10,... | collective-permute-start | bytes 49160 | tf_op jit(solution)/shard_map/ppermute | solution.py:24
  50.3 1.7 %collective-permute-done.6 = f32[16,256]{1,0:T(8,128)S(1)} collective-permute-done((f32[16,256]{1,0:T(8,128)S(1)}, f32[16,256]{1,0:T(8,128)S(1)}, u32[]{:S(2)}, u32[]{:S(2)}) %collective-permute-start.6) | collective-permute-done | bytes 16416 | tf_op jit(solution)/shard_map/ppermute | solution.py:24
  52.1 1.6 %adapter.1 = (f32[256,1792]{1,0:T(8,128)S(1)}, bf16[128,1792]{1,0:T(8,128)(2,1)S(1)}, bf16[64,1792]{1,0:T(8,128)(2,1)S(1)}, bf16[64,1792]{1,0:T(8,128)(2,1)S(1)}) custom-call(f32[16,256]{1,0:T(8,128)S(1)} %add.23.low_ref, bf16[64,256]{1,0:T(8,128)(2,1)S(1)} %get-tuple-element.42.member_ref, bf16[256,1792]{1,0:T(8,128)(2,1)S(1)} %factors.1.mine_ref, ...), custom_call_target="tpu_custom_call" | custom-call | tf_op jit(solution)/shard_map/adapter/pallas_call | solution.py:261
  53.7 1.8 %collective-permute-start.9 = (bf16[128,1792]{1,0:T(8,128)(2,1)S(1)}, bf16[128,1792]{1,0:T(8,128)(2,1)S(1)}, u32[]{:S(2)}, u32[]{:S(2)}) collective-permute-start(bf16[128,1792]{1,0:T(8,128)(2,1)S(1)} %get-tuple-element.48), channel_id=1, source_target_pairs={{0,16},{8,24},{16,0},{24,8},{1,17},{9,25},{17,1},{25,9},{2,18},{10... | collective-permute-start | bytes 1376264 | tf_op jit(solution)/shard_map/ppermute | solution.py:24
  55.4 0.6 shard_map.109.act_ref
  56.1 6.5 %collective-permute-done.9.up_ref = bf16[128,1792]{1,0:T(8,128)(2,1)S(1)} collective-permute-done((bf16[128,1792]{1,0:T(8,128)(2,1)S(1)}, bf16[128,1792]{1,0:T(8,128)(2,1)S(1)}, u32[]{:S(2)}, u32[]{:S(2)}) %collective-permute-start.9) | collective-permute-done | bytes 458784 | tf_op jit(solution)/shard_map/ppermute | solution.py:24
  62.6 0.1 shard_map.111.hid_ref
  62.7 0.1 collective-permute-start.10
  62.7 1.5 %collective-permute-start.12 = (bf16[64,1792]{1,0:T(8,128)(2,1)S(1)}, bf16[64,1792]{1,0:T(8,128)(2,1)S(1)}, u32[]{:S(2)}, u32[]{:S(2)}) collective-permute-start(bf16[64,1792]{1,0:T(8,128)(2,1)S(1)} %get-tuple-element.53), channel_id=1, source_target_pairs={{0,16},{8,24},{16,0},{24,8},{1,17},{9,25},{17,1},{25,9},{2,18},{10... | collective-permute-start | bytes 688136 | tf_op jit(solution)/shard_map/ppermute | solution.py:24
  64.3 0.6 collective-permute-start.18
  64.8 6.5 %collective-permute-done.12.up_ref = bf16[64,1792]{1,0:T(8,128)(2,1)S(1)} collective-permute-done((bf16[64,1792]{1,0:T(8,128)(2,1)S(1)}, bf16[64,1792]{1,0:T(8,128)(2,1)S(1)}, u32[]{:S(2)}, u32[]{:S(2)}) %collective-permute-start.12) | collective-permute-done | bytes 229408 | tf_op jit(solution)/shard_map/ppermute | solution.py:24
  71.4 4.2 %collective-permute-done.18.up_ref = bf16[64,1792]{1,0:T(8,128)(2,1)S(1)} collective-permute-done((bf16[64,1792]{1,0:T(8,128)(2,1)S(1)}, bf16[64,1792]{1,0:T(8,128)(2,1)S(1)}, u32[]{:S(2)}, u32[]{:S(2)}) %collective-permute-start.18) | collective-permute-done | bytes 229408 | tf_op jit(solution)/shard_map/ppermute | solution.py:24
  75.8 0.7 shard_map.112
  76.5 0.7 shard_map.113
  77.2 1.5 %collective-permute-start.11 = (bf16[2,4,16,1024]{3,2,1,0:T(8,128)(2,1)S(1)}, bf16[2,4,16,1024]{3,2,1,0:T(8,128)(2,1)S(1)}, u32[]{:S(2)}, u32[]{:S(2)}) collective-permute-start(bf16[2,4,16,1024]{3,2,1,0:T(8,128)(2,1)S(1)} %get-tuple-element.52), channel_id=1, source_target_pairs={{0,1},{1,0},{2,3},{3,2},{4,5},{5,4},{6,7},{7,6},{8,9},{9,8},{10,11... | collective-permute-start | bytes 786440 | tf_op jit(solution)/shard_map/ppermute | solution.py:24
  78.7 0.7 shard_map.115
  79.4 0.8 shard_map.116
  80.2 0.7 collective-permute-start.14
  80.9 0.7 shard_map.119
  81.6 0.8 shard_map.120
  82.4 1.5 %collective-permute-start.20 = (bf16[2,4,8,1024]{3,2,1,0:T(8,128)(2,1)S(1)}, bf16[2,4,8,1024]{3,2,1,0:T(8,128)(2,1)S(1)}, u32[]{:S(2)}, u32[]{:S(2)}) collective-permute-start(bf16[2,4,8,1024]{3,2,1,0:T(8,128)(2,1)S(1)} %get-tuple-element.66), channel_id=1, source_target_pairs={{0,1},{1,0},{2,3},{3,2},{4,5},{5,4},{6,7},{7,6},{8,9},{9,8},{10,11... | collective-permute-start | bytes 393224 | tf_op jit(solution)/shard_map/ppermute | solution.py:24
  83.9 5.4 %collective-permute-done.14.refs_3_ = bf16[2,4,8,1024]{3,2,1,0:T(8,128)(2,1)S(1)} collective-permute-done((bf16[2,4,8,1024]{3,2,1,0:T(8,128)(2,1)S(1)}, bf16[2,4,8,1024]{3,2,1,0:T(8,128)(2,1)S(1)}, u32[]{:S(2)}, u32[]{:S(2)}) %collective-permute-start.14) | collective-permute-done | bytes 131104 | tf_op jit(solution)/shard_map/ppermute | solution.py:24
  89.3 1.7 %collective-permute-start.15 = (bf16[2,1,24,1024]{3,2,1,0:T(8,128)(2,1)S(1)}, bf16[2,1,24,1024]{3,2,1,0:T(8,128)(2,1)S(1)}, u32[]{:S(2)}, u32[]{:S(2)}) collective-permute-start(bf16[2,1,24,1024]{3,2,1,0:T(8,128)(2,1)S(1)} %get-tuple-element.59), channel_id=1, source_target_pairs={{0,2},{1,3},{2,0},{3,1},{4,6},{5,7},{6,4},{7,5},{8,10},{9,11},{10,... | collective-permute-start | bytes 294920 | tf_op jit(solution)/shard_map/ppermute | solution.py:24
  91.0 2.5 %collective-permute-start.16 = (bf16[2,1,24,1024]{3,2,1,0:T(8,128)(2,1)S(1)}, bf16[2,1,24,1024]{3,2,1,0:T(8,128)(2,1)S(1)}, u32[]{:S(2)}, u32[]{:S(2)}) collective-permute-start(bf16[2,1,24,1024]{3,2,1,0:T(8,128)(2,1)S(1)} %get-tuple-element.60), channel_id=1, source_target_pairs={{0,4},{1,5},{2,6},{3,7},{4,0},{5,1},{6,2},{7,3},{8,12},{9,13},{10,... | collective-permute-start | bytes 294920 | tf_op jit(solution)/shard_map/ppermute | solution.py:24
  93.6 0.2 collective-permute-start.17
  93.8 0.8 collective-permute-start.21
  94.6 3.4 %collective-permute-start.22 = (bf16[2,1,8,1024]{3,2,1,0:T(8,128)(2,1)S(1)}, bf16[2,1,8,1024]{3,2,1,0:T(8,128)(2,1)S(1)}, u32[]{:S(2)}, u32[]{:S(2)}) collective-permute-start(bf16[2,1,8,1024]{3,2,1,0:T(8,128)(2,1)S(1)} %get-tuple-element.69), channel_id=1, source_target_pairs={{0,4},{1,5},{2,6},{3,7},{4,0},{5,1},{6,2},{7,3},{8,12},{9,13},{10,... | collective-permute-start | bytes 98312 | tf_op jit(solution)/shard_map/ppermute | solution.py:24
  98.0 0.4 collective-permute-done.21.refs_5_
  98.5 4.0 %collective-permute-start.23 = (bf16[2,1,8,1024]{3,2,1,0:T(8,128)(2,1)S(1)}, bf16[2,1,8,1024]{3,2,1,0:T(8,128)(2,1)S(1)}, u32[]{:S(2)}, u32[]{:S(2)}) collective-permute-start(bf16[2,1,8,1024]{3,2,1,0:T(8,128)(2,1)S(1)} %get-tuple-element.70), channel_id=1, source_target_pairs={{0,6},{1,7},{2,4},{3,5},{4,2},{5,3},{6,0},{7,1},{8,14},{9,15},{10,... | collective-permute-start | bytes 98312 | tf_op jit(solution)/shard_map/ppermute | solution.py:24
  102.5 1.5 %collective-permute-done.22.refs_6_ = bf16[2,1,8,1024]{3,2,1,0:T(8,128)(2,1)S(1)} collective-permute-done((bf16[2,1,8,1024]{3,2,1,0:T(8,128)(2,1)S(1)}, bf16[2,1,8,1024]{3,2,1,0:T(8,128)(2,1)S(1)}, u32[]{:S(2)}, u32[]{:S(2)}) %collective-permute-start.22) | collective-permute-done | bytes 32800 | tf_op jit(solution)/shard_map/ppermute | solution.py:24
  104.0 0.5 collective-permute-done.23.refs_7_
  104.5 0.7 shard_map.122
  (29 shorter events, 0.4 us)
Async XLA Ops:
  0.0 8.6 %copy-start.1 = (bf16[512,4,1792]{2,1,0:T(4,128)(2,1)S(1)}, bf16[512,4,1792]{2,1,0:T(4,128)(2,1)}, u32[]{:S(2)}) copy-start(bf16[512,4,1792]{2,1,0:T(4,128)(2,1)} %gen_ref.1) | copy-start | bytes 22020100
  8.0 7.8 %collective-permute-start = (bf16[256,1792]{1,0:T(8,128)(2,1)S(1)}, bf16[256,1792]{1,0:T(8,128)(2,1)S(1)}, u32[]{:S(2)}, u32[]{:S(2)}) collective-permute-start(bf16[256,1792]{1,0:T(8,128)(2,1)S(1)} %get-tuple-element.39), channel_id=1, source_target_pairs={{0,8},{8,0},{16,24},{24,16},{1,9},{9,1},{17,25},{25,17},{2,10},{10... | collective-permute-start | bytes 2752520 | tf_op jit(solution)/shard_map/ppermute | solution.py:24
  8.6 3.7 %copy-start.2 = (bf16[1024,1792]{1,0:T(8,128)(2,1)S(1)}, bf16[1024,1792]{1,0:T(8,128)(2,1)}, u32[]{:S(2)}) copy-start(bf16[1024,1792]{1,0:T(8,128)(2,1)} %w_ref.7) | copy-start | bytes 11010052
  12.1 39.9 %collective-permute-start.7 = (bf16[256,1792]{1,0:T(8,128)(2,1)S(1)}, bf16[256,1792]{1,0:T(8,128)(2,1)S(1)}, u32[]{:S(2)}, u32[]{:S(2)}) collective-permute-start(bf16[256,1792]{1,0:T(8,128)(2,1)S(1)} %factors.1.mine_ref), channel_id=1, source_target_pairs={{0,8},{8,0},{16,24},{24,16},{1,9},{9,1},{17,25},{25,17},{2,10},{10... | collective-permute-start | bytes 2752520 | tf_op jit(solution)/shard_map/ppermute | solution.py:24
  15.3 36.8 %collective-permute-start.8 = (bf16[256,1792]{1,0:T(8,128)(2,1)S(1)}, bf16[256,1792]{1,0:T(8,128)(2,1)S(1)}, u32[]{:S(2)}, u32[]{:S(2)}) collective-permute-start(bf16[256,1792]{1,0:T(8,128)(2,1)S(1)} %get-tuple-element.46), channel_id=1, source_target_pairs={{0,8},{8,0},{16,24},{24,16},{1,9},{9,1},{17,25},{25,17},{2,10},{10... | collective-permute-start | bytes 2752520 | tf_op jit(solution)/shard_map/ppermute | solution.py:24
  16.0 39.5 %collective-permute-start.1 = (bf16[256,1792]{1,0:T(8,128)(2,1)S(1)}, bf16[256,1792]{1,0:T(8,128)(2,1)S(1)}, u32[]{:S(2)}, u32[]{:S(2)}) collective-permute-start(bf16[256,1792]{1,0:T(8,128)(2,1)S(1)} %add_convert_fusion), channel_id=1, source_target_pairs={{0,16},{8,24},{16,0},{24,8},{1,17},{9,25},{17,1},{25,9},{2,18},{10... | collective-permute-start | bytes 2752520 | tf_op jit(solution)/shard_map/ppermute | solution.py:24
  18.6 1.2 %collective-permute-start.2 = (f32[16,256]{1,0:T(8,128)S(1)}, f32[16,256]{1,0:T(8,128)S(1)}, u32[]{:S(2)}, u32[]{:S(2)}) collective-permute-start(f32[16,256]{1,0:T(8,128)S(1)} %get-tuple-element.41), channel_id=1, source_target_pairs={{0,8},{8,0},{16,24},{24,16},{1,9},{9,1},{17,25},{25,17},{2,10},{10... | collective-permute-start | bytes 49160 | tf_op jit(solution)/shard_map/ppermute | solution.py:24
  19.7 20.1 %collective-permute-start.3 = (f32[16,256]{1,0:T(8,128)S(1)}, f32[16,256]{1,0:T(8,128)S(1)}, u32[]{:S(2)}, u32[]{:S(2)}) collective-permute-start(f32[16,256]{1,0:T(8,128)S(1)} %add.19), channel_id=1, source_target_pairs={{0,16},{8,24},{16,0},{24,8},{1,17},{9,25},{17,1},{25,9},{2,18},{10... | collective-permute-start | bytes 49160 | tf_op jit(solution)/shard_map/ppermute | solution.py:24
  39.9 3.7 %collective-permute-start.4 = (f32[16,256]{1,0:T(8,128)S(1)}, f32[16,256]{1,0:T(8,128)S(1)}, u32[]{:S(2)}, u32[]{:S(2)}) collective-permute-start(f32[16,256]{1,0:T(8,128)S(1)} %add.20), channel_id=1, source_target_pairs={{0,1},{1,0},{2,3},{3,2},{4,5},{5,4},{6,7},{7,6},{8,9},{9,8},{10,11... | collective-permute-start | bytes 49160 | tf_op jit(solution)/shard_map/ppermute | solution.py:24
  43.6 3.7 %collective-permute-start.5 = (f32[16,256]{1,0:T(8,128)S(1)}, f32[16,256]{1,0:T(8,128)S(1)}, u32[]{:S(2)}, u32[]{:S(2)}) collective-permute-start(f32[16,256]{1,0:T(8,128)S(1)} %add.21), channel_id=1, source_target_pairs={{0,2},{1,3},{2,0},{3,1},{4,6},{5,7},{6,4},{7,5},{8,10},{9,11},{10,... | collective-permute-start | bytes 49160 | tf_op jit(solution)/shard_map/ppermute | solution.py:24
  47.4 4.7 %collective-permute-start.6 = (f32[16,256]{1,0:T(8,128)S(1)}, f32[16,256]{1,0:T(8,128)S(1)}, u32[]{:S(2)}, u32[]{:S(2)}) collective-permute-start(f32[16,256]{1,0:T(8,128)S(1)} %add.22), channel_id=1, source_target_pairs={{0,4},{1,5},{2,6},{3,7},{4,0},{5,1},{6,2},{7,3},{8,12},{9,13},{10,... | collective-permute-start | bytes 49160 | tf_op jit(solution)/shard_map/ppermute | solution.py:24
  52.1 3.4 %copy-start = (bf16[1792,1024]{1,0:T(8,128)(2,1)S(1)}, bf16[1792,1024]{1,0:T(8,128)(2,1)}, u32[]{:S(2)}) copy-start(bf16[1792,1024]{1,0:T(8,128)(2,1)} %w_ref.13) | copy-start | bytes 11010052
  53.7 8.9 %collective-permute-start.9 = (bf16[128,1792]{1,0:T(8,128)(2,1)S(1)}, bf16[128,1792]{1,0:T(8,128)(2,1)S(1)}, u32[]{:S(2)}, u32[]{:S(2)}) collective-permute-start(bf16[128,1792]{1,0:T(8,128)(2,1)S(1)} %get-tuple-element.48), channel_id=1, source_target_pairs={{0,16},{8,24},{16,0},{24,8},{1,17},{9,25},{17,1},{25,9},{2,18},{10... | collective-permute-start | bytes 1376264 | tf_op jit(solution)/shard_map/ppermute | solution.py:24
  62.7 13.8 %collective-permute-start.10 = (bf16[128,1792]{1,0:T(8,128)(2,1)S(1)}, bf16[128,1792]{1,0:T(8,128)(2,1)S(1)}, u32[]{:S(2)}, u32[]{:S(2)}) collective-permute-start(bf16[128,1792]{1,0:T(8,128)(2,1)S(1)} %shard_map.111.hid_ref), channel_id=1, source_target_pairs={{0,8},{8,0},{16,24},{24,16},{1,9},{9,1},{17,25},{25,17},{2,10},{10... | collective-permute-start | bytes 1376264 | tf_op jit(solution)/shard_map/ppermute | solution.py:24
  62.7 8.5 %collective-permute-start.12 = (bf16[64,1792]{1,0:T(8,128)(2,1)S(1)}, bf16[64,1792]{1,0:T(8,128)(2,1)S(1)}, u32[]{:S(2)}, u32[]{:S(2)}) collective-permute-start(bf16[64,1792]{1,0:T(8,128)(2,1)S(1)} %get-tuple-element.53), channel_id=1, source_target_pairs={{0,16},{8,24},{16,0},{24,8},{1,17},{9,25},{17,1},{25,9},{2,18},{10... | collective-permute-start | bytes 688136 | tf_op jit(solution)/shard_map/ppermute | solution.py:24
  64.3 11.4 %collective-permute-start.18 = (bf16[64,1792]{1,0:T(8,128)(2,1)S(1)}, bf16[64,1792]{1,0:T(8,128)(2,1)S(1)}, u32[]{:S(2)}, u32[]{:S(2)}) collective-permute-start(bf16[64,1792]{1,0:T(8,128)(2,1)S(1)} %get-tuple-element.62), channel_id=1, source_target_pairs={{0,16},{8,24},{16,0},{24,8},{1,17},{9,25},{17,1},{25,9},{2,18},{10... | collective-permute-start | bytes 688136 | tf_op jit(solution)/shard_map/ppermute | solution.py:24
  71.3 8.1 %collective-permute-start.13 = (bf16[64,1792]{1,0:T(8,128)(2,1)S(1)}, bf16[64,1792]{1,0:T(8,128)(2,1)S(1)}, u32[]{:S(2)}, u32[]{:S(2)}) collective-permute-start(bf16[64,1792]{1,0:T(8,128)(2,1)S(1)} %shard_map.114.hid_ref), channel_id=1, source_target_pairs={{0,8},{8,0},{16,24},{24,16},{1,9},{9,1},{17,25},{25,17},{2,10},{10... | collective-permute-start | bytes 688136 | tf_op jit(solution)/shard_map/ppermute | solution.py:24
  75.7 5.9 %collective-permute-start.19 = (bf16[64,1792]{1,0:T(8,128)(2,1)S(1)}, bf16[64,1792]{1,0:T(8,128)(2,1)S(1)}, u32[]{:S(2)}, u32[]{:S(2)}) collective-permute-start(bf16[64,1792]{1,0:T(8,128)(2,1)S(1)} %shard_map.118.hid_ref), channel_id=1, source_target_pairs={{0,8},{8,0},{16,24},{24,16},{1,9},{9,1},{17,25},{25,17},{2,10},{10... | collective-permute-start | bytes 688136 | tf_op jit(solution)/shard_map/ppermute | solution.py:24
  77.2 12.1 %collective-permute-start.11 = (bf16[2,4,16,1024]{3,2,1,0:T(8,128)(2,1)S(1)}, bf16[2,4,16,1024]{3,2,1,0:T(8,128)(2,1)S(1)}, u32[]{:S(2)}, u32[]{:S(2)}) collective-permute-start(bf16[2,4,16,1024]{3,2,1,0:T(8,128)(2,1)S(1)} %get-tuple-element.52), channel_id=1, source_target_pairs={{0,1},{1,0},{2,3},{3,2},{4,5},{5,4},{6,7},{7,6},{8,9},{9,8},{10,11... | collective-permute-start | bytes 786440 | tf_op jit(solution)/shard_map/ppermute | solution.py:24
  80.2 9.0 %collective-permute-start.14 = (bf16[2,4,8,1024]{3,2,1,0:T(8,128)(2,1)S(1)}, bf16[2,4,8,1024]{3,2,1,0:T(8,128)(2,1)S(1)}, u32[]{:S(2)}, u32[]{:S(2)}) collective-permute-start(bf16[2,4,8,1024]{3,2,1,0:T(8,128)(2,1)S(1)} %get-tuple-element.57), channel_id=1, source_target_pairs={{0,1},{1,0},{2,3},{3,2},{4,5},{5,4},{6,7},{7,6},{8,9},{9,8},{10,11... | collective-permute-start | bytes 393224 | tf_op jit(solution)/shard_map/ppermute | solution.py:24
  82.4 11.4 %collective-permute-start.20 = (bf16[2,4,8,1024]{3,2,1,0:T(8,128)(2,1)S(1)}, bf16[2,4,8,1024]{3,2,1,0:T(8,128)(2,1)S(1)}, u32[]{:S(2)}, u32[]{:S(2)}) collective-permute-start(bf16[2,4,8,1024]{3,2,1,0:T(8,128)(2,1)S(1)} %get-tuple-element.66), channel_id=1, source_target_pairs={{0,1},{1,0},{2,3},{3,2},{4,5},{5,4},{6,7},{7,6},{8,9},{9,8},{10,11... | collective-permute-start | bytes 393224 | tf_op jit(solution)/shard_map/ppermute | solution.py:24
  89.3 15.1 %collective-permute-start.15 = (bf16[2,1,24,1024]{3,2,1,0:T(8,128)(2,1)S(1)}, bf16[2,1,24,1024]{3,2,1,0:T(8,128)(2,1)S(1)}, u32[]{:S(2)}, u32[]{:S(2)}) collective-permute-start(bf16[2,1,24,1024]{3,2,1,0:T(8,128)(2,1)S(1)} %get-tuple-element.59), channel_id=1, source_target_pairs={{0,2},{1,3},{2,0},{3,1},{4,6},{5,7},{6,4},{7,5},{8,10},{9,11},{10,... | collective-permute-start | bytes 294920 | tf_op jit(solution)/shard_map/ppermute | solution.py:24
  91.0 13.4 %collective-permute-start.16 = (bf16[2,1,24,1024]{3,2,1,0:T(8,128)(2,1)S(1)}, bf16[2,1,24,1024]{3,2,1,0:T(8,128)(2,1)S(1)}, u32[]{:S(2)}, u32[]{:S(2)}) collective-permute-start(bf16[2,1,24,1024]{3,2,1,0:T(8,128)(2,1)S(1)} %get-tuple-element.60), channel_id=1, source_target_pairs={{0,4},{1,5},{2,6},{3,7},{4,0},{5,1},{6,2},{7,3},{8,12},{9,13},{10,... | collective-permute-start | bytes 294920 | tf_op jit(solution)/shard_map/ppermute | solution.py:24
  93.6 10.9 %collective-permute-start.17 = (bf16[2,1,24,1024]{3,2,1,0:T(8,128)(2,1)S(1)}, bf16[2,1,24,1024]{3,2,1,0:T(8,128)(2,1)S(1)}, u32[]{:S(2)}, u32[]{:S(2)}) collective-permute-start(bf16[2,1,24,1024]{3,2,1,0:T(8,128)(2,1)S(1)} %get-tuple-element.61), channel_id=1, source_target_pairs={{0,6},{1,7},{2,4},{3,5},{4,2},{5,3},{6,0},{7,1},{8,14},{9,15},{10,... | collective-permute-start | bytes 294920 | tf_op jit(solution)/shard_map/ppermute | solution.py:24
  93.8 4.7 %collective-permute-start.21 = (bf16[2,1,8,1024]{3,2,1,0:T(8,128)(2,1)S(1)}, bf16[2,1,8,1024]{3,2,1,0:T(8,128)(2,1)S(1)}, u32[]{:S(2)}, u32[]{:S(2)}) collective-permute-start(bf16[2,1,8,1024]{3,2,1,0:T(8,128)(2,1)S(1)} %get-tuple-element.68), channel_id=1, source_target_pairs={{0,2},{1,3},{2,0},{3,1},{4,6},{5,7},{6,4},{7,5},{8,10},{9,11},{10,... | collective-permute-start | bytes 98312 | tf_op jit(solution)/shard_map/ppermute | solution.py:24
  94.6 9.3 %collective-permute-start.22 = (bf16[2,1,8,1024]{3,2,1,0:T(8,128)(2,1)S(1)}, bf16[2,1,8,1024]{3,2,1,0:T(8,128)(2,1)S(1)}, u32[]{:S(2)}, u32[]{:S(2)}) collective-permute-start(bf16[2,1,8,1024]{3,2,1,0:T(8,128)(2,1)S(1)} %get-tuple-element.69), channel_id=1, source_target_pairs={{0,4},{1,5},{2,6},{3,7},{4,0},{5,1},{6,2},{7,3},{8,12},{9,13},{10,... | collective-permute-start | bytes 98312 | tf_op jit(solution)/shard_map/ppermute | solution.py:24
  98.5 6.0 %collective-permute-start.23 = (bf16[2,1,8,1024]{3,2,1,0:T(8,128)(2,1)S(1)}, bf16[2,1,8,1024]{3,2,1,0:T(8,128)(2,1)S(1)}, u32[]{:S(2)}, u32[]{:S(2)}) collective-permute-start(bf16[2,1,8,1024]{3,2,1,0:T(8,128)(2,1)S(1)} %get-tuple-element.70), channel_id=1, source_target_pairs={{0,6},{1,7},{2,4},{3,5},{4,2},{5,3},{6,0},{7,1},{8,14},{9,15},{10,... | collective-permute-start | bytes 98312 | tf_op jit(solution)/shard_map/ppermute | solution.py:24

commit v4 on v3

--- a/solution.py
+++ b/solution.py
@@ -15,8 +15,8 @@
 
 def plan(per_dest):
     if per_dest % 64 == 0:
-        return (2, 1, 1), ((0, 1), (2,))
-    return (1, 1), ((0,), (1,))
+        return (1, 1, 1, 1), ((1, 2), (3,)), True
+    return (1, 1), ((0,), (1,)), False
 
 
 def swap(x, axis, mask):
@@ -53,8 +53,8 @@
     w_hbm, *rest
 ):
     x_in, rest = (None, rest) if slab % 128 == 0 else (rest[0], rest[1:])
-    low_ref, peer_ref, hyper_ref, member_ref, toks_ref, kept_ref, sent_ref = rest[:7]
-    count_ref, task_ref, request_ref, tok_ref, emb_ref, gen_in_ref, a_ref, w_ref, ht_ref, sems = rest[7:]
+    low_ref, hyper_ref, member_ref, toks_ref, kept_ref, sent_ref = rest[:6]
+    count_ref, task_ref, request_ref, tok_ref, emb_ref, gen_in_ref, a_ref, w_ref, ht_ref, sems = rest[6:]
     copies = [
         pltpu.make_async_copy(src, dst, sems.at[i])
         for i, (src, dst) in enumerate(
@@ -75,8 +75,8 @@
     groups = count_ref.shape[1]
     tasks = emb_ref.shape[0]
     hidden = gen_in_ref.shape[1]
-    rank, half = low_ref.shape
-    rows = 2 * half
+    rank, rows = low_ref.shape
+    half = rows // 2
     core = lax.axis_index("row") & 1
     across_rows = (((0,), (0,)), ((), ()))
     for copy in copies[:3]:
@@ -120,8 +120,7 @@
         return acc + jnp.sum(t * ht_ref[pl.ds(h, part), :][:, None, :], axis=0)
 
     low = lax.fori_loop(0, hidden // part, body, jnp.zeros((rank, rows), F32))
-    low_ref[...] = low[:, :half]
-    peer_ref[...] = low[:, half:]
+    low_ref[...] = low
     copies[7].wait()
     ff = w_ref.shape[1]
     tile = halves_of(ff)
@@ -141,10 +140,9 @@
     return pl.pallas_call(
         functools.partial(low_kernel, blocks, slab, shift),
         in_specs=[hbm] * len(moved) + [vmem] * len(extra),
-        out_specs=[vmem] * 7,
+        out_specs=[vmem] * 6,
         out_shape=(
-            jax.ShapeDtypeStruct((rank, rows // 2), F32),
-            jax.ShapeDtypeStruct((rank, rows // 2), F32),
+            jax.ShapeDtypeStruct((rank, rows), F32),
             jax.ShapeDtypeStruct((groups, hidden), BF16),
             jax.ShapeDtypeStruct((groups, rows // 2), BF16),
             jax.ShapeDtypeStruct((rows, width), BF16),
@@ -279,13 +277,14 @@
     return in_vmem(gate_kernel, pltpu.VMEM(kept.shape, F32), kept, core_got, rest, later)
 
 
-def in_vmem(kernel, out, *args):
+def in_vmem(kernel, out, *args, scratch=()):
     vmem = pl.BlockSpec(memory_space=pltpu.VMEM)
     return pl.pallas_call(
         kernel,
         in_specs=[vmem] * len(args),
         out_specs=jax.tree.map(lambda _: vmem, out),
         out_shape=out,
+        scratch_shapes=scratch,
         compiler_params=pltpu.CompilerParams(vmem_limit_bytes=8 << 20),
     )(*args)
 
@@ -319,6 +318,51 @@
 def cross(other, w, own):
     out = tuple(jax.ShapeDtypeStruct((2,) + x.shape, x.dtype) for x in own)
     return in_vmem(cross_kernel, out, other, w, *own)
+
+
+def turned_split(hid_ref, w_ref, scratch):
+    acc = jnp.dot(hid_ref[...], w_ref[...], preferred_element_type=F32)
+    col = lax.axis_size("col")
+    scratch[...] = acc.reshape(col // 2, 2, acc.shape[0] // col, acc.shape[1])
+    here = lax.axis_index("col") >> 1
+    return [scratch[pl.ds(here ^ q, 1)][0] for q in range(4)]
+
+
+def turned_down_kernel(hid_ref, w_ref, *refs):
+    for part, ref in zip(turned_split(hid_ref, w_ref, refs[4]), refs):
+        ref[...] = part.astype(ref.dtype)
+
+
+def turned_cross_kernel(hid_ref, w_ref, *refs):
+    for part, own, ref in zip(turned_split(hid_ref, w_ref, refs[8]), refs[:4], refs[4:]):
+        ref[0] = own[...]
+        ref[1] = part.astype(ref.dtype)
+
+
+def turned_down(hid, w, own):
+    col = lax.axis_size("col")
+    shape = (2, hid.shape[0] // col, w.shape[1])
+    scratch = [pltpu.VMEM((col // 2,) + shape, F32)]
+    lead = () if own is None else (2,)
+    out = [jax.ShapeDtypeStruct(lead + shape, F32 if q == 0 else BF16) for q in range(4)]
+    kernel, own = (turned_down_kernel, ()) if own is None else (turned_cross_kernel, own)
+    return in_vmem(kernel, out, hid, w, *own, scratch=scratch)
+
+
+def turned_fold_kernel(total_ref, *refs):
+    side = lax.axis_index("col") & 1
+    for ref, which in ((refs[3], side), (refs[4], 1 - side)):
+        at = pl.ds(which, 1)
+        value = total_ref[:, at]
+        for got in refs[:3]:
+            value += got[:, at].astype(F32)
+        ref[...] = value.astype(ref.dtype)
+
+
+def turned_fold(total, gots):
+    shape = total.shape[:1] + (1,) + total.shape[2:]
+    out = (jax.ShapeDtypeStruct(shape, F32), jax.ShapeDtypeStruct(shape, BF16))
+    return in_vmem(turned_fold_kernel, out, total, *gots)
 
 
 def fold_kernel(bit, keep_ref, got_ref, new_ref, give_ref):
@@ -356,13 +400,13 @@
     return in_vmem(kernel, out, *[x for part in parts for x in part])
 
 
-def join_kernel(count, *refs):
+def join_kernel(counts, *refs):
     out_ref = refs[-1]
     requests, draft, width = out_ref.shape
     core = lax.axis_index("row") & 1
     start = 0
-    for k in range(count):
-        total, *got = refs[4 * k : 4 * k + 4]
+    for count in counts:
+        (total, *got), refs = refs[:count], refs[count:]
         for side in range(2):
             value = total[side, 0]
             for g in got:
@@ -374,7 +418,8 @@
 
 
 def join(parts, out):
-    return in_vmem(functools.partial(join_kernel, len(parts)), out, *[x for p in parts for x in p])
+    kernel = functools.partial(join_kernel, tuple(len(p) for p in parts))
+    return in_vmem(kernel, out, *[x for p in parts for x in p])
 
 
 def hidden_kernel(start, act_ref, half_ref, up_ref, out_ref):
@@ -398,7 +443,8 @@
     slab = gen_a.shape[1]
 
     per_dest = rows // cn
-    chunks, joint = plan(per_dest)
+    chunks, joint, turned = plan(per_dest)
+    turned = turned and len(cmasks) == 3
     sizes = [per_dest * part // sum(chunks) for part in chunks]
     blocks, pieces, target, source = [], [], 0, 0
     for size in sizes:
@@ -421,7 +467,7 @@
                 for begin, _, size in blocks
             ]
         )
-    low, low_sent, hyper, own_member, toks, gate_kept, gate_sent = low_part(
+    low, hyper, own_member, toks, gate_kept, gate_sent = low_part(
         tuple(blocks),
         shift,
         group_count[None, :],
@@ -434,7 +480,6 @@
         w_gate,
         x,
     )
-    low = low + swap(low_sent, "row", 1)
     gate_got = swap(gate_sent, "row", 1)
     for m in rmasks[1:]:
         low = low + swap(low, "row", m)
@@ -456,8 +501,11 @@
     up_got = swap(up_sent, "row", 1)
     b_mine = factors(hyper, gen_b)
     b_peer = swap(b_mine, "row", 1)
-    for m in cmasks:
+    for m in cmasks[:-2]:
         low = low + swap(low, "col", m)
+    gots = [swap(low, "col", q * cmasks[-2]) for q in (1, 2, 3)]
+    low = low + gots[0] + gots[1] + gots[2]
+    low = low[:, : rows // 2] + swap(low[:, rows // 2 :], "row", 1)
 
     up_half, *up_sums = add_adapter(
         tuple(pieces), low, own_member, b_mine, b_peer, up_kept, up_got
@@ -469,6 +517,14 @@
         up_rest = others(up_sums[k])
         hid = hidden_units(piece, act, up_half, up_rest)
         other = swap(hid, "row", 1)
+        if k == 0 and turned:
+            own = turned_down(hid, w_down, None)
+            total, *gives = turned_down(other, w_down, own)
+            gots = [swap(give, "col", (q + 1) << 1) for q, give in enumerate(gives)]
+            keep, give = turned_fold(total, gots)
+            first = [keep, swap(give, "col", 1)]
+            outs.append(None)
+            continue
         keep, give = cross(other, w_down, down(hid, w_down))
         for s, m in enumerate(cmasks[:-2]):
             got = swap(give, "col", m)
@@ -476,7 +532,7 @@
                 keep, give = fold(s + 1, keep, got)
         outs.append((keep, got))
     low_bit = len(cmasks) - 2
-    parts = []
+    parts = [first] if turned else []
     for members in joint:
         total, *gives = last_split(low_bit, [outs[k] for k in members])
         gots = [swap(give, "col", (q + 1) << low_bit) for q, give in enumerate(gives)]

time: 105 us -> 113 us (1.076)
  waiting for transfers between devices: 50.8 us -> 57.4 us
  Pallas kernels: 22.1 us -> 24 us
    ppermute x24 -> x31, waiting for transfers between devices: 50.8 us -> 57.4 us  [swap(): return lax.ppermute(x, axis, [(i, i ^ mask) for i in range(n)])]
    pallas_call x13 -> x17, Pallas kernels: 6.01 us -> 7.71 us  [in_vmem(): pl.pallas_call(kernel, in_specs=[vmem] * len(args), out_specs=jax.tree.ma...]
    ppermute x24 -> x31, starting transfers between devices: 31.9 us -> 30.9 us  [swap(): return lax.ppermute(x, axis, [(i, i ^ mask) for i in range(n)])]
  transfers between devices with their start and end apart: 24 -> 31, of which waited for: 12 -> 13; matrix products, arithmetic and copies ran while one was open for 0% -> 0% of each run, Pallas kernels for 13% -> 14%
where the time goes in v4:
time: 113 us
  waiting for transfers between devices  57.4 us (51%)
  starting transfers between devices  30.9 us (27%)
  Pallas kernels  24 us (21%)
    ppermute x31, waiting for transfers between devices, swap(): return lax.ppermute(x, axis, [(i, i ^ mask) for i in range(n)])  57.4 us
    ppermute x31, starting transfers between devices, swap(): return lax.ppermute(x, axis, [(i, i ^ mask) for i in range(n)])  30.9 us
    pallas_call x1, Pallas kernels, low_part(): pl.pallas_call(functools.partial(low_kernel, blocks, slab, shift), in_spe...  7.99 us
    pallas_call x17, Pallas kernels, in_vmem(): pl.pallas_call(kernel, in_specs=[vmem] * len(args), out_specs=jax.tree.ma...  7.71 us
    pallas_call x1, Pallas kernels, factors(): pl.pallas_call(factor_kernel, grid=(ff // tile,), in_specs=[pl.BlockSpec(...  3.55 us
    pallas_call x1, Pallas kernels, split_matmul(): pl.pallas_call(split_kernel, grid=(ff // tile,), in_specs=[pl.BlockSpec((...  3.01 us
  transfers between devices with their start and end apart: 31, of which 13 were waited for; matrix products, arithmetic and copies ran while one was open for 0% of the time, Pallas kernels for 14%

profile of v4, /device:TPU:0, one launch (start us, length us, event | category | flops | bytes accessed | tf_op | source)
XLA Modules:
  0.0 112.8 jit_solution(15104823837142400866)
XLA Ops:
  0.0 8.0 %low_part.1 = (f32[16,512]{1,0:T(8,128)S(1)}, bf16[64,512]{1,0:T(8,128)(2,1)S(1)}, bf16[64,256]{1,0:T(8,128)(2,1)S(1)}, bf16[512,1024]{1,0:T(8,128)(2,1)S(1)}, f...) custom-call(s32[1,64]{1,0:T(1,128)} %bitcast.6, s32[1,64]{1,0:T(1,128)} %bitcast.7, ...), custom_call_target="tpu_custom_call" | custom-call | tf_op jit(solution)/shard_map/low_part/pallas_call | solution.py:140
  8.0 0.6 collective-permute-start
  8.6 3.5 %factors.1.mine_ref = bf16[256,1792]{1,0:T(8,128)(2,1)S(1)} custom-call(bf16[64,512]{1,0:T(8,128)(2,1)S(1)} %get-tuple-element.52.hyper_ref, bf16[512,4,1792]{2,1,0:T(4,128)(2,1)S(1)} %copy-done.1), custom_call_target="tpu_custom_call" | custom-call | tf_op jit(solution)/shard_map/factors/pallas_call | solution.py:216
  12.2 3.0 %shard_map.110 = (f32[256,1792]{1,0:T(8,128)S(1)}, bf16[256,1792]{1,0:T(8,128)(2,1)S(1)}) custom-call(bf16[512,1024]{1,0:T(8,128)(2,1)S(1)} %get-tuple-element.53.x_ref, bf16[1024,1792]{1,0:T(8,128)(2,1)S(1)} %copy-done.2), custom_call_target="tpu_custom_call" | custom-call | tf_op jit(solution)/shard_map/pallas_call | solution.py:167
  15.2 0.5 collective-permute-start.9
  15.8 0.2 add_convert_fusion
  15.9 2.6 %collective-permute-start.1 = (bf16[256,1792]{1,0:T(8,128)(2,1)S(1)}, bf16[256,1792]{1,0:T(8,128)(2,1)S(1)}, u32[]{:S(2)}, u32[]{:S(2)}) collective-permute-start(bf16[256,1792]{1,0:T(8,128)(2,1)S(1)} %add_convert_fusion), channel_id=1, source_target_pairs={{0,16},{8,24},{16,0},{24,8},{1,17},{9,25},{17,1},{25,9},{2,18},{10... | collective-permute-start | bytes 2752520 | tf_op jit(solution)/shard_map/ppermute | solution.py:24
  18.6 21.6 %collective-permute-done.2 = f32[16,512]{1,0:T(8,128)S(1)} collective-permute-done((f32[16,512]{1,0:T(8,128)S(1)}, f32[16,512]{1,0:T(8,128)S(1)}, u32[]{:S(2)}, u32[]{:S(2)}) %collective-permute-start.2) | collective-permute-done | bytes 32800 | tf_op jit(solution)/shard_map/ppermute | solution.py:24
  40.2 1.7 %collective-permute-start.3 = (f32[16,512]{1,0:T(8,128)S(1)}, f32[16,512]{1,0:T(8,128)S(1)}, u32[]{:S(2)}, u32[]{:S(2)}) collective-permute-start(f32[16,512]{1,0:T(8,128)S(1)} %add.22), channel_id=1, source_target_pairs={{0,1},{1,0},{2,3},{3,2},{4,5},{5,4},{6,7},{7,6},{8,9},{9,8},{10,11... | collective-permute-start | bytes 98312 | tf_op jit(solution)/shard_map/ppermute | solution.py:24
  42.0 2.2 %collective-permute-done.3 = f32[16,512]{1,0:T(8,128)S(1)} collective-permute-done((f32[16,512]{1,0:T(8,128)S(1)}, f32[16,512]{1,0:T(8,128)S(1)}, u32[]{:S(2)}, u32[]{:S(2)}) %collective-permute-start.3) | collective-permute-done | bytes 32800 | tf_op jit(solution)/shard_map/ppermute | solution.py:24
  44.2 3.8 %collective-permute-start.6 = (f32[16,512]{1,0:T(8,128)S(1)}, f32[16,512]{1,0:T(8,128)S(1)}, u32[]{:S(2)}, u32[]{:S(2)}) collective-permute-start(f32[16,512]{1,0:T(8,128)S(1)} %add.23), channel_id=1, source_target_pairs={{0,6},{1,7},{2,4},{3,5},{4,2},{5,3},{6,0},{7,1},{8,14},{9,15},{10,... | collective-permute-start | bytes 98312 | tf_op jit(solution)/shard_map/ppermute | solution.py:24
  48.0 1.9 %collective-permute-done.6 = f32[16,512]{1,0:T(8,128)S(1)} collective-permute-done((f32[16,512]{1,0:T(8,128)S(1)}, f32[16,512]{1,0:T(8,128)S(1)}, u32[]{:S(2)}, u32[]{:S(2)}) %collective-permute-start.6) | collective-permute-done | bytes 32800 | tf_op jit(solution)/shard_map/ppermute | solution.py:24
  49.9 2.9 %collective-permute-done.5 = f32[16,512]{1,0:T(8,128)S(1)} collective-permute-done((f32[16,512]{1,0:T(8,128)S(1)}, f32[16,512]{1,0:T(8,128)S(1)}, u32[]{:S(2)}, u32[]{:S(2)}) %collective-permute-start.5) | collective-permute-done | bytes 32800 | tf_op jit(solution)/shard_map/ppermute | solution.py:24
  52.8 1.0 collective-permute-done.4
  53.9 1.2 %collective-permute-done.7 = f32[16,256]{1,0:T(8,128)S(1)} collective-permute-done((f32[16,256]{1,0:T(8,128)S(1)}, f32[16,256]{1,0:T(8,128)S(1)}, u32[]{:S(2)}, u32[]{:S(2)}) %collective-permute-start.7) | collective-permute-done | bytes 16416 | tf_op jit(solution)/shard_map/ppermute | solution.py:24
  55.1 1.8 %adapter.1 = (f32[256,1792]{1,0:T(8,128)S(1)}, bf16[64,1792]{1,0:T(8,128)(2,1)S(1)}, bf16[64,1792]{1,0:T(8,128)(2,1)S(1)}, bf16[64,1792]{1,0:T(8,128)(2,1)S(1)}, bf16[64,1792]{1,0:T(8,128)(2,1)S(1)}) custom-call(f32[16,256]{1,0:T(8,128)S(1)} %slice_add_fusion.low_ref, bf16[64,256]{1,0:T(8,128)(2,1)S(1)} %get-tuple-element.51.member_ref, ...), custom_call_target="tpu_custom_call" | custom-call | tf_op jit(solution)/shard_map/adapter/pallas_call | solution.py:259
  56.9 1.9 %collective-permute-start.10 = (bf16[64,1792]{1,0:T(8,128)(2,1)S(1)}, bf16[64,1792]{1,0:T(8,128)(2,1)S(1)}, u32[]{:S(2)}, u32[]{:S(2)}) collective-permute-start(bf16[64,1792]{1,0:T(8,128)(2,1)S(1)} %get-tuple-element.57), channel_id=1, source_target_pairs={{0,16},{8,24},{16,0},{24,8},{1,17},{9,25},{17,1},{25,9},{2,18},{10... | collective-permute-start | bytes 688136 | tf_op jit(solution)/shard_map/ppermute | solution.py:24
  58.8 0.2 collective-permute-start.16
  59.0 1.8 %collective-permute-start.25 = (bf16[64,1792]{1,0:T(8,128)(2,1)S(1)}, bf16[64,1792]{1,0:T(8,128)(2,1)S(1)}, u32[]{:S(2)}, u32[]{:S(2)}) collective-permute-start(bf16[64,1792]{1,0:T(8,128)(2,1)S(1)} %get-tuple-element.82), channel_id=1, source_target_pairs={{0,16},{8,24},{16,0},{24,8},{1,17},{9,25},{17,1},{25,9},{2,18},{10... | collective-permute-start | bytes 688136 | tf_op jit(solution)/shard_map/ppermute | solution.py:24
  60.8 0.2 collective-permute-start.19
  61.0 0.6 shard_map.109.act_ref
  61.6 3.8 %collective-permute-done.10.up_ref = bf16[64,1792]{1,0:T(8,128)(2,1)S(1)} collective-permute-done((bf16[64,1792]{1,0:T(8,128)(2,1)S(1)}, bf16[64,1792]{1,0:T(8,128)(2,1)S(1)}, u32[]{:S(2)}, u32[]{:S(2)}) %collective-permute-start.10) | collective-permute-done | bytes 229408 | tf_op jit(solution)/shard_map/ppermute | solution.py:24
  65.6 4.8 %collective-permute-done.16.up_ref = bf16[64,1792]{1,0:T(8,128)(2,1)S(1)} collective-permute-done((bf16[64,1792]{1,0:T(8,128)(2,1)S(1)}, bf16[64,1792]{1,0:T(8,128)(2,1)S(1)}, u32[]{:S(2)}, u32[]{:S(2)}) %collective-permute-start.16) | collective-permute-done | bytes 229408 | tf_op jit(solution)/shard_map/ppermute | solution.py:24
  70.5 4.8 %collective-permute-done.25.up_ref = bf16[64,1792]{1,0:T(8,128)(2,1)S(1)} collective-permute-done((bf16[64,1792]{1,0:T(8,128)(2,1)S(1)}, bf16[64,1792]{1,0:T(8,128)(2,1)S(1)}, u32[]{:S(2)}, u32[]{:S(2)}) %collective-permute-start.25) | collective-permute-done | bytes 229408 | tf_op jit(solution)/shard_map/ppermute | solution.py:24
  75.4 4.1 %collective-permute-done.19.up_ref = bf16[64,1792]{1,0:T(8,128)(2,1)S(1)} collective-permute-done((bf16[64,1792]{1,0:T(8,128)(2,1)S(1)}, bf16[64,1792]{1,0:T(8,128)(2,1)S(1)}, u32[]{:S(2)}, u32[]{:S(2)}) %collective-permute-start.19) | collective-permute-done | bytes 229408 | tf_op jit(solution)/shard_map/ppermute | solution.py:24
  79.6 0.8 shard_map.112
  80.4 0.8 shard_map.116
  81.1 0.8 shard_map.119
  81.9 0.8 shard_map.123
  82.7 0.8 shard_map.113
  83.5 0.8 shard_map.117
  84.3 1.8 %collective-permute-start.18 = (bf16[2,4,8,1024]{3,2,1,0:T(8,128)(2,1)S(1)}, bf16[2,4,8,1024]{3,2,1,0:T(8,128)(2,1)S(1)}, u32[]{:S(2)}, u32[]{:S(2)}) collective-permute-start(bf16[2,4,8,1024]{3,2,1,0:T(8,128)(2,1)S(1)} %get-tuple-element.72), channel_id=1, source_target_pairs={{0,1},{1,0},{2,3},{3,2},{4,5},{5,4},{6,7},{7,6},{8,9},{9,8},{10,11... | collective-permute-start | bytes 393224 | tf_op jit(solution)/shard_map/ppermute | solution.py:24
  86.1 0.8 shard_map.124
  86.8 0.4 collective-permute-start.27
  87.2 0.8 shard_map.120
  88.0 1.8 %collective-permute-start.21 = (bf16[2,4,8,1024]{3,2,1,0:T(8,128)(2,1)S(1)}, bf16[2,4,8,1024]{3,2,1,0:T(8,128)(2,1)S(1)}, u32[]{:S(2)}, u32[]{:S(2)}) collective-permute-start(bf16[2,4,8,1024]{3,2,1,0:T(8,128)(2,1)S(1)} %get-tuple-element.77), channel_id=1, source_target_pairs={{0,1},{1,0},{2,3},{3,2},{4,5},{5,4},{6,7},{7,6},{8,9},{9,8},{10,11... | collective-permute-start | bytes 393224 | tf_op jit(solution)/shard_map/ppermute | solution.py:24
  89.7 4.0 %collective-permute-start.13 = (bf16[2,2,8,1024]{3,2,1,0:T(8,128)(2,1)S(1)}, bf16[2,2,8,1024]{3,2,1,0:T(8,128)(2,1)S(1)}, u32[]{:S(2)}, u32[]{:S(2)}) collective-permute-start(bf16[2,2,8,1024]{3,2,1,0:T(8,128)(2,1)S(1)} %get-tuple-element.64), channel_id=1, source_target_pairs={{0,4},{1,5},{2,6},{3,7},{4,0},{5,1},{6,2},{7,3},{8,12},{9,13},{10,... | collective-permute-start | bytes 196616 | tf_op jit(solution)/shard_map/ppermute | solution.py:24
  93.8 0.3 collective-permute-start.14
  94.1 4.0 %collective-permute-done.13.refs_1_ = bf16[2,2,8,1024]{3,2,1,0:T(8,128)(2,1)S(1)} collective-permute-done((bf16[2,2,8,1024]{3,2,1,0:T(8,128)(2,1)S(1)}, bf16[2,2,8,1024]{3,2,1,0:T(8,128)(2,1)S(1)}, u32[]{:S(2)}, u32[]{:S(2)}) %collective-permute-start.13) | collective-permute-done | bytes 65568 | tf_op jit(solution)/shard_map/ppermute | solution.py:24
  98.1 1.7 %collective-permute-done.14.refs_2_ = bf16[2,2,8,1024]{3,2,1,0:T(8,128)(2,1)S(1)} collective-permute-done((bf16[2,2,8,1024]{3,2,1,0:T(8,128)(2,1)S(1)}, bf16[2,2,8,1024]{3,2,1,0:T(8,128)(2,1)S(1)}, u32[]{:S(2)}, u32[]{:S(2)}) %collective-permute-start.14) | collective-permute-done | bytes 65568 | tf_op jit(solution)/shard_map/ppermute | solution.py:24
  99.9 0.6 collective-permute-start.15
  100.7 2.0 %collective-permute-start.22 = (bf16[2,1,16,1024]{3,2,1,0:T(8,128)(2,1)S(1)}, bf16[2,1,16,1024]{3,2,1,0:T(8,128)(2,1)S(1)}, u32[]{:S(2)}, u32[]{:S(2)}) collective-permute-start(bf16[2,1,16,1024]{3,2,1,0:T(8,128)(2,1)S(1)} %get-tuple-element.79), channel_id=1, source_target_pairs={{0,2},{1,3},{2,0},{3,1},{4,6},{5,7},{6,4},{7,5},{8,10},{9,11},{10,... | collective-permute-start | bytes 196616 | tf_op jit(solution)/shard_map/ppermute | solution.py:24
  102.7 1.3 %collective-permute-start.23 = (bf16[2,1,16,1024]{3,2,1,0:T(8,128)(2,1)S(1)}, bf16[2,1,16,1024]{3,2,1,0:T(8,128)(2,1)S(1)}, u32[]{:S(2)}, u32[]{:S(2)}) collective-permute-start(bf16[2,1,16,1024]{3,2,1,0:T(8,128)(2,1)S(1)} %get-tuple-element.80), channel_id=1, source_target_pairs={{0,4},{1,5},{2,6},{3,7},{4,0},{5,1},{6,2},{7,3},{8,12},{9,13},{10,... | collective-permute-start | bytes 196616 | tf_op jit(solution)/shard_map/ppermute | solution.py:24
  104.0 1.2 %collective-permute-start.24 = (bf16[2,1,16,1024]{3,2,1,0:T(8,128)(2,1)S(1)}, bf16[2,1,16,1024]{3,2,1,0:T(8,128)(2,1)S(1)}, u32[]{:S(2)}, u32[]{:S(2)}) collective-permute-start(bf16[2,1,16,1024]{3,2,1,0:T(8,128)(2,1)S(1)} %get-tuple-element.81), channel_id=1, source_target_pairs={{0,6},{1,7},{2,4},{3,5},{4,2},{5,3},{6,0},{7,1},{8,14},{9,15},{10,... | collective-permute-start | bytes 196616 | tf_op jit(solution)/shard_map/ppermute | solution.py:24
  105.2 1.0 collective-permute-start.29
  106.2 2.4 %collective-permute-start.30 = (bf16[2,1,8,1024]{3,2,1,0:T(8,128)(2,1)S(1)}, bf16[2,1,8,1024]{3,2,1,0:T(8,128)(2,1)S(1)}, u32[]{:S(2)}, u32[]{:S(2)}) collective-permute-start(bf16[2,1,8,1024]{3,2,1,0:T(8,128)(2,1)S(1)} %get-tuple-element.90), channel_id=1, source_target_pairs={{0,6},{1,7},{2,4},{3,5},{4,2},{5,3},{6,0},{7,1},{8,14},{9,15},{10,... | collective-permute-start | bytes 98312 | tf_op jit(solution)/shard_map/ppermute | solution.py:24
  108.6 3.5 %collective-permute-done.29.refs_8_ = bf16[2,1,8,1024]{3,2,1,0:T(8,128)(2,1)S(1)} collective-permute-done((bf16[2,1,8,1024]{3,2,1,0:T(8,128)(2,1)S(1)}, bf16[2,1,8,1024]{3,2,1,0:T(8,128)(2,1)S(1)}, u32[]{:S(2)}, u32[]{:S(2)}) %collective-permute-start.29) | collective-permute-done | bytes 32800 | tf_op jit(solution)/shard_map/ppermute | solution.py:24
  112.1 0.7 shard_map.126
  (47 shorter events, 1.1 us)
Async XLA Ops:
  0.0 8.6 %copy-start.1 = (bf16[512,4,1792]{2,1,0:T(4,128)(2,1)S(1)}, bf16[512,4,1792]{2,1,0:T(4,128)(2,1)}, u32[]{:S(2)}) copy-start(bf16[512,4,1792]{2,1,0:T(4,128)(2,1)} %gen_ref.1) | copy-start | bytes 22020100
  8.0 7.8 %collective-permute-start = (bf16[256,1792]{1,0:T(8,128)(2,1)S(1)}, bf16[256,1792]{1,0:T(8,128)(2,1)S(1)}, u32[]{:S(2)}, u32[]{:S(2)}) collective-permute-start(bf16[256,1792]{1,0:T(8,128)(2,1)S(1)} %get-tuple-element.49), channel_id=1, source_target_pairs={{0,8},{8,0},{16,24},{24,16},{1,9},{9,1},{17,25},{25,17},{2,10},{10... | collective-permute-start | bytes 2752520 | tf_op jit(solution)/shard_map/ppermute | solution.py:24
  8.6 3.7 %copy-start.2 = (bf16[1024,1792]{1,0:T(8,128)(2,1)S(1)}, bf16[1024,1792]{1,0:T(8,128)(2,1)}, u32[]{:S(2)}) copy-start(bf16[1024,1792]{1,0:T(8,128)(2,1)} %w_ref.9) | copy-start | bytes 11010052
  12.1 43.0 %collective-permute-start.8 = (bf16[256,1792]{1,0:T(8,128)(2,1)S(1)}, bf16[256,1792]{1,0:T(8,128)(2,1)S(1)}, u32[]{:S(2)}, u32[]{:S(2)}) collective-permute-start(bf16[256,1792]{1,0:T(8,128)(2,1)S(1)} %factors.1.mine_ref), channel_id=1, source_target_pairs={{0,8},{8,0},{16,24},{24,16},{1,9},{9,1},{17,25},{25,17},{2,10},{10... | collective-permute-start | bytes 2752520 | tf_op jit(solution)/shard_map/ppermute | solution.py:24
  15.2 39.9 %collective-permute-start.9 = (bf16[256,1792]{1,0:T(8,128)(2,1)S(1)}, bf16[256,1792]{1,0:T(8,128)(2,1)S(1)}, u32[]{:S(2)}, u32[]{:S(2)}) collective-permute-start(bf16[256,1792]{1,0:T(8,128)(2,1)S(1)} %get-tuple-element.55), channel_id=1, source_target_pairs={{0,8},{8,0},{16,24},{24,16},{1,9},{9,1},{17,25},{25,17},{2,10},{10... | collective-permute-start | bytes 2752520 | tf_op jit(solution)/shard_map/ppermute | solution.py:24
  15.9 45.1 %collective-permute-start.1 = (bf16[256,1792]{1,0:T(8,128)(2,1)S(1)}, bf16[256,1792]{1,0:T(8,128)(2,1)S(1)}, u32[]{:S(2)}, u32[]{:S(2)}) collective-permute-start(bf16[256,1792]{1,0:T(8,128)(2,1)S(1)} %add_convert_fusion), channel_id=1, source_target_pairs={{0,16},{8,24},{16,0},{24,8},{1,17},{9,25},{17,1},{25,9},{2,18},{10... | collective-permute-start | bytes 2752520 | tf_op jit(solution)/shard_map/ppermute | solution.py:24
  18.5 21.7 %collective-permute-start.2 = (f32[16,512]{1,0:T(8,128)S(1)}, f32[16,512]{1,0:T(8,128)S(1)}, u32[]{:S(2)}, u32[]{:S(2)}) collective-permute-start(f32[16,512]{1,0:T(8,128)S(1)} %get-tuple-element.50), channel_id=1, source_target_pairs={{0,16},{8,24},{16,0},{24,8},{1,17},{9,25},{17,1},{25,9},{2,18},{10... | collective-permute-start | bytes 98312 | tf_op jit(solution)/shard_map/ppermute | solution.py:24
  40.2 3.9 %collective-permute-start.3 = (f32[16,512]{1,0:T(8,128)S(1)}, f32[16,512]{1,0:T(8,128)S(1)}, u32[]{:S(2)}, u32[]{:S(2)}) collective-permute-start(f32[16,512]{1,0:T(8,128)S(1)} %add.22), channel_id=1, source_target_pairs={{0,1},{1,0},{2,3},{3,2},{4,5},{5,4},{6,7},{7,6},{8,9},{9,8},{10,11... | collective-permute-start | bytes 98312 | tf_op jit(solution)/shard_map/ppermute | solution.py:24
  44.2 5.7 %collective-permute-start.6 = (f32[16,512]{1,0:T(8,128)S(1)}, f32[16,512]{1,0:T(8,128)S(1)}, u32[]{:S(2)}, u32[]{:S(2)}) collective-permute-start(f32[16,512]{1,0:T(8,128)S(1)} %add.23), channel_id=1, source_target_pairs={{0,6},{1,7},{2,4},{3,5},{4,2},{5,3},{6,0},{7,1},{8,14},{9,15},{10,... | collective-permute-start | bytes 98312 | tf_op jit(solution)/shard_map/ppermute | solution.py:24
  48.0 4.8 %collective-permute-start.5 = (f32[16,512]{1,0:T(8,128)S(1)}, f32[16,512]{1,0:T(8,128)S(1)}, u32[]{:S(2)}, u32[]{:S(2)}) collective-permute-start(f32[16,512]{1,0:T(8,128)S(1)} %add.23), channel_id=1, source_target_pairs={{0,4},{1,5},{2,6},{3,7},{4,0},{5,1},{6,2},{7,3},{8,12},{9,13},{10,... | collective-permute-start | bytes 98312 | tf_op jit(solution)/shard_map/ppermute | solution.py:24
  49.9 3.9 %collective-permute-start.4 = (f32[16,512]{1,0:T(8,128)S(1)}, f32[16,512]{1,0:T(8,128)S(1)}, u32[]{:S(2)}, u32[]{:S(2)}) collective-permute-start(f32[16,512]{1,0:T(8,128)S(1)} %add.23), channel_id=1, source_target_pairs={{0,2},{1,3},{2,0},{3,1},{4,6},{5,7},{6,4},{7,5},{8,10},{9,11},{10,... | collective-permute-start | bytes 98312 | tf_op jit(solution)/shard_map/ppermute | solution.py:24
  53.8 1.2 %collective-permute-start.7 = (f32[16,256]{1,0:T(8,128)S(1)}, f32[16,256]{1,0:T(8,128)S(1)}, u32[]{:S(2)}, u32[]{:S(2)}) collective-permute-start(f32[16,256]{1,0:T(8,128)S(1)} %slice.9), channel_id=1, source_target_pairs={{0,8},{8,0},{16,24},{24,16},{1,9},{9,1},{17,25},{25,17},{2,10},{10... | collective-permute-start | bytes 49160 | tf_op jit(solution)/shard_map/ppermute | solution.py:24
  55.1 5.9 %copy-start = (bf16[1792,1024]{1,0:T(8,128)(2,1)S(1)}, bf16[1792,1024]{1,0:T(8,128)(2,1)}, u32[]{:S(2)}) copy-start(bf16[1792,1024]{1,0:T(8,128)(2,1)} %w_ref.17) | copy-start | bytes 11010052
  56.9 8.5 %collective-permute-start.10 = (bf16[64,1792]{1,0:T(8,128)(2,1)S(1)}, bf16[64,1792]{1,0:T(8,128)(2,1)S(1)}, u32[]{:S(2)}, u32[]{:S(2)}) collective-permute-start(bf16[64,1792]{1,0:T(8,128)(2,1)S(1)} %get-tuple-element.57), channel_id=1, source_target_pairs={{0,16},{8,24},{16,0},{24,8},{1,17},{9,25},{17,1},{25,9},{2,18},{10... | collective-permute-start | bytes 688136 | tf_op jit(solution)/shard_map/ppermute | solution.py:24
  58.8 11.6 %collective-permute-start.16 = (bf16[64,1792]{1,0:T(8,128)(2,1)S(1)}, bf16[64,1792]{1,0:T(8,128)(2,1)S(1)}, u32[]{:S(2)}, u32[]{:S(2)}) collective-permute-start(bf16[64,1792]{1,0:T(8,128)(2,1)S(1)} %get-tuple-element.68), channel_id=1, source_target_pairs={{0,16},{8,24},{16,0},{24,8},{1,17},{9,25},{17,1},{25,9},{2,18},{10... | collective-permute-start | bytes 688136 | tf_op jit(solution)/shard_map/ppermute | solution.py:24
  59.0 16.3 %collective-permute-start.25 = (bf16[64,1792]{1,0:T(8,128)(2,1)S(1)}, bf16[64,1792]{1,0:T(8,128)(2,1)S(1)}, u32[]{:S(2)}, u32[]{:S(2)}) collective-permute-start(bf16[64,1792]{1,0:T(8,128)(2,1)S(1)} %get-tuple-element.82), channel_id=1, source_target_pairs={{0,16},{8,24},{16,0},{24,8},{1,17},{9,25},{17,1},{25,9},{2,18},{10... | collective-permute-start | bytes 688136 | tf_op jit(solution)/shard_map/ppermute | solution.py:24
  60.8 18.7 %collective-permute-start.19 = (bf16[64,1792]{1,0:T(8,128)(2,1)S(1)}, bf16[64,1792]{1,0:T(8,128)(2,1)S(1)}, u32[]{:S(2)}, u32[]{:S(2)}) collective-permute-start(bf16[64,1792]{1,0:T(8,128)(2,1)S(1)} %get-tuple-element.73), channel_id=1, source_target_pairs={{0,16},{8,24},{16,0},{24,8},{1,17},{9,25},{17,1},{25,9},{2,18},{10... | collective-permute-start | bytes 688136 | tf_op jit(solution)/shard_map/ppermute | solution.py:24
  65.5 17.2 %collective-permute-start.11 = (bf16[64,1792]{1,0:T(8,128)(2,1)S(1)}, bf16[64,1792]{1,0:T(8,128)(2,1)S(1)}, u32[]{:S(2)}, u32[]{:S(2)}) collective-permute-start(bf16[64,1792]{1,0:T(8,128)(2,1)S(1)} %shard_map.111.hid_ref), channel_id=1, source_target_pairs={{0,8},{8,0},{16,24},{24,16},{1,9},{9,1},{17,25},{25,17},{2,10},{10... | collective-permute-start | bytes 688136 | tf_op jit(solution)/shard_map/ppermute | solution.py:24
  70.4 13.1 %collective-permute-start.17 = (bf16[64,1792]{1,0:T(8,128)(2,1)S(1)}, bf16[64,1792]{1,0:T(8,128)(2,1)S(1)}, u32[]{:S(2)}, u32[]{:S(2)}) collective-permute-start(bf16[64,1792]{1,0:T(8,128)(2,1)S(1)} %shard_map.115.hid_ref), channel_id=1, source_target_pairs={{0,8},{8,0},{16,24},{24,16},{1,9},{9,1},{17,25},{25,17},{2,10},{10... | collective-permute-start | bytes 688136 | tf_op jit(solution)/shard_map/ppermute | solution.py:24
  75.3 10.8 %collective-permute-start.26 = (bf16[64,1792]{1,0:T(8,128)(2,1)S(1)}, bf16[64,1792]{1,0:T(8,128)(2,1)S(1)}, u32[]{:S(2)}, u32[]{:S(2)}) collective-permute-start(bf16[64,1792]{1,0:T(8,128)(2,1)S(1)} %shard_map.122.hid_ref), channel_id=1, source_target_pairs={{0,8},{8,0},{16,24},{24,16},{1,9},{9,1},{17,25},{25,17},{2,10},{10... | collective-permute-start | bytes 688136 | tf_op jit(solution)/shard_map/ppermute | solution.py:24
  79.5 7.7 %collective-permute-start.20 = (bf16[64,1792]{1,0:T(8,128)(2,1)S(1)}, bf16[64,1792]{1,0:T(8,128)(2,1)S(1)}, u32[]{:S(2)}, u32[]{:S(2)}) collective-permute-start(bf16[64,1792]{1,0:T(8,128)(2,1)S(1)} %shard_map.118.hid_ref), channel_id=1, source_target_pairs={{0,8},{8,0},{16,24},{24,16},{1,9},{9,1},{17,25},{25,17},{2,10},{10... | collective-permute-start | bytes 688136 | tf_op jit(solution)/shard_map/ppermute | solution.py:24
  83.4 10.4 %collective-permute-start.12 = (bf16[2,2,8,1024]{3,2,1,0:T(8,128)(2,1)S(1)}, bf16[2,2,8,1024]{3,2,1,0:T(8,128)(2,1)S(1)}, u32[]{:S(2)}, u32[]{:S(2)}) collective-permute-start(bf16[2,2,8,1024]{3,2,1,0:T(8,128)(2,1)S(1)} %get-tuple-element.63), channel_id=1, source_target_pairs={{0,2},{1,3},{2,0},{3,1},{4,6},{5,7},{6,4},{7,5},{8,10},{9,11},{10,... | collective-permute-start | bytes 196616 | tf_op jit(solution)/shard_map/ppermute | solution.py:24
  84.3 16.3 %collective-permute-start.18 = (bf16[2,4,8,1024]{3,2,1,0:T(8,128)(2,1)S(1)}, bf16[2,4,8,1024]{3,2,1,0:T(8,128)(2,1)S(1)}, u32[]{:S(2)}, u32[]{:S(2)}) collective-permute-start(bf16[2,4,8,1024]{3,2,1,0:T(8,128)(2,1)S(1)} %get-tuple-element.72), channel_id=1, source_target_pairs={{0,1},{1,0},{2,3},{3,2},{4,5},{5,4},{6,7},{7,6},{8,9},{9,8},{10,11... | collective-permute-start | bytes 393224 | tf_op jit(solution)/shard_map/ppermute | solution.py:24
  86.8 13.7 %collective-permute-start.27 = (bf16[2,4,8,1024]{3,2,1,0:T(8,128)(2,1)S(1)}, bf16[2,4,8,1024]{3,2,1,0:T(8,128)(2,1)S(1)}, u32[]{:S(2)}, u32[]{:S(2)}) collective-permute-start(bf16[2,4,8,1024]{3,2,1,0:T(8,128)(2,1)S(1)} %get-tuple-element.86), channel_id=1, source_target_pairs={{0,1},{1,0},{2,3},{3,2},{4,5},{5,4},{6,7},{7,6},{8,9},{9,8},{10,11... | collective-permute-start | bytes 393224 | tf_op jit(solution)/shard_map/ppermute | solution.py:24
  88.0 12.7 %collective-permute-start.21 = (bf16[2,4,8,1024]{3,2,1,0:T(8,128)(2,1)S(1)}, bf16[2,4,8,1024]{3,2,1,0:T(8,128)(2,1)S(1)}, u32[]{:S(2)}, u32[]{:S(2)}) collective-permute-start(bf16[2,4,8,1024]{3,2,1,0:T(8,128)(2,1)S(1)} %get-tuple-element.77), channel_id=1, source_target_pairs={{0,1},{1,0},{2,3},{3,2},{4,5},{5,4},{6,7},{7,6},{8,9},{9,8},{10,11... | collective-permute-start | bytes 393224 | tf_op jit(solution)/shard_map/ppermute | solution.py:24
  89.7 8.4 %collective-permute-start.13 = (bf16[2,2,8,1024]{3,2,1,0:T(8,128)(2,1)S(1)}, bf16[2,2,8,1024]{3,2,1,0:T(8,128)(2,1)S(1)}, u32[]{:S(2)}, u32[]{:S(2)}) collective-permute-start(bf16[2,2,8,1024]{3,2,1,0:T(8,128)(2,1)S(1)} %get-tuple-element.64), channel_id=1, source_target_pairs={{0,4},{1,5},{2,6},{3,7},{4,0},{5,1},{6,2},{7,3},{8,12},{9,13},{10,... | collective-permute-start | bytes 196616 | tf_op jit(solution)/shard_map/ppermute | solution.py:24
  93.8 6.1 %collective-permute-start.14 = (bf16[2,2,8,1024]{3,2,1,0:T(8,128)(2,1)S(1)}, bf16[2,2,8,1024]{3,2,1,0:T(8,128)(2,1)S(1)}, u32[]{:S(2)}, u32[]{:S(2)}) collective-permute-start(bf16[2,2,8,1024]{3,2,1,0:T(8,128)(2,1)S(1)} %get-tuple-element.65), channel_id=1, source_target_pairs={{0,6},{1,7},{2,4},{3,5},{4,2},{5,3},{6,0},{7,1},{8,14},{9,15},{10,... | collective-permute-start | bytes 196616 | tf_op jit(solution)/shard_map/ppermute | solution.py:24
  99.9 5.3 %collective-permute-start.15 = (bf16[2,1,8,1024]{3,2,1,0:T(8,128)(2,1)S(1)}, bf16[2,1,8,1024]{3,2,1,0:T(8,128)(2,1)S(1)}, u32[]{:S(2)}, u32[]{:S(2)}) collective-permute-start(bf16[2,1,8,1024]{3,2,1,0:T(8,128)(2,1)S(1)} %get-tuple-element.67), channel_id=1, source_target_pairs={{0,1},{1,0},{2,3},{3,2},{4,5},{5,4},{6,7},{7,6},{8,9},{9,8},{10,11... | collective-permute-start | bytes 98312 | tf_op jit(solution)/shard_map/ppermute | solution.py:24
  100.5 5.7 %collective-permute-start.28 = (bf16[2,1,8,1024]{3,2,1,0:T(8,128)(2,1)S(1)}, bf16[2,1,8,1024]{3,2,1,0:T(8,128)(2,1)S(1)}, u32[]{:S(2)}, u32[]{:S(2)}) collective-permute-start(bf16[2,1,8,1024]{3,2,1,0:T(8,128)(2,1)S(1)} %get-tuple-element.88), channel_id=1, source_target_pairs={{0,2},{1,3},{2,0},{3,1},{4,6},{5,7},{6,4},{7,5},{8,10},{9,11},{10,... | collective-permute-start | bytes 98312 | tf_op jit(solution)/shard_map/ppermute | solution.py:24
  100.7 11.4 %collective-permute-start.22 = (bf16[2,1,16,1024]{3,2,1,0:T(8,128)(2,1)S(1)}, bf16[2,1,16,1024]{3,2,1,0:T(8,128)(2,1)S(1)}, u32[]{:S(2)}, u32[]{:S(2)}) collective-permute-start(bf16[2,1,16,1024]{3,2,1,0:T(8,128)(2,1)S(1)} %get-tuple-element.79), channel_id=1, source_target_pairs={{0,2},{1,3},{2,0},{3,1},{4,6},{5,7},{6,4},{7,5},{8,10},{9,11},{10,... | collective-permute-start | bytes 196616 | tf_op jit(solution)/shard_map/ppermute | solution.py:24
  102.7 9.3 %collective-permute-start.23 = (bf16[2,1,16,1024]{3,2,1,0:T(8,128)(2,1)S(1)}, bf16[2,1,16,1024]{3,2,1,0:T(8,128)(2,1)S(1)}, u32[]{:S(2)}, u32[]{:S(2)}) collective-permute-start(bf16[2,1,16,1024]{3,2,1,0:T(8,128)(2,1)S(1)} %get-tuple-element.80), channel_id=1, source_target_pairs={{0,4},{1,5},{2,6},{3,7},{4,0},{5,1},{6,2},{7,3},{8,12},{9,13},{10,... | collective-permute-start | bytes 196616 | tf_op jit(solution)/shard_map/ppermute | solution.py:24
  104.0 8.1 %collective-permute-start.24 = (bf16[2,1,16,1024]{3,2,1,0:T(8,128)(2,1)S(1)}, bf16[2,1,16,1024]{3,2,1,0:T(8,128)(2,1)S(1)}, u32[]{:S(2)}, u32[]{:S(2)}) collective-permute-start(bf16[2,1,16,1024]{3,2,1,0:T(8,128)(2,1)S(1)} %get-tuple-element.81), channel_id=1, source_target_pairs={{0,6},{1,7},{2,4},{3,5},{4,2},{5,3},{6,0},{7,1},{8,14},{9,15},{10,... | collective-permute-start | bytes 196616 | tf_op jit(solution)/shard_map/ppermute | solution.py:24
  105.2 6.9 %collective-permute-start.29 = (bf16[2,1,8,1024]{3,2,1,0:T(8,128)(2,1)S(1)}, bf16[2,1,8,1024]{3,2,1,0:T(8,128)(2,1)S(1)}, u32[]{:S(2)}, u32[]{:S(2)}) collective-permute-start(bf16[2,1,8,1024]{3,2,1,0:T(8,128)(2,1)S(1)} %get-tuple-element.89), channel_id=1, source_target_pairs={{0,4},{1,5},{2,6},{3,7},{4,0},{5,1},{6,2},{7,3},{8,12},{9,13},{10,... | collective-permute-start | bytes 98312 | tf_op jit(solution)/shard_map/ppermute | solution.py:24
  106.2 5.8 %collective-permute-start.30 = (bf16[2,1,8,1024]{3,2,1,0:T(8,128)(2,1)S(1)}, bf16[2,1,8,1024]{3,2,1,0:T(8,128)(2,1)S(1)}, u32[]{:S(2)}, u32[]{:S(2)}) collective-permute-start(bf16[2,1,8,1024]{3,2,1,0:T(8,128)(2,1)S(1)} %get-tuple-element.90), channel_id=1, source_target_pairs={{0,6},{1,7},{2,4},{3,5},{4,2},{5,3},{6,0},{7,1},{8,14},{9,15},{10,... | collective-permute-start | bytes 98312 | tf_op jit(solution)/shard_map/ppermute | solution.py:24

commit v5 on v4

--- a/solution.py
+++ b/solution.py
@@ -11,6 +11,7 @@
 
 F32 = jnp.float32
 BF16 = jnp.bfloat16
+ROW, COL = "row", "col"
 
 
 def plan(per_dest):
@@ -77,7 +78,7 @@
     hidden = gen_in_ref.shape[1]
     rank, rows = low_ref.shape
     half = rows // 2
-    core = lax.axis_index("row") & 1
+    core = lax.axis_index(ROW) & 1
     across_rows = (((0,), (0,)), ((), ()))
     for copy in copies[:3]:
         copy.wait()
@@ -105,7 +106,7 @@
             toks_ref[side * half + target : side * half + target + size, :] = rows_of(
                 tok_ref, begin, size
             )
-    x = toks_ref[:, pl.ds(pl.multiple_of(lax.axis_index("col") * slab, 128), slab)] if x_in is None else x_in[...]
+    x = toks_ref[:, pl.ds(pl.multiple_of(lax.axis_index(COL) * slab, 128), slab)] if x_in is None else x_in[...]
     xt = x.T
     copies[6].wait()
     part = hidden // 4
@@ -234,7 +235,7 @@
     member = member_ref[...].astype(F32)
     total = kept_ref[...] + got_ref[...].astype(F32)
     for which, factor in ((0, mine_ref), (1, peer_ref)):
-        first = (lax.axis_index("row") ^ which) * ranks
+        first = (lax.axis_index(ROW) ^ which) * ranks
         spread = jnp.concatenate(
             [
                 (member * low_ref[pl.ds(first + r, 1), :].astype(BF16).astype(F32)).astype(BF16)
@@ -291,9 +292,9 @@
 
 def split_rows(hid_ref, w_ref):
     acc = jnp.dot(hid_ref[...], w_ref[...], preferred_element_type=F32)
-    col = lax.axis_size("col")
+    col = lax.axis_size(COL)
     acc = acc.reshape(col // 2, 2, acc.shape[0] // col, acc.shape[1])
-    low_bit = (lax.axis_index("col") & 1) == 0
+    low_bit = (lax.axis_index(COL) & 1) == 0
     keep = jnp.where(low_bit, acc[:, 0], acc[:, 1])
     give = jnp.where(low_bit, acc[:, 1], acc[:, 0])
     return keep, give.astype(BF16)
@@ -309,7 +310,7 @@
 
 
 def down(hid, w):
-    col = lax.axis_size("col")
+    col = lax.axis_size(COL)
     shape = (col // 2, hid.shape[0] // col, w.shape[1])
     out = (jax.ShapeDtypeStruct(shape, F32), jax.ShapeDtypeStruct(shape, BF16))
     return in_vmem(down_kernel, out, hid, w)
@@ -322,9 +323,9 @@
 
 def turned_split(hid_ref, w_ref, scratch):
     acc = jnp.dot(hid_ref[...], w_ref[...], preferred_element_type=F32)
-    col = lax.axis_size("col")
+    col = lax.axis_size(COL)
     scratch[...] = acc.reshape(col // 2, 2, acc.shape[0] // col, acc.shape[1])
-    here = lax.axis_index("col") >> 1
+    here = lax.axis_index(COL) >> 1
     return [scratch[pl.ds(here ^ q, 1)][0] for q in range(4)]
 
 
@@ -340,7 +341,7 @@
 
 
 def turned_down(hid, w, own):
-    col = lax.axis_size("col")
+    col = lax.axis_size(COL)
     shape = (2, hid.shape[0] // col, w.shape[1])
     scratch = [pltpu.VMEM((col // 2,) + shape, F32)]
     lead = () if own is None else (2,)
@@ -350,7 +351,7 @@
 
 
 def turned_fold_kernel(total_ref, *refs):
-    side = lax.axis_index("col") & 1
+    side = lax.axis_index(COL) & 1
     for ref, which in ((refs[3], side), (refs[4], 1 - side)):
         at = pl.ds(which, 1)
         value = total_ref[:, at]
@@ -367,7 +368,7 @@
 
 def fold_kernel(bit, keep_ref, got_ref, new_ref, give_ref):
     parts = keep_ref.shape[1]
-    side = (lax.axis_index("col") >> bit) & 1
+    side = (lax.axis_index(COL) >> bit) & 1
     for j in range(parts // 2):
         for ref, which in ((new_ref, side), (give_ref, 1 - side)):
             at = pl.ds(2 * j + which, 1)
@@ -381,7 +382,7 @@
 
 
 def last_kernel(bit, count, *refs):
-    here = lax.axis_index("col") >> bit
+    here = lax.axis_index(COL) >> bit
     start = 0
     for k in range(count):
         keep_ref, got_ref = refs[2 * k : 2 * k + 2]
@@ -403,7 +404,7 @@
 def join_kernel(counts, *refs):
     out_ref = refs[-1]
     requests, draft, width = out_ref.shape
-    core = lax.axis_index("row") & 1
+    core = lax.axis_index(ROW) & 1
     start = 0
     for count in counts:
         (total, *got), refs = refs[:count], refs[count:]
@@ -436,8 +437,8 @@
 def shards(tokens, task_emb, gen_in, gen_a, gen_b, w_gate, w_up, w_down, group_count, group_task):
     batch, draft, _ = tokens.shape
     rows = batch * draft
-    rn, cn = lax.axis_size("row"), lax.axis_size("col")
-    ri, ci = lax.axis_index("row"), lax.axis_index("col")
+    rn, cn = lax.axis_size(ROW), lax.axis_size(COL)
+    ri, ci = lax.axis_index(ROW), lax.axis_index(COL)
     core = ri & 1
     rmasks, cmasks = masks_of(rn), masks_of(cn)
     slab = gen_a.shape[1]
@@ -480,15 +481,15 @@
         w_gate,
         x,
     )
-    gate_got = swap(gate_sent, "row", 1)
+    gate_got = swap(gate_sent, ROW, 1)
     for m in rmasks[1:]:
-        low = low + swap(low, "row", m)
+        low = low + swap(low, ROW, m)
     gate_sum = (gate_kept + gate_got.astype(F32)).astype(BF16)
 
     def others(sent):
         total = None
         for s, m in enumerate(rmasks[1:]):
-            got = swap(sent, "row", m)
+            got = swap(sent, ROW, m)
             if s + 2 == len(rmasks) and total is None:
                 return got
             total = got.astype(F32) if total is None else total + got.astype(F32)
@@ -498,14 +499,14 @@
     gate_rest = others(gate_sum)
 
     up_kept, up_sent = split_matmul(toks, w_up)
-    up_got = swap(up_sent, "row", 1)
+    up_got = swap(up_sent, ROW, 1)
     b_mine = factors(hyper, gen_b)
-    b_peer = swap(b_mine, "row", 1)
+    b_peer = swap(b_mine, ROW, 1)
     for m in cmasks[:-2]:
-        low = low + swap(low, "col", m)
-    gots = [swap(low, "col", q * cmasks[-2]) for q in (1, 2, 3)]
+        low = low + swap(low, COL, m)
+    gots = [swap(low, COL, q * cmasks[-2]) for q in (1, 2, 3)]
     low = low + gots[0] + gots[1] + gots[2]
-    low = low[:, : rows // 2] + swap(low[:, rows // 2 :], "row", 1)
+    low = low[:, : rows // 2] + swap(low[:, rows // 2 :], ROW, 1)
 
     up_half, *up_sums = add_adapter(
         tuple(pieces), low, own_member, b_mine, b_peer, up_kept, up_got
@@ -516,18 +517,18 @@
     for k, piece in enumerate(pieces):
         up_rest = others(up_sums[k])
         hid = hidden_units(piece, act, up_half, up_rest)
-        other = swap(hid, "row", 1)
+        other = swap(hid, ROW, 1)
         if k == 0 and turned:
             own = turned_down(hid, w_down, None)
             total, *gives = turned_down(other, w_down, own)
-            gots = [swap(give, "col", (q + 1) << 1) for q, give in enumerate(gives)]
+            gots = [swap(give, COL, (q + 1) << 1) for q, give in enumerate(gives)]
             keep, give = turned_fold(total, gots)
-            first = [keep, swap(give, "col", 1)]
+            first = [keep, swap(give, COL, 1)]
             outs.append(None)
             continue
         keep, give = cross(other, w_down, down(hid, w_down))
         for s, m in enumerate(cmasks[:-2]):
-            got = swap(give, "col", m)
+            got = swap(give, COL, m)
             if s + 3 < len(cmasks):
                 keep, give = fold(s + 1, keep, got)
         outs.append((keep, got))
@@ -535,24 +536,24 @@
     parts = [first] if turned else []
     for members in joint:
         total, *gives = last_split(low_bit, [outs[k] for k in members])
-        gots = [swap(give, "col", (q + 1) << low_bit) for q, give in enumerate(gives)]
+        gots = [swap(give, COL, (q + 1) << low_bit) for q, give in enumerate(gives)]
         parts.append([total] + gots)
     return join(parts, jax.ShapeDtypeStruct((batch // cn, draft, w_down.shape[1]), BF16))
 
 
 def solution(mesh):
     in_specs = (
-        P(None, None, "row"),
+        P(None, None, ROW),
         P(),
         P(),
-        P(None, ("row", "col"), None),
-        P(None, "row", "col"),
-        P("row", "col"),
-        P("row", "col"),
-        P("col", "row"),
+        P(None, (ROW, COL), None),
+        P(None, ROW, COL),
+        P(ROW, COL),
+        P(ROW, COL),
+        P(COL, ROW),
         P(),
         P(),
     )
-    out_specs = P("col", None, "row")
+    out_specs = P(COL, None, ROW)
 
     return jax.shard_map(shards, mesh=mesh, in_specs=in_specs, out_specs=out_specs, check_vma=False)

time: 113 us -> 113 us (level)
  no operation moved by 1% of the time
where the time goes in v5:
time: 113 us
  waiting for transfers between devices  57.4 us (51%)
  starting transfers between devices  30.9 us (27%)
  Pallas kernels  24 us (21%)
    ppermute x31, waiting for transfers between devices, swap(): return lax.ppermute(x, axis, [(i, i ^ mask) for i in range(n)])  57.4 us
    ppermute x31, starting transfers between devices, swap(): return lax.ppermute(x, axis, [(i, i ^ mask) for i in range(n)])  30.9 us
    pallas_call x1, Pallas kernels, low_part(): pl.pallas_call(functools.partial(low_kernel, blocks, slab, shift), in_spe...  7.99 us
    pallas_call x17, Pallas kernels, in_vmem(): pl.pallas_call(kernel, in_specs=[vmem] * len(args), out_specs=jax.tree.ma...  7.71 us
    pallas_call x1, Pallas kernels, factors(): pl.pallas_call(factor_kernel, grid=(ff // tile,), in_specs=[pl.BlockSpec(...  3.55 us
    pallas_call x1, Pallas kernels, split_matmul(): pl.pallas_call(split_kernel, grid=(ff // tile,), in_specs=[pl.BlockSpec((...  3.01 us
  transfers between devices with their start and end apart: 31, of which 13 were waited for; matrix products, arithmetic and copies ran while one was open for 0% of the time, Pallas kernels for 14%

profile of v5, /device:TPU:0, one launch (start us, length us, event | category | flops | bytes accessed | tf_op | source)
XLA Modules:
  0.0 112.8 jit_solution(15104823837142400866)
XLA Ops:
  0.0 8.0 %low_part.1 = (f32[16,512]{1,0:T(8,128)S(1)}, bf16[64,512]{1,0:T(8,128)(2,1)S(1)}, bf16[64,256]{1,0:T(8,128)(2,1)S(1)}, bf16[512,1024]{1,0:T(8,128)(2,1)S(1)}, f...) custom-call(s32[1,64]{1,0:T(1,128)} %bitcast.6, s32[1,64]{1,0:T(1,128)} %bitcast.7, ...), custom_call_target="tpu_custom_call" | custom-call | tf_op jit(solution)/shard_map/low_part/pallas_call | solution.py:141
  8.0 0.6 collective-permute-start
  8.6 3.5 %factors.1.mine_ref = bf16[256,1792]{1,0:T(8,128)(2,1)S(1)} custom-call(bf16[64,512]{1,0:T(8,128)(2,1)S(1)} %get-tuple-element.52.hyper_ref, bf16[512,4,1792]{2,1,0:T(4,128)(2,1)S(1)} %copy-done.1), custom_call_target="tpu_custom_call" | custom-call | tf_op jit(solution)/shard_map/factors/pallas_call | solution.py:217
  12.2 3.0 %shard_map.110 = (f32[256,1792]{1,0:T(8,128)S(1)}, bf16[256,1792]{1,0:T(8,128)(2,1)S(1)}) custom-call(bf16[512,1024]{1,0:T(8,128)(2,1)S(1)} %get-tuple-element.53.x_ref, bf16[1024,1792]{1,0:T(8,128)(2,1)S(1)} %copy-done.2), custom_call_target="tpu_custom_call" | custom-call | tf_op jit(solution)/shard_map/pallas_call | solution.py:168
  15.2 0.5 collective-permute-start.9
  15.8 0.2 add_convert_fusion
  15.9 2.6 %collective-permute-start.1 = (bf16[256,1792]{1,0:T(8,128)(2,1)S(1)}, bf16[256,1792]{1,0:T(8,128)(2,1)S(1)}, u32[]{:S(2)}, u32[]{:S(2)}) collective-permute-start(bf16[256,1792]{1,0:T(8,128)(2,1)S(1)} %add_convert_fusion), channel_id=1, source_target_pairs={{0,16},{8,24},{16,0},{24,8},{1,17},{9,25},{17,1},{25,9},{2,18},{10... | collective-permute-start | bytes 2752520 | tf_op jit(solution)/shard_map/ppermute | solution.py:25
  18.6 21.6 %collective-permute-done.2 = f32[16,512]{1,0:T(8,128)S(1)} collective-permute-done((f32[16,512]{1,0:T(8,128)S(1)}, f32[16,512]{1,0:T(8,128)S(1)}, u32[]{:S(2)}, u32[]{:S(2)}) %collective-permute-start.2) | collective-permute-done | bytes 32800 | tf_op jit(solution)/shard_map/ppermute | solution.py:25
  40.2 1.7 %collective-permute-start.3 = (f32[16,512]{1,0:T(8,128)S(1)}, f32[16,512]{1,0:T(8,128)S(1)}, u32[]{:S(2)}, u32[]{:S(2)}) collective-permute-start(f32[16,512]{1,0:T(8,128)S(1)} %add.22), channel_id=1, source_target_pairs={{0,1},{1,0},{2,3},{3,2},{4,5},{5,4},{6,7},{7,6},{8,9},{9,8},{10,11... | collective-permute-start | bytes 98312 | tf_op jit(solution)/shard_map/ppermute | solution.py:25
  42.0 2.2 %collective-permute-done.3 = f32[16,512]{1,0:T(8,128)S(1)} collective-permute-done((f32[16,512]{1,0:T(8,128)S(1)}, f32[16,512]{1,0:T(8,128)S(1)}, u32[]{:S(2)}, u32[]{:S(2)}) %collective-permute-start.3) | collective-permute-done | bytes 32800 | tf_op jit(solution)/shard_map/ppermute | solution.py:25
  44.2 3.8 %collective-permute-start.6 = (f32[16,512]{1,0:T(8,128)S(1)}, f32[16,512]{1,0:T(8,128)S(1)}, u32[]{:S(2)}, u32[]{:S(2)}) collective-permute-start(f32[16,512]{1,0:T(8,128)S(1)} %add.23), channel_id=1, source_target_pairs={{0,6},{1,7},{2,4},{3,5},{4,2},{5,3},{6,0},{7,1},{8,14},{9,15},{10,... | collective-permute-start | bytes 98312 | tf_op jit(solution)/shard_map/ppermute | solution.py:25
  48.0 1.9 %collective-permute-done.6 = f32[16,512]{1,0:T(8,128)S(1)} collective-permute-done((f32[16,512]{1,0:T(8,128)S(1)}, f32[16,512]{1,0:T(8,128)S(1)}, u32[]{:S(2)}, u32[]{:S(2)}) %collective-permute-start.6) | collective-permute-done | bytes 32800 | tf_op jit(solution)/shard_map/ppermute | solution.py:25
  49.9 2.9 %collective-permute-done.5 = f32[16,512]{1,0:T(8,128)S(1)} collective-permute-done((f32[16,512]{1,0:T(8,128)S(1)}, f32[16,512]{1,0:T(8,128)S(1)}, u32[]{:S(2)}, u32[]{:S(2)}) %collective-permute-start.5) | collective-permute-done | bytes 32800 | tf_op jit(solution)/shard_map/ppermute | solution.py:25
  52.8 1.0 collective-permute-done.4
  53.9 1.2 %collective-permute-done.7 = f32[16,256]{1,0:T(8,128)S(1)} collective-permute-done((f32[16,256]{1,0:T(8,128)S(1)}, f32[16,256]{1,0:T(8,128)S(1)}, u32[]{:S(2)}, u32[]{:S(2)}) %collective-permute-start.7) | collective-permute-done | bytes 16416 | tf_op jit(solution)/shard_map/ppermute | solution.py:25
  55.1 1.8 %adapter.1 = (f32[256,1792]{1,0:T(8,128)S(1)}, bf16[64,1792]{1,0:T(8,128)(2,1)S(1)}, bf16[64,1792]{1,0:T(8,128)(2,1)S(1)}, bf16[64,1792]{1,0:T(8,128)(2,1)S(1)}, bf16[64,1792]{1,0:T(8,128)(2,1)S(1)}) custom-call(f32[16,256]{1,0:T(8,128)S(1)} %slice_add_fusion.low_ref, bf16[64,256]{1,0:T(8,128)(2,1)S(1)} %get-tuple-element.51.member_ref, ...), custom_call_target="tpu_custom_call" | custom-call | tf_op jit(solution)/shard_map/adapter/pallas_call | solution.py:260
  56.9 1.9 %collective-permute-start.10 = (bf16[64,1792]{1,0:T(8,128)(2,1)S(1)}, bf16[64,1792]{1,0:T(8,128)(2,1)S(1)}, u32[]{:S(2)}, u32[]{:S(2)}) collective-permute-start(bf16[64,1792]{1,0:T(8,128)(2,1)S(1)} %get-tuple-element.57), channel_id=1, source_target_pairs={{0,16},{8,24},{16,0},{24,8},{1,17},{9,25},{17,1},{25,9},{2,18},{10... | collective-permute-start | bytes 688136 | tf_op jit(solution)/shard_map/ppermute | solution.py:25
  58.8 0.2 collective-permute-start.16
  59.0 1.8 %collective-permute-start.25 = (bf16[64,1792]{1,0:T(8,128)(2,1)S(1)}, bf16[64,1792]{1,0:T(8,128)(2,1)S(1)}, u32[]{:S(2)}, u32[]{:S(2)}) collective-permute-start(bf16[64,1792]{1,0:T(8,128)(2,1)S(1)} %get-tuple-element.82), channel_id=1, source_target_pairs={{0,16},{8,24},{16,0},{24,8},{1,17},{9,25},{17,1},{25,9},{2,18},{10... | collective-permute-start | bytes 688136 | tf_op jit(solution)/shard_map/ppermute | solution.py:25
  60.8 0.2 collective-permute-start.19
  61.0 0.6 shard_map.109.act_ref
  61.6 3.8 %collective-permute-done.10.up_ref = bf16[64,1792]{1,0:T(8,128)(2,1)S(1)} collective-permute-done((bf16[64,1792]{1,0:T(8,128)(2,1)S(1)}, bf16[64,1792]{1,0:T(8,128)(2,1)S(1)}, u32[]{:S(2)}, u32[]{:S(2)}) %collective-permute-start.10) | collective-permute-done | bytes 229408 | tf_op jit(solution)/shard_map/ppermute | solution.py:25
  65.6 4.8 %collective-permute-done.16.up_ref = bf16[64,1792]{1,0:T(8,128)(2,1)S(1)} collective-permute-done((bf16[64,1792]{1,0:T(8,128)(2,1)S(1)}, bf16[64,1792]{1,0:T(8,128)(2,1)S(1)}, u32[]{:S(2)}, u32[]{:S(2)}) %collective-permute-start.16) | collective-permute-done | bytes 229408 | tf_op jit(solution)/shard_map/ppermute | solution.py:25
  70.5 4.8 %collective-permute-done.25.up_ref = bf16[64,1792]{1,0:T(8,128)(2,1)S(1)} collective-permute-done((bf16[64,1792]{1,0:T(8,128)(2,1)S(1)}, bf16[64,1792]{1,0:T(8,128)(2,1)S(1)}, u32[]{:S(2)}, u32[]{:S(2)}) %collective-permute-start.25) | collective-permute-done | bytes 229408 | tf_op jit(solution)/shard_map/ppermute | solution.py:25
  75.4 4.1 %collective-permute-done.19.up_ref = bf16[64,1792]{1,0:T(8,128)(2,1)S(1)} collective-permute-done((bf16[64,1792]{1,0:T(8,128)(2,1)S(1)}, bf16[64,1792]{1,0:T(8,128)(2,1)S(1)}, u32[]{:S(2)}, u32[]{:S(2)}) %collective-permute-start.19) | collective-permute-done | bytes 229408 | tf_op jit(solution)/shard_map/ppermute | solution.py:25
  79.6 0.8 shard_map.112
  80.4 0.8 shard_map.116
  81.1 0.8 shard_map.119
  81.9 0.8 shard_map.123
  82.7 0.8 shard_map.113
  83.5 0.8 shard_map.117
  84.3 1.8 %collective-permute-start.18 = (bf16[2,4,8,1024]{3,2,1,0:T(8,128)(2,1)S(1)}, bf16[2,4,8,1024]{3,2,1,0:T(8,128)(2,1)S(1)}, u32[]{:S(2)}, u32[]{:S(2)}) collective-permute-start(bf16[2,4,8,1024]{3,2,1,0:T(8,128)(2,1)S(1)} %get-tuple-element.72), channel_id=1, source_target_pairs={{0,1},{1,0},{2,3},{3,2},{4,5},{5,4},{6,7},{7,6},{8,9},{9,8},{10,11... | collective-permute-start | bytes 393224 | tf_op jit(solution)/shard_map/ppermute | solution.py:25
  86.1 0.8 shard_map.124
  86.8 0.4 collective-permute-start.27
  87.2 0.8 shard_map.120
  88.0 1.8 %collective-permute-start.21 = (bf16[2,4,8,1024]{3,2,1,0:T(8,128)(2,1)S(1)}, bf16[2,4,8,1024]{3,2,1,0:T(8,128)(2,1)S(1)}, u32[]{:S(2)}, u32[]{:S(2)}) collective-permute-start(bf16[2,4,8,1024]{3,2,1,0:T(8,128)(2,1)S(1)} %get-tuple-element.77), channel_id=1, source_target_pairs={{0,1},{1,0},{2,3},{3,2},{4,5},{5,4},{6,7},{7,6},{8,9},{9,8},{10,11... | collective-permute-start | bytes 393224 | tf_op jit(solution)/shard_map/ppermute | solution.py:25
  89.7 4.0 %collective-permute-start.13 = (bf16[2,2,8,1024]{3,2,1,0:T(8,128)(2,1)S(1)}, bf16[2,2,8,1024]{3,2,1,0:T(8,128)(2,1)S(1)}, u32[]{:S(2)}, u32[]{:S(2)}) collective-permute-start(bf16[2,2,8,1024]{3,2,1,0:T(8,128)(2,1)S(1)} %get-tuple-element.64), channel_id=1, source_target_pairs={{0,4},{1,5},{2,6},{3,7},{4,0},{5,1},{6,2},{7,3},{8,12},{9,13},{10,... | collective-permute-start | bytes 196616 | tf_op jit(solution)/shard_map/ppermute | solution.py:25
  93.8 0.3 collective-permute-start.14
  94.1 4.0 %collective-permute-done.13.refs_1_ = bf16[2,2,8,1024]{3,2,1,0:T(8,128)(2,1)S(1)} collective-permute-done((bf16[2,2,8,1024]{3,2,1,0:T(8,128)(2,1)S(1)}, bf16[2,2,8,1024]{3,2,1,0:T(8,128)(2,1)S(1)}, u32[]{:S(2)}, u32[]{:S(2)}) %collective-permute-start.13) | collective-permute-done | bytes 65568 | tf_op jit(solution)/shard_map/ppermute | solution.py:25
  98.1 1.7 %collective-permute-done.14.refs_2_ = bf16[2,2,8,1024]{3,2,1,0:T(8,128)(2,1)S(1)} collective-permute-done((bf16[2,2,8,1024]{3,2,1,0:T(8,128)(2,1)S(1)}, bf16[2,2,8,1024]{3,2,1,0:T(8,128)(2,1)S(1)}, u32[]{:S(2)}, u32[]{:S(2)}) %collective-permute-start.14) | collective-permute-done | bytes 65568 | tf_op jit(solution)/shard_map/ppermute | solution.py:25
  99.9 0.6 collective-permute-start.15
  100.7 2.0 %collective-permute-start.22 = (bf16[2,1,16,1024]{3,2,1,0:T(8,128)(2,1)S(1)}, bf16[2,1,16,1024]{3,2,1,0:T(8,128)(2,1)S(1)}, u32[]{:S(2)}, u32[]{:S(2)}) collective-permute-start(bf16[2,1,16,1024]{3,2,1,0:T(8,128)(2,1)S(1)} %get-tuple-element.79), channel_id=1, source_target_pairs={{0,2},{1,3},{2,0},{3,1},{4,6},{5,7},{6,4},{7,5},{8,10},{9,11},{10,... | collective-permute-start | bytes 196616 | tf_op jit(solution)/shard_map/ppermute | solution.py:25
  102.7 1.3 %collective-permute-start.23 = (bf16[2,1,16,1024]{3,2,1,0:T(8,128)(2,1)S(1)}, bf16[2,1,16,1024]{3,2,1,0:T(8,128)(2,1)S(1)}, u32[]{:S(2)}, u32[]{:S(2)}) collective-permute-start(bf16[2,1,16,1024]{3,2,1,0:T(8,128)(2,1)S(1)} %get-tuple-element.80), channel_id=1, source_target_pairs={{0,4},{1,5},{2,6},{3,7},{4,0},{5,1},{6,2},{7,3},{8,12},{9,13},{10,... | collective-permute-start | bytes 196616 | tf_op jit(solution)/shard_map/ppermute | solution.py:25
  104.0 1.2 %collective-permute-start.24 = (bf16[2,1,16,1024]{3,2,1,0:T(8,128)(2,1)S(1)}, bf16[2,1,16,1024]{3,2,1,0:T(8,128)(2,1)S(1)}, u32[]{:S(2)}, u32[]{:S(2)}) collective-permute-start(bf16[2,1,16,1024]{3,2,1,0:T(8,128)(2,1)S(1)} %get-tuple-element.81), channel_id=1, source_target_pairs={{0,6},{1,7},{2,4},{3,5},{4,2},{5,3},{6,0},{7,1},{8,14},{9,15},{10,... | collective-permute-start | bytes 196616 | tf_op jit(solution)/shard_map/ppermute | solution.py:25
  105.2 1.0 collective-permute-start.29
  106.2 2.4 %collective-permute-start.30 = (bf16[2,1,8,1024]{3,2,1,0:T(8,128)(2,1)S(1)}, bf16[2,1,8,1024]{3,2,1,0:T(8,128)(2,1)S(1)}, u32[]{:S(2)}, u32[]{:S(2)}) collective-permute-start(bf16[2,1,8,1024]{3,2,1,0:T(8,128)(2,1)S(1)} %get-tuple-element.90), channel_id=1, source_target_pairs={{0,6},{1,7},{2,4},{3,5},{4,2},{5,3},{6,0},{7,1},{8,14},{9,15},{10,... | collective-permute-start | bytes 98312 | tf_op jit(solution)/shard_map/ppermute | solution.py:25
  108.6 3.5 %collective-permute-done.29.refs_8_ = bf16[2,1,8,1024]{3,2,1,0:T(8,128)(2,1)S(1)} collective-permute-done((bf16[2,1,8,1024]{3,2,1,0:T(8,128)(2,1)S(1)}, bf16[2,1,8,1024]{3,2,1,0:T(8,128)(2,1)S(1)}, u32[]{:S(2)}, u32[]{:S(2)}) %collective-permute-start.29) | collective-permute-done | bytes 32800 | tf_op jit(solution)/shard_map/ppermute | solution.py:25
  112.1 0.7 shard_map.126
  (47 shorter events, 1.1 us)
Async XLA Ops:
  0.0 8.6 %copy-start.1 = (bf16[512,4,1792]{2,1,0:T(4,128)(2,1)S(1)}, bf16[512,4,1792]{2,1,0:T(4,128)(2,1)}, u32[]{:S(2)}) copy-start(bf16[512,4,1792]{2,1,0:T(4,128)(2,1)} %gen_ref.1) | copy-start | bytes 22020100
  8.0 7.8 %collective-permute-start = (bf16[256,1792]{1,0:T(8,128)(2,1)S(1)}, bf16[256,1792]{1,0:T(8,128)(2,1)S(1)}, u32[]{:S(2)}, u32[]{:S(2)}) collective-permute-start(bf16[256,1792]{1,0:T(8,128)(2,1)S(1)} %get-tuple-element.49), channel_id=1, source_target_pairs={{0,8},{8,0},{16,24},{24,16},{1,9},{9,1},{17,25},{25,17},{2,10},{10... | collective-permute-start | bytes 2752520 | tf_op jit(solution)/shard_map/ppermute | solution.py:25
  8.6 3.7 %copy-start.2 = (bf16[1024,1792]{1,0:T(8,128)(2,1)S(1)}, bf16[1024,1792]{1,0:T(8,128)(2,1)}, u32[]{:S(2)}) copy-start(bf16[1024,1792]{1,0:T(8,128)(2,1)} %w_ref.9) | copy-start | bytes 11010052
  12.1 43.0 %collective-permute-start.8 = (bf16[256,1792]{1,0:T(8,128)(2,1)S(1)}, bf16[256,1792]{1,0:T(8,128)(2,1)S(1)}, u32[]{:S(2)}, u32[]{:S(2)}) collective-permute-start(bf16[256,1792]{1,0:T(8,128)(2,1)S(1)} %factors.1.mine_ref), channel_id=1, source_target_pairs={{0,8},{8,0},{16,24},{24,16},{1,9},{9,1},{17,25},{25,17},{2,10},{10... | collective-permute-start | bytes 2752520 | tf_op jit(solution)/shard_map/ppermute | solution.py:25
  15.2 39.9 %collective-permute-start.9 = (bf16[256,1792]{1,0:T(8,128)(2,1)S(1)}, bf16[256,1792]{1,0:T(8,128)(2,1)S(1)}, u32[]{:S(2)}, u32[]{:S(2)}) collective-permute-start(bf16[256,1792]{1,0:T(8,128)(2,1)S(1)} %get-tuple-element.55), channel_id=1, source_target_pairs={{0,8},{8,0},{16,24},{24,16},{1,9},{9,1},{17,25},{25,17},{2,10},{10... | collective-permute-start | bytes 2752520 | tf_op jit(solution)/shard_map/ppermute | solution.py:25
  15.9 45.1 %collective-permute-start.1 = (bf16[256,1792]{1,0:T(8,128)(2,1)S(1)}, bf16[256,1792]{1,0:T(8,128)(2,1)S(1)}, u32[]{:S(2)}, u32[]{:S(2)}) collective-permute-start(bf16[256,1792]{1,0:T(8,128)(2,1)S(1)} %add_convert_fusion), channel_id=1, source_target_pairs={{0,16},{8,24},{16,0},{24,8},{1,17},{9,25},{17,1},{25,9},{2,18},{10... | collective-permute-start | bytes 2752520 | tf_op jit(solution)/shard_map/ppermute | solution.py:25
  18.5 21.7 %collective-permute-start.2 = (f32[16,512]{1,0:T(8,128)S(1)}, f32[16,512]{1,0:T(8,128)S(1)}, u32[]{:S(2)}, u32[]{:S(2)}) collective-permute-start(f32[16,512]{1,0:T(8,128)S(1)} %get-tuple-element.50), channel_id=1, source_target_pairs={{0,16},{8,24},{16,0},{24,8},{1,17},{9,25},{17,1},{25,9},{2,18},{10... | collective-permute-start | bytes 98312 | tf_op jit(solution)/shard_map/ppermute | solution.py:25
  40.2 3.9 %collective-permute-start.3 = (f32[16,512]{1,0:T(8,128)S(1)}, f32[16,512]{1,0:T(8,128)S(1)}, u32[]{:S(2)}, u32[]{:S(2)}) collective-permute-start(f32[16,512]{1,0:T(8,128)S(1)} %add.22), channel_id=1, source_target_pairs={{0,1},{1,0},{2,3},{3,2},{4,5},{5,4},{6,7},{7,6},{8,9},{9,8},{10,11... | collective-permute-start | bytes 98312 | tf_op jit(solution)/shard_map/ppermute | solution.py:25
  44.2 5.7 %collective-permute-start.6 = (f32[16,512]{1,0:T(8,128)S(1)}, f32[16,512]{1,0:T(8,128)S(1)}, u32[]{:S(2)}, u32[]{:S(2)}) collective-permute-start(f32[16,512]{1,0:T(8,128)S(1)} %add.23), channel_id=1, source_target_pairs={{0,6},{1,7},{2,4},{3,5},{4,2},{5,3},{6,0},{7,1},{8,14},{9,15},{10,... | collective-permute-start | bytes 98312 | tf_op jit(solution)/shard_map/ppermute | solution.py:25
  48.0 4.8 %collective-permute-start.5 = (f32[16,512]{1,0:T(8,128)S(1)}, f32[16,512]{1,0:T(8,128)S(1)}, u32[]{:S(2)}, u32[]{:S(2)}) collective-permute-start(f32[16,512]{1,0:T(8,128)S(1)} %add.23), channel_id=1, source_target_pairs={{0,4},{1,5},{2,6},{3,7},{4,0},{5,1},{6,2},{7,3},{8,12},{9,13},{10,... | collective-permute-start | bytes 98312 | tf_op jit(solution)/shard_map/ppermute | solution.py:25
  49.9 3.9 %collective-permute-start.4 = (f32[16,512]{1,0:T(8,128)S(1)}, f32[16,512]{1,0:T(8,128)S(1)}, u32[]{:S(2)}, u32[]{:S(2)}) collective-permute-start(f32[16,512]{1,0:T(8,128)S(1)} %add.23), channel_id=1, source_target_pairs={{0,2},{1,3},{2,0},{3,1},{4,6},{5,7},{6,4},{7,5},{8,10},{9,11},{10,... | collective-permute-start | bytes 98312 | tf_op jit(solution)/shard_map/ppermute | solution.py:25
  53.8 1.2 %collective-permute-start.7 = (f32[16,256]{1,0:T(8,128)S(1)}, f32[16,256]{1,0:T(8,128)S(1)}, u32[]{:S(2)}, u32[]{:S(2)}) collective-permute-start(f32[16,256]{1,0:T(8,128)S(1)} %slice.9), channel_id=1, source_target_pairs={{0,8},{8,0},{16,24},{24,16},{1,9},{9,1},{17,25},{25,17},{2,10},{10... | collective-permute-start | bytes 49160 | tf_op jit(solution)/shard_map/ppermute | solution.py:25
  55.1 5.9 %copy-start = (bf16[1792,1024]{1,0:T(8,128)(2,1)S(1)}, bf16[1792,1024]{1,0:T(8,128)(2,1)}, u32[]{:S(2)}) copy-start(bf16[1792,1024]{1,0:T(8,128)(2,1)} %w_ref.17) | copy-start | bytes 11010052
  56.9 8.5 %collective-permute-start.10 = (bf16[64,1792]{1,0:T(8,128)(2,1)S(1)}, bf16[64,1792]{1,0:T(8,128)(2,1)S(1)}, u32[]{:S(2)}, u32[]{:S(2)}) collective-permute-start(bf16[64,1792]{1,0:T(8,128)(2,1)S(1)} %get-tuple-element.57), channel_id=1, source_target_pairs={{0,16},{8,24},{16,0},{24,8},{1,17},{9,25},{17,1},{25,9},{2,18},{10... | collective-permute-start | bytes 688136 | tf_op jit(solution)/shard_map/ppermute | solution.py:25
  58.8 11.6 %collective-permute-start.16 = (bf16[64,1792]{1,0:T(8,128)(2,1)S(1)}, bf16[64,1792]{1,0:T(8,128)(2,1)S(1)}, u32[]{:S(2)}, u32[]{:S(2)}) collective-permute-start(bf16[64,1792]{1,0:T(8,128)(2,1)S(1)} %get-tuple-element.68), channel_id=1, source_target_pairs={{0,16},{8,24},{16,0},{24,8},{1,17},{9,25},{17,1},{25,9},{2,18},{10... | collective-permute-start | bytes 688136 | tf_op jit(solution)/shard_map/ppermute | solution.py:25
  59.0 16.3 %collective-permute-start.25 = (bf16[64,1792]{1,0:T(8,128)(2,1)S(1)}, bf16[64,1792]{1,0:T(8,128)(2,1)S(1)}, u32[]{:S(2)}, u32[]{:S(2)}) collective-permute-start(bf16[64,1792]{1,0:T(8,128)(2,1)S(1)} %get-tuple-element.82), channel_id=1, source_target_pairs={{0,16},{8,24},{16,0},{24,8},{1,17},{9,25},{17,1},{25,9},{2,18},{10... | collective-permute-start | bytes 688136 | tf_op jit(solution)/shard_map/ppermute | solution.py:25
  60.8 18.7 %collective-permute-start.19 = (bf16[64,1792]{1,0:T(8,128)(2,1)S(1)}, bf16[64,1792]{1,0:T(8,128)(2,1)S(1)}, u32[]{:S(2)}, u32[]{:S(2)}) collective-permute-start(bf16[64,1792]{1,0:T(8,128)(2,1)S(1)} %get-tuple-element.73), channel_id=1, source_target_pairs={{0,16},{8,24},{16,0},{24,8},{1,17},{9,25},{17,1},{25,9},{2,18},{10... | collective-permute-start | bytes 688136 | tf_op jit(solution)/shard_map/ppermute | solution.py:25
  65.5 17.2 %collective-permute-start.11 = (bf16[64,1792]{1,0:T(8,128)(2,1)S(1)}, bf16[64,1792]{1,0:T(8,128)(2,1)S(1)}, u32[]{:S(2)}, u32[]{:S(2)}) collective-permute-start(bf16[64,1792]{1,0:T(8,128)(2,1)S(1)} %shard_map.111.hid_ref), channel_id=1, source_target_pairs={{0,8},{8,0},{16,24},{24,16},{1,9},{9,1},{17,25},{25,17},{2,10},{10... | collective-permute-start | bytes 688136 | tf_op jit(solution)/shard_map/ppermute | solution.py:25
  70.4 13.1 %collective-permute-start.17 = (bf16[64,1792]{1,0:T(8,128)(2,1)S(1)}, bf16[64,1792]{1,0:T(8,128)(2,1)S(1)}, u32[]{:S(2)}, u32[]{:S(2)}) collective-permute-start(bf16[64,1792]{1,0:T(8,128)(2,1)S(1)} %shard_map.115.hid_ref), channel_id=1, source_target_pairs={{0,8},{8,0},{16,24},{24,16},{1,9},{9,1},{17,25},{25,17},{2,10},{10... | collective-permute-start | bytes 688136 | tf_op jit(solution)/shard_map/ppermute | solution.py:25
  75.3 10.8 %collective-permute-start.26 = (bf16[64,1792]{1,0:T(8,128)(2,1)S(1)}, bf16[64,1792]{1,0:T(8,128)(2,1)S(1)}, u32[]{:S(2)}, u32[]{:S(2)}) collective-permute-start(bf16[64,1792]{1,0:T(8,128)(2,1)S(1)} %shard_map.122.hid_ref), channel_id=1, source_target_pairs={{0,8},{8,0},{16,24},{24,16},{1,9},{9,1},{17,25},{25,17},{2,10},{10... | collective-permute-start | bytes 688136 | tf_op jit(solution)/shard_map/ppermute | solution.py:25
  79.5 7.7 %collective-permute-start.20 = (bf16[64,1792]{1,0:T(8,128)(2,1)S(1)}, bf16[64,1792]{1,0:T(8,128)(2,1)S(1)}, u32[]{:S(2)}, u32[]{:S(2)}) collective-permute-start(bf16[64,1792]{1,0:T(8,128)(2,1)S(1)} %shard_map.118.hid_ref), channel_id=1, source_target_pairs={{0,8},{8,0},{16,24},{24,16},{1,9},{9,1},{17,25},{25,17},{2,10},{10... | collective-permute-start | bytes 688136 | tf_op jit(solution)/shard_map/ppermute | solution.py:25
  83.4 10.4 %collective-permute-start.12 = (bf16[2,2,8,1024]{3,2,1,0:T(8,128)(2,1)S(1)}, bf16[2,2,8,1024]{3,2,1,0:T(8,128)(2,1)S(1)}, u32[]{:S(2)}, u32[]{:S(2)}) collective-permute-start(bf16[2,2,8,1024]{3,2,1,0:T(8,128)(2,1)S(1)} %get-tuple-element.63), channel_id=1, source_target_pairs={{0,2},{1,3},{2,0},{3,1},{4,6},{5,7},{6,4},{7,5},{8,10},{9,11},{10,... | collective-permute-start | bytes 196616 | tf_op jit(solution)/shard_map/ppermute | solution.py:25
  84.3 16.3 %collective-permute-start.18 = (bf16[2,4,8,1024]{3,2,1,0:T(8,128)(2,1)S(1)}, bf16[2,4,8,1024]{3,2,1,0:T(8,128)(2,1)S(1)}, u32[]{:S(2)}, u32[]{:S(2)}) collective-permute-start(bf16[2,4,8,1024]{3,2,1,0:T(8,128)(2,1)S(1)} %get-tuple-element.72), channel_id=1, source_target_pairs={{0,1},{1,0},{2,3},{3,2},{4,5},{5,4},{6,7},{7,6},{8,9},{9,8},{10,11... | collective-permute-start | bytes 393224 | tf_op jit(solution)/shard_map/ppermute | solution.py:25
  86.8 13.7 %collective-permute-start.27 = (bf16[2,4,8,1024]{3,2,1,0:T(8,128)(2,1)S(1)}, bf16[2,4,8,1024]{3,2,1,0:T(8,128)(2,1)S(1)}, u32[]{:S(2)}, u32[]{:S(2)}) collective-permute-start(bf16[2,4,8,1024]{3,2,1,0:T(8,128)(2,1)S(1)} %get-tuple-element.86), channel_id=1, source_target_pairs={{0,1},{1,0},{2,3},{3,2},{4,5},{5,4},{6,7},{7,6},{8,9},{9,8},{10,11... | collective-permute-start | bytes 393224 | tf_op jit(solution)/shard_map/ppermute | solution.py:25
  88.0 12.7 %collective-permute-start.21 = (bf16[2,4,8,1024]{3,2,1,0:T(8,128)(2,1)S(1)}, bf16[2,4,8,1024]{3,2,1,0:T(8,128)(2,1)S(1)}, u32[]{:S(2)}, u32[]{:S(2)}) collective-permute-start(bf16[2,4,8,1024]{3,2,1,0:T(8,128)(2,1)S(1)} %get-tuple-element.77), channel_id=1, source_target_pairs={{0,1},{1,0},{2,3},{3,2},{4,5},{5,4},{6,7},{7,6},{8,9},{9,8},{10,11... | collective-permute-start | bytes 393224 | tf_op jit(solution)/shard_map/ppermute | solution.py:25
  89.7 8.4 %collective-permute-start.13 = (bf16[2,2,8,1024]{3,2,1,0:T(8,128)(2,1)S(1)}, bf16[2,2,8,1024]{3,2,1,0:T(8,128)(2,1)S(1)}, u32[]{:S(2)}, u32[]{:S(2)}) collective-permute-start(bf16[2,2,8,1024]{3,2,1,0:T(8,128)(2,1)S(1)} %get-tuple-element.64), channel_id=1, source_target_pairs={{0,4},{1,5},{2,6},{3,7},{4,0},{5,1},{6,2},{7,3},{8,12},{9,13},{10,... | collective-permute-start | bytes 196616 | tf_op jit(solution)/shard_map/ppermute | solution.py:25
  93.8 6.1 %collective-permute-start.14 = (bf16[2,2,8,1024]{3,2,1,0:T(8,128)(2,1)S(1)}, bf16[2,2,8,1024]{3,2,1,0:T(8,128)(2,1)S(1)}, u32[]{:S(2)}, u32[]{:S(2)}) collective-permute-start(bf16[2,2,8,1024]{3,2,1,0:T(8,128)(2,1)S(1)} %get-tuple-element.65), channel_id=1, source_target_pairs={{0,6},{1,7},{2,4},{3,5},{4,2},{5,3},{6,0},{7,1},{8,14},{9,15},{10,... | collective-permute-start | bytes 196616 | tf_op jit(solution)/shard_map/ppermute | solution.py:25
  99.9 5.3 %collective-permute-start.15 = (bf16[2,1,8,1024]{3,2,1,0:T(8,128)(2,1)S(1)}, bf16[2,1,8,1024]{3,2,1,0:T(8,128)(2,1)S(1)}, u32[]{:S(2)}, u32[]{:S(2)}) collective-permute-start(bf16[2,1,8,1024]{3,2,1,0:T(8,128)(2,1)S(1)} %get-tuple-element.67), channel_id=1, source_target_pairs={{0,1},{1,0},{2,3},{3,2},{4,5},{5,4},{6,7},{7,6},{8,9},{9,8},{10,11... | collective-permute-start | bytes 98312 | tf_op jit(solution)/shard_map/ppermute | solution.py:25
  100.5 5.7 %collective-permute-start.28 = (bf16[2,1,8,1024]{3,2,1,0:T(8,128)(2,1)S(1)}, bf16[2,1,8,1024]{3,2,1,0:T(8,128)(2,1)S(1)}, u32[]{:S(2)}, u32[]{:S(2)}) collective-permute-start(bf16[2,1,8,1024]{3,2,1,0:T(8,128)(2,1)S(1)} %get-tuple-element.88), channel_id=1, source_target_pairs={{0,2},{1,3},{2,0},{3,1},{4,6},{5,7},{6,4},{7,5},{8,10},{9,11},{10,... | collective-permute-start | bytes 98312 | tf_op jit(solution)/shard_map/ppermute | solution.py:25
  100.7 11.4 %collective-permute-start.22 = (bf16[2,1,16,1024]{3,2,1,0:T(8,128)(2,1)S(1)}, bf16[2,1,16,1024]{3,2,1,0:T(8,128)(2,1)S(1)}, u32[]{:S(2)}, u32[]{:S(2)}) collective-permute-start(bf16[2,1,16,1024]{3,2,1,0:T(8,128)(2,1)S(1)} %get-tuple-element.79), channel_id=1, source_target_pairs={{0,2},{1,3},{2,0},{3,1},{4,6},{5,7},{6,4},{7,5},{8,10},{9,11},{10,... | collective-permute-start | bytes 196616 | tf_op jit(solution)/shard_map/ppermute | solution.py:25
  102.7 9.3 %collective-permute-start.23 = (bf16[2,1,16,1024]{3,2,1,0:T(8,128)(2,1)S(1)}, bf16[2,1,16,1024]{3,2,1,0:T(8,128)(2,1)S(1)}, u32[]{:S(2)}, u32[]{:S(2)}) collective-permute-start(bf16[2,1,16,1024]{3,2,1,0:T(8,128)(2,1)S(1)} %get-tuple-element.80), channel_id=1, source_target_pairs={{0,4},{1,5},{2,6},{3,7},{4,0},{5,1},{6,2},{7,3},{8,12},{9,13},{10,... | collective-permute-start | bytes 196616 | tf_op jit(solution)/shard_map/ppermute | solution.py:25
  104.0 8.1 %collective-permute-start.24 = (bf16[2,1,16,1024]{3,2,1,0:T(8,128)(2,1)S(1)}, bf16[2,1,16,1024]{3,2,1,0:T(8,128)(2,1)S(1)}, u32[]{:S(2)}, u32[]{:S(2)}) collective-permute-start(bf16[2,1,16,1024]{3,2,1,0:T(8,128)(2,1)S(1)} %get-tuple-element.81), channel_id=1, source_target_pairs={{0,6},{1,7},{2,4},{3,5},{4,2},{5,3},{6,0},{7,1},{8,14},{9,15},{10,... | collective-permute-start | bytes 196616 | tf_op jit(solution)/shard_map/ppermute | solution.py:25
  105.2 6.9 %collective-permute-start.29 = (bf16[2,1,8,1024]{3,2,1,0:T(8,128)(2,1)S(1)}, bf16[2,1,8,1024]{3,2,1,0:T(8,128)(2,1)S(1)}, u32[]{:S(2)}, u32[]{:S(2)}) collective-permute-start(bf16[2,1,8,1024]{3,2,1,0:T(8,128)(2,1)S(1)} %get-tuple-element.89), channel_id=1, source_target_pairs={{0,4},{1,5},{2,6},{3,7},{4,0},{5,1},{6,2},{7,3},{8,12},{9,13},{10,... | collective-permute-start | bytes 98312 | tf_op jit(solution)/shard_map/ppermute | solution.py:25
  106.2 5.8 %collective-permute-start.30 = (bf16[2,1,8,1024]{3,2,1,0:T(8,128)(2,1)S(1)}, bf16[2,1,8,1024]{3,2,1,0:T(8,128)(2,1)S(1)}, u32[]{:S(2)}, u32[]{:S(2)}) collective-permute-start(bf16[2,1,8,1024]{3,2,1,0:T(8,128)(2,1)S(1)} %get-tuple-element.90), channel_id=1, source_target_pairs={{0,6},{1,7},{2,4},{3,5},{4,2},{5,3},{6,0},{7,1},{8,14},{9,15},{10,... | collective-permute-start | bytes 98312 | tf_op jit(solution)/shard_map/ppermute | solution.py:25

commit v6 on v5

--- a/solution.py
+++ b/solution.py
@@ -409,13 +409,35 @@
     for count in counts:
         (total, *got), refs = refs[:count], refs[count:]
         for side in range(2):
-            value = total[side, 0]
-            for g in got:
-                value += g[side, 0].astype(F32)
-            size = value.shape[0] // draft
+            if got:
+                value = total[side, 0]
+                for g in got:
+                    value += g[side, 0].astype(F32)
+                size = value.shape[0] // draft
+                value = value.astype(BF16).reshape(size, draft, width)
+            else:
+                value = total[side]
+                size = value.shape[0]
             at = start + (requests // 2) * (core if side == 0 else 1 - core)
-            out_ref[pl.ds(at, size)] = value.astype(BF16).reshape(size, draft, width)
+            out_ref[pl.ds(at, size)] = value
         start += size
+
+
+def settle_kernel(*refs):
+    total_ref, *got_refs, out_ref = refs
+    draft = out_ref.shape[2]
+    value = total_ref[:, 0]
+    for got in got_refs:
+        value += got[:, 0].astype(F32)
+    size, width = value.shape[1:]
+    for side in range(2):
+        out_ref[side] = value[side].astype(BF16).reshape(size // draft, draft, width)
+
+
+def settle(part, draft):
+    _, _, size, width = part[0].shape
+    out = jax.ShapeDtypeStruct((2, size // draft, draft, width), BF16)
+    return [in_vmem(settle_kernel, out, *part)]
 
 
 def join(parts, out):
@@ -538,6 +560,7 @@
         total, *gives = last_split(low_bit, [outs[k] for k in members])
         gots = [swap(give, COL, (q + 1) << low_bit) for q, give in enumerate(gives)]
         parts.append([total] + gots)
+    parts = [settle(p, draft) for p in parts[:-1]] + parts[-1:]
     return join(parts, jax.ShapeDtypeStruct((batch // cn, draft, w_down.shape[1]), BF16))
 
 

time: 113 us -> 113 us (level)
  waiting for transfers between devices: 57.4 us -> 58.6 us
  starting transfers between devices: 30.9 us -> 29.7 us
    ppermute x31, starting transfers between devices: 30.9 us -> 29.7 us  [swap(): return lax.ppermute(x, axis, [(i, i ^ mask) for i in range(n)])]
    pallas_call x17 -> x19, Pallas kernels: 7.71 us -> 7.71 us  [in_vmem(): pl.pallas_call(kernel, in_specs=[vmem] * len(args), out_specs=jax.tree.ma...]
  transfers between devices with their start and end apart: 31 -> 31, of which waited for: 13 -> 15; matrix products, arithmetic and copies ran while one was open for 0% -> 0% of each run, Pallas kernels for 14% -> 14%
where the time goes in v6:
time: 113 us
  waiting for transfers between devices  58.6 us (52%)
  starting transfers between devices  29.7 us (26%)
  Pallas kernels  24 us (21%)
    ppermute x31, waiting for transfers between devices, swap(): return lax.ppermute(x, axis, [(i, i ^ mask) for i in range(n)])  58.6 us
    ppermute x31, starting transfers between devices, swap(): return lax.ppermute(x, axis, [(i, i ^ mask) for i in range(n)])  29.7 us
    pallas_call x1, Pallas kernels, low_part(): pl.pallas_call(functools.partial(low_kernel, blocks, slab, shift), in_spe...  7.99 us
    pallas_call x19, Pallas kernels, in_vmem(): pl.pallas_call(kernel, in_specs=[vmem] * len(args), out_specs=jax.tree.ma...  7.71 us
    pallas_call x1, Pallas kernels, factors(): pl.pallas_call(factor_kernel, grid=(ff // tile,), in_specs=[pl.BlockSpec(...  3.55 us
    pallas_call x1, Pallas kernels, split_matmul(): pl.pallas_call(split_kernel, grid=(ff // tile,), in_specs=[pl.BlockSpec((...  3.01 us
  transfers between devices with their start and end apart: 31, of which 15 were waited for; matrix products, arithmetic and copies ran while one was open for 0% of the time, Pallas kernels for 14%

profile of v6, /device:TPU:0, one launch (start us, length us, event | category | flops | bytes accessed | tf_op | source)
XLA Modules:
  0.0 112.7 jit_solution(5521090106082446269)
XLA Ops:
  0.0 8.0 %low_part.1 = (f32[16,512]{1,0:T(8,128)S(1)}, bf16[64,512]{1,0:T(8,128)(2,1)S(1)}, bf16[64,256]{1,0:T(8,128)(2,1)S(1)}, bf16[512,1024]{1,0:T(8,128)(2,1)S(1)}, f...) custom-call(s32[1,64]{1,0:T(1,128)} %bitcast.6, s32[1,64]{1,0:T(1,128)} %bitcast.7, ...), custom_call_target="tpu_custom_call" | custom-call | tf_op jit(solution)/shard_map/low_part/pallas_call | solution.py:141
  8.0 0.6 collective-permute-start
  8.6 3.5 %factors.1.mine_ref = bf16[256,1792]{1,0:T(8,128)(2,1)S(1)} custom-call(bf16[64,512]{1,0:T(8,128)(2,1)S(1)} %get-tuple-element.52.hyper_ref, bf16[512,4,1792]{2,1,0:T(4,128)(2,1)S(1)} %copy-done.1), custom_call_target="tpu_custom_call" | custom-call | tf_op jit(solution)/shard_map/factors/pallas_call | solution.py:217
  12.2 3.0 %shard_map.110 = (f32[256,1792]{1,0:T(8,128)S(1)}, bf16[256,1792]{1,0:T(8,128)(2,1)S(1)}) custom-call(bf16[512,1024]{1,0:T(8,128)(2,1)S(1)} %get-tuple-element.53.x_ref, bf16[1024,1792]{1,0:T(8,128)(2,1)S(1)} %copy-done.2), custom_call_target="tpu_custom_call" | custom-call | tf_op jit(solution)/shard_map/pallas_call | solution.py:168
  15.2 0.5 collective-permute-start.9
  15.9 2.6 %collective-permute-start.1 = (bf16[256,1792]{1,0:T(8,128)(2,1)S(1)}, bf16[256,1792]{1,0:T(8,128)(2,1)S(1)}, u32[]{:S(2)}, u32[]{:S(2)}) collective-permute-start(bf16[256,1792]{1,0:T(8,128)(2,1)S(1)} %add_convert_fusion), channel_id=1, source_target_pairs={{0,16},{8,24},{16,0},{24,8},{1,17},{9,25},{17,1},{25,9},{2,18},{10... | collective-permute-start | bytes 2752520 | tf_op jit(solution)/shard_map/ppermute | solution.py:25
  18.6 21.6 %collective-permute-done.2 = f32[16,512]{1,0:T(8,128)S(1)} collective-permute-done((f32[16,512]{1,0:T(8,128)S(1)}, f32[16,512]{1,0:T(8,128)S(1)}, u32[]{:S(2)}, u32[]{:S(2)}) %collective-permute-start.2) | collective-permute-done | bytes 32800 | tf_op jit(solution)/shard_map/ppermute | solution.py:25
  40.2 1.7 %collective-permute-start.3 = (f32[16,512]{1,0:T(8,128)S(1)}, f32[16,512]{1,0:T(8,128)S(1)}, u32[]{:S(2)}, u32[]{:S(2)}) collective-permute-start(f32[16,512]{1,0:T(8,128)S(1)} %add.22), channel_id=1, source_target_pairs={{0,1},{1,0},{2,3},{3,2},{4,5},{5,4},{6,7},{7,6},{8,9},{9,8},{10,11... | collective-permute-start | bytes 98312 | tf_op jit(solution)/shard_map/ppermute | solution.py:25
  42.0 2.2 %collective-permute-done.3 = f32[16,512]{1,0:T(8,128)S(1)} collective-permute-done((f32[16,512]{1,0:T(8,128)S(1)}, f32[16,512]{1,0:T(8,128)S(1)}, u32[]{:S(2)}, u32[]{:S(2)}) %collective-permute-start.3) | collective-permute-done | bytes 32800 | tf_op jit(solution)/shard_map/ppermute | solution.py:25
  44.2 3.8 %collective-permute-start.6 = (f32[16,512]{1,0:T(8,128)S(1)}, f32[16,512]{1,0:T(8,128)S(1)}, u32[]{:S(2)}, u32[]{:S(2)}) collective-permute-start(f32[16,512]{1,0:T(8,128)S(1)} %add.23), channel_id=1, source_target_pairs={{0,6},{1,7},{2,4},{3,5},{4,2},{5,3},{6,0},{7,1},{8,14},{9,15},{10,... | collective-permute-start | bytes 98312 | tf_op jit(solution)/shard_map/ppermute | solution.py:25
  48.0 1.9 %collective-permute-done.6 = f32[16,512]{1,0:T(8,128)S(1)} collective-permute-done((f32[16,512]{1,0:T(8,128)S(1)}, f32[16,512]{1,0:T(8,128)S(1)}, u32[]{:S(2)}, u32[]{:S(2)}) %collective-permute-start.6) | collective-permute-done | bytes 32800 | tf_op jit(solution)/shard_map/ppermute | solution.py:25
  49.9 2.9 %collective-permute-done.5 = f32[16,512]{1,0:T(8,128)S(1)} collective-permute-done((f32[16,512]{1,0:T(8,128)S(1)}, f32[16,512]{1,0:T(8,128)S(1)}, u32[]{:S(2)}, u32[]{:S(2)}) %collective-permute-start.5) | collective-permute-done | bytes 32800 | tf_op jit(solution)/shard_map/ppermute | solution.py:25
  52.8 1.0 collective-permute-done.4
  53.9 1.2 %collective-permute-done.7 = f32[16,256]{1,0:T(8,128)S(1)} collective-permute-done((f32[16,256]{1,0:T(8,128)S(1)}, f32[16,256]{1,0:T(8,128)S(1)}, u32[]{:S(2)}, u32[]{:S(2)}) %collective-permute-start.7) | collective-permute-done | bytes 16416 | tf_op jit(solution)/shard_map/ppermute | solution.py:25
  55.1 1.8 %adapter.1 = (f32[256,1792]{1,0:T(8,128)S(1)}, bf16[64,1792]{1,0:T(8,128)(2,1)S(1)}, bf16[64,1792]{1,0:T(8,128)(2,1)S(1)}, bf16[64,1792]{1,0:T(8,128)(2,1)S(1)}, bf16[64,1792]{1,0:T(8,128)(2,1)S(1)}) custom-call(f32[16,256]{1,0:T(8,128)S(1)} %slice_add_fusion.low_ref, bf16[64,256]{1,0:T(8,128)(2,1)S(1)} %get-tuple-element.51.member_ref, ...), custom_call_target="tpu_custom_call" | custom-call | tf_op jit(solution)/shard_map/adapter/pallas_call | solution.py:260
  56.9 1.9 %collective-permute-start.16 = (bf16[64,1792]{1,0:T(8,128)(2,1)S(1)}, bf16[64,1792]{1,0:T(8,128)(2,1)S(1)}, u32[]{:S(2)}, u32[]{:S(2)}) collective-permute-start(bf16[64,1792]{1,0:T(8,128)(2,1)S(1)} %get-tuple-element.68), channel_id=1, source_target_pairs={{0,16},{8,24},{16,0},{24,8},{1,17},{9,25},{17,1},{25,9},{2,18},{10... | collective-permute-start | bytes 688136 | tf_op jit(solution)/shard_map/ppermute | solution.py:25
  59.0 1.8 %collective-permute-start.25 = (bf16[64,1792]{1,0:T(8,128)(2,1)S(1)}, bf16[64,1792]{1,0:T(8,128)(2,1)S(1)}, u32[]{:S(2)}, u32[]{:S(2)}) collective-permute-start(bf16[64,1792]{1,0:T(8,128)(2,1)S(1)} %get-tuple-element.82), channel_id=1, source_target_pairs={{0,16},{8,24},{16,0},{24,8},{1,17},{9,25},{17,1},{25,9},{2,18},{10... | collective-permute-start | bytes 688136 | tf_op jit(solution)/shard_map/ppermute | solution.py:25
  61.0 0.6 shard_map.109.act_ref
  61.6 3.8 %collective-permute-done.16.up_ref = bf16[64,1792]{1,0:T(8,128)(2,1)S(1)} collective-permute-done((bf16[64,1792]{1,0:T(8,128)(2,1)S(1)}, bf16[64,1792]{1,0:T(8,128)(2,1)S(1)}, u32[]{:S(2)}, u32[]{:S(2)}) %collective-permute-start.16) | collective-permute-done | bytes 229408 | tf_op jit(solution)/shard_map/ppermute | solution.py:25
  65.6 4.8 %collective-permute-done.19.up_ref = bf16[64,1792]{1,0:T(8,128)(2,1)S(1)} collective-permute-done((bf16[64,1792]{1,0:T(8,128)(2,1)S(1)}, bf16[64,1792]{1,0:T(8,128)(2,1)S(1)}, u32[]{:S(2)}, u32[]{:S(2)}) %collective-permute-start.19) | collective-permute-done | bytes 229408 | tf_op jit(solution)/shard_map/ppermute | solution.py:25
  70.5 4.8 %collective-permute-done.25.up_ref = bf16[64,1792]{1,0:T(8,128)(2,1)S(1)} collective-permute-done((bf16[64,1792]{1,0:T(8,128)(2,1)S(1)}, bf16[64,1792]{1,0:T(8,128)(2,1)S(1)}, u32[]{:S(2)}, u32[]{:S(2)}) %collective-permute-start.25) | collective-permute-done | bytes 229408 | tf_op jit(solution)/shard_map/ppermute | solution.py:25
  75.4 4.1 %collective-permute-done.10.up_ref = bf16[64,1792]{1,0:T(8,128)(2,1)S(1)} collective-permute-done((bf16[64,1792]{1,0:T(8,128)(2,1)S(1)}, bf16[64,1792]{1,0:T(8,128)(2,1)S(1)}, u32[]{:S(2)}, u32[]{:S(2)}) %collective-permute-start.10) | collective-permute-done | bytes 229408 | tf_op jit(solution)/shard_map/ppermute | solution.py:25
  79.6 0.8 shard_map.117
  80.4 0.8 shard_map.118
  81.1 1.8 %collective-permute-start.18 = (bf16[2,4,8,1024]{3,2,1,0:T(8,128)(2,1)S(1)}, bf16[2,4,8,1024]{3,2,1,0:T(8,128)(2,1)S(1)}, u32[]{:S(2)}, u32[]{:S(2)}) collective-permute-start(bf16[2,4,8,1024]{3,2,1,0:T(8,128)(2,1)S(1)} %get-tuple-element.72), channel_id=1, source_target_pairs={{0,1},{1,0},{2,3},{3,2},{4,5},{5,4},{6,7},{7,6},{8,9},{9,8},{10,11... | collective-permute-start | bytes 393224 | tf_op jit(solution)/shard_map/ppermute | solution.py:25
  82.9 0.7 shard_map.120
  83.7 0.8 shard_map.121
  84.4 0.4 collective-permute-start.21
  84.8 0.7 shard_map.125
  85.6 0.8 shard_map.126
  86.3 1.8 %collective-permute-start.27 = (bf16[2,4,8,1024]{3,2,1,0:T(8,128)(2,1)S(1)}, bf16[2,4,8,1024]{3,2,1,0:T(8,128)(2,1)S(1)}, u32[]{:S(2)}, u32[]{:S(2)}) collective-permute-start(bf16[2,4,8,1024]{3,2,1,0:T(8,128)(2,1)S(1)} %get-tuple-element.86), channel_id=1, source_target_pairs={{0,1},{1,0},{2,3},{3,2},{4,5},{5,4},{6,7},{7,6},{8,9},{9,8},{10,11... | collective-permute-start | bytes 393224 | tf_op jit(solution)/shard_map/ppermute | solution.py:25
  88.1 0.8 shard_map.112
  88.9 0.8 shard_map.113
  89.8 4.0 %collective-permute-start.13 = (bf16[2,2,8,1024]{3,2,1,0:T(8,128)(2,1)S(1)}, bf16[2,2,8,1024]{3,2,1,0:T(8,128)(2,1)S(1)}, u32[]{:S(2)}, u32[]{:S(2)}) collective-permute-start(bf16[2,2,8,1024]{3,2,1,0:T(8,128)(2,1)S(1)} %get-tuple-element.64), channel_id=1, source_target_pairs={{0,4},{1,5},{2,6},{3,7},{4,0},{5,1},{6,2},{7,3},{8,12},{9,13},{10,... | collective-permute-start | bytes 196616 | tf_op jit(solution)/shard_map/ppermute | solution.py:25
  93.8 0.3 collective-permute-start.14
  94.2 0.3 collective-permute-start.22
  94.5 3.7 %collective-permute-done.13.refs_1_ = bf16[2,2,8,1024]{3,2,1,0:T(8,128)(2,1)S(1)} collective-permute-done((bf16[2,2,8,1024]{3,2,1,0:T(8,128)(2,1)S(1)}, bf16[2,2,8,1024]{3,2,1,0:T(8,128)(2,1)S(1)}, u32[]{:S(2)}, u32[]{:S(2)}) %collective-permute-start.13) | collective-permute-done | bytes 65568 | tf_op jit(solution)/shard_map/ppermute | solution.py:25
  98.2 1.6 %collective-permute-done.14.refs_2_ = bf16[2,2,8,1024]{3,2,1,0:T(8,128)(2,1)S(1)} collective-permute-done((bf16[2,2,8,1024]{3,2,1,0:T(8,128)(2,1)S(1)}, bf16[2,2,8,1024]{3,2,1,0:T(8,128)(2,1)S(1)}, u32[]{:S(2)}, u32[]{:S(2)}) %collective-permute-start.14) | collective-permute-done | bytes 65568 | tf_op jit(solution)/shard_map/ppermute | solution.py:25
  99.9 0.6 collective-permute-start.15
  100.5 1.3 %collective-permute-start.23 = (bf16[2,1,16,1024]{3,2,1,0:T(8,128)(2,1)S(1)}, bf16[2,1,16,1024]{3,2,1,0:T(8,128)(2,1)S(1)}, u32[]{:S(2)}, u32[]{:S(2)}) collective-permute-start(bf16[2,1,16,1024]{3,2,1,0:T(8,128)(2,1)S(1)} %get-tuple-element.80), channel_id=1, source_target_pairs={{0,4},{1,5},{2,6},{3,7},{4,0},{5,1},{6,2},{7,3},{8,12},{9,13},{10,... | collective-permute-start | bytes 196616 | tf_op jit(solution)/shard_map/ppermute | solution.py:25
  101.8 0.7 collective-permute-start.24
  102.5 1.6 %collective-permute-start.28 = (bf16[2,1,8,1024]{3,2,1,0:T(8,128)(2,1)S(1)}, bf16[2,1,8,1024]{3,2,1,0:T(8,128)(2,1)S(1)}, u32[]{:S(2)}, u32[]{:S(2)}) collective-permute-start(bf16[2,1,8,1024]{3,2,1,0:T(8,128)(2,1)S(1)} %get-tuple-element.88), channel_id=1, source_target_pairs={{0,2},{1,3},{2,0},{3,1},{4,6},{5,7},{6,4},{7,5},{8,10},{9,11},{10,... | collective-permute-start | bytes 98312 | tf_op jit(solution)/shard_map/ppermute | solution.py:25
  104.1 2.2 %collective-permute-start.29 = (bf16[2,1,8,1024]{3,2,1,0:T(8,128)(2,1)S(1)}, bf16[2,1,8,1024]{3,2,1,0:T(8,128)(2,1)S(1)}, u32[]{:S(2)}, u32[]{:S(2)}) collective-permute-start(bf16[2,1,8,1024]{3,2,1,0:T(8,128)(2,1)S(1)} %get-tuple-element.89), channel_id=1, source_target_pairs={{0,4},{1,5},{2,6},{3,7},{4,0},{5,1},{6,2},{7,3},{8,12},{9,13},{10,... | collective-permute-start | bytes 98312 | tf_op jit(solution)/shard_map/ppermute | solution.py:25
  106.3 0.7 collective-permute-start.30
  107.0 1.2 %collective-permute-done.24.refs_3_ = bf16[2,1,16,1024]{3,2,1,0:T(8,128)(2,1)S(1)} collective-permute-done((bf16[2,1,16,1024]{3,2,1,0:T(8,128)(2,1)S(1)}, bf16[2,1,16,1024]{3,2,1,0:T(8,128)(2,1)S(1)}, u32[]{:S(2)}, u32[]{:S(2)}) %collective-permute-start.24) | collective-permute-done | bytes 65568 | tf_op jit(solution)/shard_map/ppermute | solution.py:25
  108.3 1.2 %collective-permute-done.29.refs_4_ = bf16[2,1,8,1024]{3,2,1,0:T(8,128)(2,1)S(1)} collective-permute-done((bf16[2,1,8,1024]{3,2,1,0:T(8,128)(2,1)S(1)}, bf16[2,1,8,1024]{3,2,1,0:T(8,128)(2,1)S(1)}, u32[]{:S(2)}, u32[]{:S(2)}) %collective-permute-start.29) | collective-permute-done | bytes 32800 | tf_op jit(solution)/shard_map/ppermute | solution.py:25
  109.6 2.5 %collective-permute-done.30.refs_5_ = bf16[2,1,8,1024]{3,2,1,0:T(8,128)(2,1)S(1)} collective-permute-done((bf16[2,1,8,1024]{3,2,1,0:T(8,128)(2,1)S(1)}, bf16[2,1,8,1024]{3,2,1,0:T(8,128)(2,1)S(1)}, u32[]{:S(2)}, u32[]{:S(2)}) %collective-permute-start.30) | collective-permute-done | bytes 32800 | tf_op jit(solution)/shard_map/ppermute | solution.py:25
  112.0 0.7 shard_map.128
  (49 shorter events, 1.7 us)
Async XLA Ops:
  0.0 8.6 %copy-start.1 = (bf16[512,4,1792]{2,1,0:T(4,128)(2,1)S(1)}, bf16[512,4,1792]{2,1,0:T(4,128)(2,1)}, u32[]{:S(2)}) copy-start(bf16[512,4,1792]{2,1,0:T(4,128)(2,1)} %gen_ref.1) | copy-start | bytes 22020100
  8.0 7.8 %collective-permute-start = (bf16[256,1792]{1,0:T(8,128)(2,1)S(1)}, bf16[256,1792]{1,0:T(8,128)(2,1)S(1)}, u32[]{:S(2)}, u32[]{:S(2)}) collective-permute-start(bf16[256,1792]{1,0:T(8,128)(2,1)S(1)} %get-tuple-element.49), channel_id=1, source_target_pairs={{0,8},{8,0},{16,24},{24,16},{1,9},{9,1},{17,25},{25,17},{2,10},{10... | collective-permute-start | bytes 2752520 | tf_op jit(solution)/shard_map/ppermute | solution.py:25
  8.6 3.7 %copy-start.2 = (bf16[1024,1792]{1,0:T(8,128)(2,1)S(1)}, bf16[1024,1792]{1,0:T(8,128)(2,1)}, u32[]{:S(2)}) copy-start(bf16[1024,1792]{1,0:T(8,128)(2,1)} %w_ref.9) | copy-start | bytes 11010052
  12.1 43.0 %collective-permute-start.8 = (bf16[256,1792]{1,0:T(8,128)(2,1)S(1)}, bf16[256,1792]{1,0:T(8,128)(2,1)S(1)}, u32[]{:S(2)}, u32[]{:S(2)}) collective-permute-start(bf16[256,1792]{1,0:T(8,128)(2,1)S(1)} %factors.1.mine_ref), channel_id=1, source_target_pairs={{0,8},{8,0},{16,24},{24,16},{1,9},{9,1},{17,25},{25,17},{2,10},{10... | collective-permute-start | bytes 2752520 | tf_op jit(solution)/shard_map/ppermute | solution.py:25
  15.2 39.9 %collective-permute-start.9 = (bf16[256,1792]{1,0:T(8,128)(2,1)S(1)}, bf16[256,1792]{1,0:T(8,128)(2,1)S(1)}, u32[]{:S(2)}, u32[]{:S(2)}) collective-permute-start(bf16[256,1792]{1,0:T(8,128)(2,1)S(1)} %get-tuple-element.55), channel_id=1, source_target_pairs={{0,8},{8,0},{16,24},{24,16},{1,9},{9,1},{17,25},{25,17},{2,10},{10... | collective-permute-start | bytes 2752520 | tf_op jit(solution)/shard_map/ppermute | solution.py:25
  15.9 45.1 %collective-permute-start.1 = (bf16[256,1792]{1,0:T(8,128)(2,1)S(1)}, bf16[256,1792]{1,0:T(8,128)(2,1)S(1)}, u32[]{:S(2)}, u32[]{:S(2)}) collective-permute-start(bf16[256,1792]{1,0:T(8,128)(2,1)S(1)} %add_convert_fusion), channel_id=1, source_target_pairs={{0,16},{8,24},{16,0},{24,8},{1,17},{9,25},{17,1},{25,9},{2,18},{10... | collective-permute-start | bytes 2752520 | tf_op jit(solution)/shard_map/ppermute | solution.py:25
  18.5 21.7 %collective-permute-start.2 = (f32[16,512]{1,0:T(8,128)S(1)}, f32[16,512]{1,0:T(8,128)S(1)}, u32[]{:S(2)}, u32[]{:S(2)}) collective-permute-start(f32[16,512]{1,0:T(8,128)S(1)} %get-tuple-element.50), channel_id=1, source_target_pairs={{0,16},{8,24},{16,0},{24,8},{1,17},{9,25},{17,1},{25,9},{2,18},{10... | collective-permute-start | bytes 98312 | tf_op jit(solution)/shard_map/ppermute | solution.py:25
  40.2 3.9 %collective-permute-start.3 = (f32[16,512]{1,0:T(8,128)S(1)}, f32[16,512]{1,0:T(8,128)S(1)}, u32[]{:S(2)}, u32[]{:S(2)}) collective-permute-start(f32[16,512]{1,0:T(8,128)S(1)} %add.22), channel_id=1, source_target_pairs={{0,1},{1,0},{2,3},{3,2},{4,5},{5,4},{6,7},{7,6},{8,9},{9,8},{10,11... | collective-permute-start | bytes 98312 | tf_op jit(solution)/shard_map/ppermute | solution.py:25
  44.2 5.7 %collective-permute-start.6 = (f32[16,512]{1,0:T(8,128)S(1)}, f32[16,512]{1,0:T(8,128)S(1)}, u32[]{:S(2)}, u32[]{:S(2)}) collective-permute-start(f32[16,512]{1,0:T(8,128)S(1)} %add.23), channel_id=1, source_target_pairs={{0,6},{1,7},{2,4},{3,5},{4,2},{5,3},{6,0},{7,1},{8,14},{9,15},{10,... | collective-permute-start | bytes 98312 | tf_op jit(solution)/shard_map/ppermute | solution.py:25
  48.0 4.8 %collective-permute-start.5 = (f32[16,512]{1,0:T(8,128)S(1)}, f32[16,512]{1,0:T(8,128)S(1)}, u32[]{:S(2)}, u32[]{:S(2)}) collective-permute-start(f32[16,512]{1,0:T(8,128)S(1)} %add.23), channel_id=1, source_target_pairs={{0,4},{1,5},{2,6},{3,7},{4,0},{5,1},{6,2},{7,3},{8,12},{9,13},{10,... | collective-permute-start | bytes 98312 | tf_op jit(solution)/shard_map/ppermute | solution.py:25
  49.9 3.9 %collective-permute-start.4 = (f32[16,512]{1,0:T(8,128)S(1)}, f32[16,512]{1,0:T(8,128)S(1)}, u32[]{:S(2)}, u32[]{:S(2)}) collective-permute-start(f32[16,512]{1,0:T(8,128)S(1)} %add.23), channel_id=1, source_target_pairs={{0,2},{1,3},{2,0},{3,1},{4,6},{5,7},{6,4},{7,5},{8,10},{9,11},{10,... | collective-permute-start | bytes 98312 | tf_op jit(solution)/shard_map/ppermute | solution.py:25
  53.8 1.2 %collective-permute-start.7 = (f32[16,256]{1,0:T(8,128)S(1)}, f32[16,256]{1,0:T(8,128)S(1)}, u32[]{:S(2)}, u32[]{:S(2)}) collective-permute-start(f32[16,256]{1,0:T(8,128)S(1)} %slice.9), channel_id=1, source_target_pairs={{0,8},{8,0},{16,24},{24,16},{1,9},{9,1},{17,25},{25,17},{2,10},{10... | collective-permute-start | bytes 49160 | tf_op jit(solution)/shard_map/ppermute | solution.py:25
  55.1 5.9 %copy-start = (bf16[1792,1024]{1,0:T(8,128)(2,1)S(1)}, bf16[1792,1024]{1,0:T(8,128)(2,1)}, u32[]{:S(2)}) copy-start(bf16[1792,1024]{1,0:T(8,128)(2,1)} %w_ref.17) | copy-start | bytes 11010052
  56.9 8.5 %collective-permute-start.16 = (bf16[64,1792]{1,0:T(8,128)(2,1)S(1)}, bf16[64,1792]{1,0:T(8,128)(2,1)S(1)}, u32[]{:S(2)}, u32[]{:S(2)}) collective-permute-start(bf16[64,1792]{1,0:T(8,128)(2,1)S(1)} %get-tuple-element.68), channel_id=1, source_target_pairs={{0,16},{8,24},{16,0},{24,8},{1,17},{9,25},{17,1},{25,9},{2,18},{10... | collective-permute-start | bytes 688136 | tf_op jit(solution)/shard_map/ppermute | solution.py:25
  58.8 11.6 %collective-permute-start.19 = (bf16[64,1792]{1,0:T(8,128)(2,1)S(1)}, bf16[64,1792]{1,0:T(8,128)(2,1)S(1)}, u32[]{:S(2)}, u32[]{:S(2)}) collective-permute-start(bf16[64,1792]{1,0:T(8,128)(2,1)S(1)} %get-tuple-element.73), channel_id=1, source_target_pairs={{0,16},{8,24},{16,0},{24,8},{1,17},{9,25},{17,1},{25,9},{2,18},{10... | collective-permute-start | bytes 688136 | tf_op jit(solution)/shard_map/ppermute | solution.py:25
  59.0 16.3 %collective-permute-start.25 = (bf16[64,1792]{1,0:T(8,128)(2,1)S(1)}, bf16[64,1792]{1,0:T(8,128)(2,1)S(1)}, u32[]{:S(2)}, u32[]{:S(2)}) collective-permute-start(bf16[64,1792]{1,0:T(8,128)(2,1)S(1)} %get-tuple-element.82), channel_id=1, source_target_pairs={{0,16},{8,24},{16,0},{24,8},{1,17},{9,25},{17,1},{25,9},{2,18},{10... | collective-permute-start | bytes 688136 | tf_op jit(solution)/shard_map/ppermute | solution.py:25
  60.8 18.7 %collective-permute-start.10 = (bf16[64,1792]{1,0:T(8,128)(2,1)S(1)}, bf16[64,1792]{1,0:T(8,128)(2,1)S(1)}, u32[]{:S(2)}, u32[]{:S(2)}) collective-permute-start(bf16[64,1792]{1,0:T(8,128)(2,1)S(1)} %get-tuple-element.57), channel_id=1, source_target_pairs={{0,16},{8,24},{16,0},{24,8},{1,17},{9,25},{17,1},{25,9},{2,18},{10... | collective-permute-start | bytes 688136 | tf_op jit(solution)/shard_map/ppermute | solution.py:25
  65.5 14.9 %collective-permute-start.17 = (bf16[64,1792]{1,0:T(8,128)(2,1)S(1)}, bf16[64,1792]{1,0:T(8,128)(2,1)S(1)}, u32[]{:S(2)}, u32[]{:S(2)}) collective-permute-start(bf16[64,1792]{1,0:T(8,128)(2,1)S(1)} %shard_map.116.hid_ref), channel_id=1, source_target_pairs={{0,8},{8,0},{16,24},{24,16},{1,9},{9,1},{17,25},{25,17},{2,10},{10... | collective-permute-start | bytes 688136 | tf_op jit(solution)/shard_map/ppermute | solution.py:25
  70.4 13.3 %collective-permute-start.20 = (bf16[64,1792]{1,0:T(8,128)(2,1)S(1)}, bf16[64,1792]{1,0:T(8,128)(2,1)S(1)}, u32[]{:S(2)}, u32[]{:S(2)}) collective-permute-start(bf16[64,1792]{1,0:T(8,128)(2,1)S(1)} %shard_map.119.hid_ref), channel_id=1, source_target_pairs={{0,8},{8,0},{16,24},{24,16},{1,9},{9,1},{17,25},{25,17},{2,10},{10... | collective-permute-start | bytes 688136 | tf_op jit(solution)/shard_map/ppermute | solution.py:25
  75.3 10.3 %collective-permute-start.26 = (bf16[64,1792]{1,0:T(8,128)(2,1)S(1)}, bf16[64,1792]{1,0:T(8,128)(2,1)S(1)}, u32[]{:S(2)}, u32[]{:S(2)}) collective-permute-start(bf16[64,1792]{1,0:T(8,128)(2,1)S(1)} %shard_map.124.hid_ref), channel_id=1, source_target_pairs={{0,8},{8,0},{16,24},{24,16},{1,9},{9,1},{17,25},{25,17},{2,10},{10... | collective-permute-start | bytes 688136 | tf_op jit(solution)/shard_map/ppermute | solution.py:25
  79.5 9.4 %collective-permute-start.11 = (bf16[64,1792]{1,0:T(8,128)(2,1)S(1)}, bf16[64,1792]{1,0:T(8,128)(2,1)S(1)}, u32[]{:S(2)}, u32[]{:S(2)}) collective-permute-start(bf16[64,1792]{1,0:T(8,128)(2,1)S(1)} %shard_map.111.hid_ref), channel_id=1, source_target_pairs={{0,8},{8,0},{16,24},{24,16},{1,9},{9,1},{17,25},{25,17},{2,10},{10... | collective-permute-start | bytes 688136 | tf_op jit(solution)/shard_map/ppermute | solution.py:25
  81.1 12.7 %collective-permute-start.18 = (bf16[2,4,8,1024]{3,2,1,0:T(8,128)(2,1)S(1)}, bf16[2,4,8,1024]{3,2,1,0:T(8,128)(2,1)S(1)}, u32[]{:S(2)}, u32[]{:S(2)}) collective-permute-start(bf16[2,4,8,1024]{3,2,1,0:T(8,128)(2,1)S(1)} %get-tuple-element.72), channel_id=1, source_target_pairs={{0,1},{1,0},{2,3},{3,2},{4,5},{5,4},{6,7},{7,6},{8,9},{9,8},{10,11... | collective-permute-start | bytes 393224 | tf_op jit(solution)/shard_map/ppermute | solution.py:25
  84.4 9.7 %collective-permute-start.21 = (bf16[2,4,8,1024]{3,2,1,0:T(8,128)(2,1)S(1)}, bf16[2,4,8,1024]{3,2,1,0:T(8,128)(2,1)S(1)}, u32[]{:S(2)}, u32[]{:S(2)}) collective-permute-start(bf16[2,4,8,1024]{3,2,1,0:T(8,128)(2,1)S(1)} %get-tuple-element.77), channel_id=1, source_target_pairs={{0,1},{1,0},{2,3},{3,2},{4,5},{5,4},{6,7},{7,6},{8,9},{9,8},{10,11... | collective-permute-start | bytes 393224 | tf_op jit(solution)/shard_map/ppermute | solution.py:25
  86.3 16.2 %collective-permute-start.27 = (bf16[2,4,8,1024]{3,2,1,0:T(8,128)(2,1)S(1)}, bf16[2,4,8,1024]{3,2,1,0:T(8,128)(2,1)S(1)}, u32[]{:S(2)}, u32[]{:S(2)}) collective-permute-start(bf16[2,4,8,1024]{3,2,1,0:T(8,128)(2,1)S(1)} %get-tuple-element.86), channel_id=1, source_target_pairs={{0,1},{1,0},{2,3},{3,2},{4,5},{5,4},{6,7},{7,6},{8,9},{9,8},{10,11... | collective-permute-start | bytes 393224 | tf_op jit(solution)/shard_map/ppermute | solution.py:25
  89.7 4.8 %collective-permute-start.12 = (bf16[2,2,8,1024]{3,2,1,0:T(8,128)(2,1)S(1)}, bf16[2,2,8,1024]{3,2,1,0:T(8,128)(2,1)S(1)}, u32[]{:S(2)}, u32[]{:S(2)}) collective-permute-start(bf16[2,2,8,1024]{3,2,1,0:T(8,128)(2,1)S(1)} %get-tuple-element.63), channel_id=1, source_target_pairs={{0,2},{1,3},{2,0},{3,1},{4,6},{5,7},{6,4},{7,5},{8,10},{9,11},{10,... | collective-permute-start | bytes 196616 | tf_op jit(solution)/shard_map/ppermute | solution.py:25
  89.8 8.5 %collective-permute-start.13 = (bf16[2,2,8,1024]{3,2,1,0:T(8,128)(2,1)S(1)}, bf16[2,2,8,1024]{3,2,1,0:T(8,128)(2,1)S(1)}, u32[]{:S(2)}, u32[]{:S(2)}) collective-permute-start(bf16[2,2,8,1024]{3,2,1,0:T(8,128)(2,1)S(1)} %get-tuple-element.64), channel_id=1, source_target_pairs={{0,4},{1,5},{2,6},{3,7},{4,0},{5,1},{6,2},{7,3},{8,12},{9,13},{10,... | collective-permute-start | bytes 196616 | tf_op jit(solution)/shard_map/ppermute | solution.py:25
  93.8 6.1 %collective-permute-start.14 = (bf16[2,2,8,1024]{3,2,1,0:T(8,128)(2,1)S(1)}, bf16[2,2,8,1024]{3,2,1,0:T(8,128)(2,1)S(1)}, u32[]{:S(2)}, u32[]{:S(2)}) collective-permute-start(bf16[2,2,8,1024]{3,2,1,0:T(8,128)(2,1)S(1)} %get-tuple-element.65), channel_id=1, source_target_pairs={{0,6},{1,7},{2,4},{3,5},{4,2},{5,3},{6,0},{7,1},{8,14},{9,15},{10,... | collective-permute-start | bytes 196616 | tf_op jit(solution)/shard_map/ppermute | solution.py:25
  94.2 12.1 %collective-permute-start.22 = (bf16[2,1,16,1024]{3,2,1,0:T(8,128)(2,1)S(1)}, bf16[2,1,16,1024]{3,2,1,0:T(8,128)(2,1)S(1)}, u32[]{:S(2)}, u32[]{:S(2)}) collective-permute-start(bf16[2,1,16,1024]{3,2,1,0:T(8,128)(2,1)S(1)} %get-tuple-element.79), channel_id=1, source_target_pairs={{0,2},{1,3},{2,0},{3,1},{4,6},{5,7},{6,4},{7,5},{8,10},{9,11},{10,... | collective-permute-start | bytes 196616 | tf_op jit(solution)/shard_map/ppermute | solution.py:25
  99.9 4.2 %collective-permute-start.15 = (bf16[2,1,8,1024]{3,2,1,0:T(8,128)(2,1)S(1)}, bf16[2,1,8,1024]{3,2,1,0:T(8,128)(2,1)S(1)}, u32[]{:S(2)}, u32[]{:S(2)}) collective-permute-start(bf16[2,1,8,1024]{3,2,1,0:T(8,128)(2,1)S(1)} %get-tuple-element.67), channel_id=1, source_target_pairs={{0,1},{1,0},{2,3},{3,2},{4,5},{5,4},{6,7},{7,6},{8,9},{9,8},{10,11... | collective-permute-start | bytes 98312 | tf_op jit(solution)/shard_map/ppermute | solution.py:25
  100.5 6.5 %collective-permute-start.23 = (bf16[2,1,16,1024]{3,2,1,0:T(8,128)(2,1)S(1)}, bf16[2,1,16,1024]{3,2,1,0:T(8,128)(2,1)S(1)}, u32[]{:S(2)}, u32[]{:S(2)}) collective-permute-start(bf16[2,1,16,1024]{3,2,1,0:T(8,128)(2,1)S(1)} %get-tuple-element.80), channel_id=1, source_target_pairs={{0,4},{1,5},{2,6},{3,7},{4,0},{5,1},{6,2},{7,3},{8,12},{9,13},{10,... | collective-permute-start | bytes 196616 | tf_op jit(solution)/shard_map/ppermute | solution.py:25
  101.8 6.5 %collective-permute-start.24 = (bf16[2,1,16,1024]{3,2,1,0:T(8,128)(2,1)S(1)}, bf16[2,1,16,1024]{3,2,1,0:T(8,128)(2,1)S(1)}, u32[]{:S(2)}, u32[]{:S(2)}) collective-permute-start(bf16[2,1,16,1024]{3,2,1,0:T(8,128)(2,1)S(1)} %get-tuple-element.81), channel_id=1, source_target_pairs={{0,6},{1,7},{2,4},{3,5},{4,2},{5,3},{6,0},{7,1},{8,14},{9,15},{10,... | collective-permute-start | bytes 196616 | tf_op jit(solution)/shard_map/ppermute | solution.py:25
  102.5 5.8 %collective-permute-start.28 = (bf16[2,1,8,1024]{3,2,1,0:T(8,128)(2,1)S(1)}, bf16[2,1,8,1024]{3,2,1,0:T(8,128)(2,1)S(1)}, u32[]{:S(2)}, u32[]{:S(2)}) collective-permute-start(bf16[2,1,8,1024]{3,2,1,0:T(8,128)(2,1)S(1)} %get-tuple-element.88), channel_id=1, source_target_pairs={{0,2},{1,3},{2,0},{3,1},{4,6},{5,7},{6,4},{7,5},{8,10},{9,11},{10,... | collective-permute-start | bytes 98312 | tf_op jit(solution)/shard_map/ppermute | solution.py:25
  104.1 5.5 %collective-permute-start.29 = (bf16[2,1,8,1024]{3,2,1,0:T(8,128)(2,1)S(1)}, bf16[2,1,8,1024]{3,2,1,0:T(8,128)(2,1)S(1)}, u32[]{:S(2)}, u32[]{:S(2)}) collective-permute-start(bf16[2,1,8,1024]{3,2,1,0:T(8,128)(2,1)S(1)} %get-tuple-element.89), channel_id=1, source_target_pairs={{0,4},{1,5},{2,6},{3,7},{4,0},{5,1},{6,2},{7,3},{8,12},{9,13},{10,... | collective-permute-start | bytes 98312 | tf_op jit(solution)/shard_map/ppermute | solution.py:25
  106.3 5.7 %collective-permute-start.30 = (bf16[2,1,8,1024]{3,2,1,0:T(8,128)(2,1)S(1)}, bf16[2,1,8,1024]{3,2,1,0:T(8,128)(2,1)S(1)}, u32[]{:S(2)}, u32[]{:S(2)}) collective-permute-start(bf16[2,1,8,1024]{3,2,1,0:T(8,128)(2,1)S(1)} %get-tuple-element.90), channel_id=1, source_target_pairs={{0,6},{1,7},{2,4},{3,5},{4,2},{5,3},{6,0},{7,1},{8,14},{9,15},{10,... | collective-permute-start | bytes 98312 | tf_op jit(solution)/shard_map/ppermute | solution.py:25
